TPU v7x, 128 devices: a whole 4x4x4 slice. The times are simulated.
128 devices in a mesh: segment: 4 (over x_hi, core), strip: 32 (over y, z, x_lo).
Axes of the slice: x: 4 (x_hi: 2, x_lo: 2; x = x_hi * 2 + x_lo), y: 4, z: 4, core: 2. Of those that a mesh axis runs over, the one named last changes fastest.
Arguments:
- features: bfloat16 [2, 256, 512, 256], P(None, 'segment', 'strip'), may hold values from -6 to 6
- weight_first: bfloat16 [3, 3, 256, 256], replicated, may hold values from -0.125 to 0.125
- weight_second: bfloat16 [3, 3, 256, 256], replicated, may hold values from -0.125 to 0.125
- weight_down: bfloat16 [2, 2, 256, 512], replicated, may hold values from -0.1875 to 0.1875
- section_weights: bfloat16 [4, 3, 3, 512, 512], P('segment'), may hold values from -0.09375 to 0.09375
Outputs:
- section_features: bfloat16 [4, 2, 128, 256, 512], P('segment', None, 'strip')
All inputs are finite; a program needn't handle non-finite values.
Results may differ from a plain program's by a relative error of at most 0.0095.
Values may be sent and summed in bfloat16 or wider, within the bound.
No kernel may reach another device: no remote copies, remote signals or barrier semaphores. Data moves between devices by JAX's collectives and lax.ppermute only.
A program may use at most 128 MiB of HBM per device.

v0:
```python
import jax
import jax.numpy as jnp
from jax import lax
from jax.sharding import PartitionSpec as P


def padded_2(block, sides, width):
    for axis, dim in sides:
        count = lax.axis_size(axis)
        forward = [(i, i + 1) for i in range(count - 1)]
        backward = [(target, source) for source, target in forward]
        low = lax.ppermute(
            lax.slice_in_dim(block, block.shape[dim] - width, None, axis=dim), axis, forward
        )
        high = lax.ppermute(lax.slice_in_dim(block, 0, width, axis=dim), axis, backward)
        block = jnp.concatenate([low, block, high], axis=dim)
    return block


def in_order(tiles, dim):
    lengths = list(tiles.shape[1:])
    lengths[dim] *= tiles.shape[0]
    return jnp.moveaxis(tiles, 0, dim).reshape(lengths)


def from_everyone(shard, axis):
    devices = lax.axis_size(axis)
    return lax.all_to_all(
        jnp.broadcast_to(shard[None], (devices, *shard.shape)), axis, 0, 0, tiled=True
    )


def gather_directly(shard, axis, dim):
    return in_order(from_everyone(shard, axis), dim)


def passed_along(value, axis, steps):
    count = lax.axis_size(axis)
    first, last = (max(0, -steps), min(count, count - steps))
    return lax.ppermute(value, axis, [(source, source + steps) for source in range(first, last)])


def conv_valid(padded, weight):
    batches, rows_pad, columns_pad, channels = padded.shape
    rows = rows_pad - 2
    columns = columns_pad - 2
    total = None
    for row_off in range(3):
        for col_off in range(3):
            window = padded[:, row_off : row_off + rows, col_off : col_off + columns, :].reshape(
                -1, channels
            )
            partial_sum = jnp.dot(
                window, weight[row_off, col_off], preferred_element_type=jnp.float32
            )
            total = partial_sum if total is None else total + partial_sum
    return total.reshape(batches, rows, columns, weight.shape[3])


def residual_valid(padded, inner, weight):
    return jax.nn.relu(inner.astype(jnp.float32) + conv_valid(padded, weight))


def tile_rimmed(inputs):
    return padded_2(inputs, (("segment", 1), ("strip", 2)), 1)


def section_layer(current, weight):
    rimmed = padded_2(current, (("strip", 0),), 1)
    padded = jnp.pad(rimmed, ((0, 0), (1, 1), (0, 0)))
    return residual_valid(padded[None], current[None], weight)[0]


def shards(features, weight_first, weight_second, weight_down, section_weights):
    batches, tile_rows, tile_columns, channels = features.shape
    first = residual_valid(tile_rimmed(features), features, weight_first).astype(jnp.bfloat16)
    second = residual_valid(tile_rimmed(first), first, weight_second).astype(jnp.bfloat16)
    blocks = second.reshape(batches, tile_rows // 2, 2, tile_columns // 2, 2, channels)
    total = None
    for row_off in range(2):
        for col_off in range(2):
            piece = blocks[:, :, row_off, :, col_off, :].reshape(-1, channels)
            partial_sum = jnp.dot(
                piece, weight_down[row_off, col_off], preferred_element_type=jnp.float32
            )
            total = partial_sum if total is None else total + partial_sum
    out_channels = weight_down.shape[3]
    reduced = (
        jax.nn.relu(total)
        .reshape(batches, tile_rows // 2, tile_columns // 2, out_channels)
        .astype(jnp.bfloat16)
    )
    banded = gather_directly(reduced, "segment", 1)
    strips = lax.all_to_all(banded, "strip", split_axis=1, concat_axis=2, tiled=True)
    strip_rows = strips.shape[1]
    full_columns = strips.shape[2]
    weight = section_weights[0]
    segment_index = lax.axis_index("segment")
    segments = lax.axis_size("segment")
    results = jnp.zeros((batches, strip_rows, full_columns, out_channels), jnp.bfloat16)
    half = full_columns // 2
    widened = jnp.pad(strips, ((0, 0), (0, 0), (segments, segments), (0, 0)))
    inputs = []
    for window_index in range(batches):
        for half_index in range(2):
            inputs.append(
                widened[
                    window_index, :, half_index * half : half_index * half + half + 2 * segments, :
                ]
            )
    micro_count = len(inputs)
    ticks = micro_count + segments - 1
    carried = jnp.zeros_like(inputs[0])
    zero_index = jnp.int32(0)
    for instant in range(ticks):
        feed = inputs[min(instant, micro_count - 1)]
        current = jnp.where(segment_index == 0, feed, carried)
        produced = section_layer(current, weight)
        micro_index = instant - segment_index
        valid = (micro_index >= 0) & (micro_index < micro_count)
        slot = jnp.clip(micro_index, 0, micro_count - 1)
        half_index = jnp.mod(slot, 2)
        col_global = half_index * half - segments + jnp.arange(half + 2 * segments)
        col_inside = (col_global >= 0) & (col_global < full_columns)
        produced = jnp.where(col_inside[None, :, None], produced, 0.0)
        produced = produced.astype(jnp.bfloat16)
        window_index = slot // 2
        start = half_index * half
        anchor = (window_index, zero_index, start, zero_index)
        previous = lax.dynamic_slice(results, anchor, (1, strip_rows, half, out_channels))
        chosen = jnp.where(valid, produced[None, :, segments : segments + half, :], previous)
        results = lax.dynamic_update_slice(results, chosen, anchor)
        if instant < ticks - 1:
            carried = passed_along(produced, "segment", 1)
    return results[None]


def solution(mesh):
    return jax.shard_map(
        shards,
        mesh=mesh,
        in_specs=(
            P(None, "segment", "strip", None),
            P(),
            P(),
            P(),
            P("segment", None, None, None, None),
        ),
        out_specs=P("segment", None, "strip", None, None),
        check_vma=False,
    )
```

profile of v0, /device:TPU:102, one launch (start us, length us, event | category | flops | bytes accessed | tf_op | source)
XLA Modules:
  0.0 361.0 jit_solution(7778182579113096713)
XLA Ops:
  2.7 5.1 %collective-permute-start.1 = (bf16[2,1,16,256]{3,2,1,0:T(8,128)(2,1)S(1)}, bf16[2,1,16,256]{3,2,1,0:T(8,128)(2,1)S(1)}, u32[]{:S(2)}, u32[]{:S(2)}) collective-permute-start(bf16[2,1,16,256]{3,2,1,0:T(8,128)(2,1)S(1)} %get-tuple-element.37), channel_id=1, source_target_pairs={{32,0},{64,32},{96,64},{33,1},{65,33},{97,65},{34,2},{66,34},{98,6... | collective-permute-start | bytes 49160 | tf_op jit(solution)/shard_map/ppermute | solution.py:15
  18.3 5.3 %collective-permute-done.3 = bf16[2,66,1,256]{3,1,2,0:T(8,128)(2,1)S(1)} collective-permute-done((bf16[2,66,1,256]{3,1,2,0:T(8,128)(2,1)S(1)}, bf16[2,66,1,256]{3,1,2,0:T(8,128)(2,1)S(1)}, u32[]{:S(2)}, u32[]{:S(2)}) %collective-permute-start.3) | collective-permute-done | bytes 67616 | tf_op jit(solution)/shard_map/ppermute | solution.py:15
  34.4 5.1 %collective-permute-start.5 = (bf16[2,1,16,256]{3,2,1,0:T(8,128)(2,1)S(1)}, bf16[2,1,16,256]{3,2,1,0:T(8,128)(2,1)S(1)}, u32[]{:S(2)}, u32[]{:S(2)}) collective-permute-start(bf16[2,1,16,256]{3,2,1,0:T(8,128)(2,1)S(1)} %get-tuple-element.33), channel_id=1, source_target_pairs={{32,0},{64,32},{96,64},{33,1},{65,33},{97,65},{34,2},{66,34},{98,6... | collective-permute-start | bytes 49160 | tf_op jit(solution)/shard_map/ppermute | solution.py:15
  43.1 4.1 %collective-permute-start.7 = (bf16[2,66,1,256]{3,1,2,0:T(8,128)(2,1)S(1)}, bf16[2,66,1,256]{3,1,2,0:T(8,128)(2,1)S(1)}, u32[]{:S(2)}, u32[]{:S(2)}) collective-permute-start(bf16[2,66,1,256]{3,1,2,0:T(8,128)(2,1)S(1)} %copy.35), channel_id=1, source_target_pairs={{1,0},{2,1},{3,2},{4,3},{5,4},{6,5},{7,6},{8,7},{9,8},{10,9},{11,1... | collective-permute-start | bytes 202760 | tf_op jit(solution)/shard_map/ppermute | solution.py:15
  47.5 4.8 %collective-permute-done.7 = bf16[2,66,1,256]{3,1,2,0:T(8,128)(2,1)S(1)} collective-permute-done((bf16[2,66,1,256]{3,1,2,0:T(8,128)(2,1)S(1)}, bf16[2,66,1,256]{3,1,2,0:T(8,128)(2,1)S(1)}, u32[]{:S(2)}, u32[]{:S(2)}) %collective-permute-start.7) | collective-permute-done | bytes 67616 | tf_op jit(solution)/shard_map/ppermute | solution.py:15
  63.1 28.7 %all_to_all.23 = bf16[4,2,32,8,512]{4,3,2,1,0:T(8,128)(2,1)S(1)} all-to-all(bf16[4,2,32,8,512]{4,3,2,1,0:T(8,128)(2,1)S(1)} %broadcast_in_dim.121), channel_id=1, replica_groups=mesh['segment'=4,'strip'=32] {'segment'}, dimensions={0} | all-to-all | bytes 4194304 | tf_op jit(solution)/shard_map/all_to_all | solution.py:28
  93.7 7.9 %all-to-all-start.1 = ((bf16[2,128,8,512]{3,2,0,1:T(8,128)(2,1)}), bf16[2,128,8,512]{3,2,0,1:T(8,128)(2,1)S(1)}, u32[]{:S(2)}, u32[]{:S(2)}) async-start(bf16[2,128,8,512]{3,2,0,1:T(8,128)(2,1)} %copy.43), calls=%async_computation.1 | async-start | bytes 4194304 | tf_op jit(solution)/shard_map/all_to_all | solution.py:94
  101.6 26.9 %all-to-all-done.1 = bf16[2,128,8,512]{3,2,0,1:T(8,128)(2,1)S(1)} async-done(((bf16[2,128,8,512]{3,2,0,1:T(8,128)(2,1)}), bf16[2,128,8,512]{3,2,0,1:T(8,128)(2,1)S(1)}, u32[]{:S(2)}, u32[]{:S(2)}) %all-to-all-start.1) | async-done | bytes 2097184 | tf_op jit(solution)/shard_map/all_to_all | solution.py:94
  131.8 6.5 %collective-permute-start.8 = (bf16[1,136,512]{2,1,0:T(8,128)(2,1)S(1)}, bf16[1,136,512]{2,1,0:T(8,128)(2,1)S(1)}, u32[]{:S(2)}, u32[]{:S(2)}) collective-permute-start(bf16[1,136,512]{2,1,0:T(8,128)(2,1)S(1)} %get-tuple-element.114), channel_id=1, source_target_pairs={{0,1},{1,2},{2,3},{3,4},{4,5},{5,6},{6,7},{7,8},{8,9},{9,10},{10,1... | collective-permute-start | bytes 417800 | tf_op jit(solution)/shard_map/ppermute | solution.py:12
  141.8 6.5 %collective-permute-done.9 = bf16[1,136,512]{2,1,0:T(8,128)(2,1)S(1)} collective-permute-done((bf16[1,136,512]{2,1,0:T(8,128)(2,1)S(1)}, bf16[1,136,512]{2,1,0:T(8,128)(2,1)S(1)}, u32[]{:S(2)}, u32[]{:S(2)}) %collective-permute-start.9) | collective-permute-done | bytes 139296 | tf_op jit(solution)/shard_map/ppermute | solution.py:15
  155.9 13.4 %collective-permute-done.10 = bf16[4,136,512]{2,1,0:T(8,128)(2,1)S(1)} collective-permute-done((bf16[4,136,512]{2,1,0:T(8,128)(2,1)S(1)}, bf16[4,136,512]{2,1,0:T(8,128)(2,1)S(1)}, u32[]{:S(2)}, u32[]{:S(2)}) %collective-permute-start.10) | collective-permute-done | bytes 557088 | tf_op jit(solution)/shard_map/ppermute | solution.py:40
  171.5 3.9 %collective-permute-start.12 = (bf16[1,136,512]{2,1,0:T(8,128)(2,1)S(1)}, bf16[1,136,512]{2,1,0:T(8,128)(2,1)}, u32[]{:S(2)}, u32[]{:S(2)}) collective-permute-start(bf16[1,136,512]{2,1,0:T(8,128)(2,1)S(1)} %get-tuple-element.113), channel_id=1, source_target_pairs={{1,0},{2,1},{3,2},{4,3},{5,4},{6,5},{7,6},{8,7},{9,8},{10,9},{11,1... | collective-permute-start | bytes 417800 | tf_op jit(solution)/shard_map/ppermute | solution.py:15
  176.6 4.9 %collective-permute-done.12 = bf16[1,136,512]{2,1,0:T(8,128)(2,1)} collective-permute-done((bf16[1,136,512]{2,1,0:T(8,128)(2,1)S(1)}, bf16[1,136,512]{2,1,0:T(8,128)(2,1)}, u32[]{:S(2)}, u32[]{:S(2)}) %collective-permute-start.12) | collective-permute-done | bytes 139296 | tf_op jit(solution)/shard_map/ppermute | solution.py:15
  191.2 12.7 %collective-permute-done.13 = bf16[4,136,512]{2,1,0:T(8,128)(2,1)S(1)} collective-permute-done((bf16[4,136,512]{2,1,0:T(8,128)(2,1)S(1)}, bf16[4,136,512]{2,1,0:T(8,128)(2,1)S(1)}, u32[]{:S(2)}, u32[]{:S(2)}) %collective-permute-start.13) | collective-permute-done | bytes 557088 | tf_op jit(solution)/shard_map/ppermute | solution.py:40
  211.2 4.9 %collective-permute-done.15 = bf16[1,136,512]{2,1,0:T(8,128)(2,1)} collective-permute-done((bf16[1,136,512]{2,1,0:T(8,128)(2,1)S(1)}, bf16[1,136,512]{2,1,0:T(8,128)(2,1)}, u32[]{:S(2)}, u32[]{:S(2)}) %collective-permute-start.15) | collective-permute-done | bytes 139296 | tf_op jit(solution)/shard_map/ppermute | solution.py:15
  225.9 12.7 %collective-permute-done.16 = bf16[4,136,512]{2,1,0:T(8,128)(2,1)S(1)} collective-permute-done((bf16[4,136,512]{2,1,0:T(8,128)(2,1)S(1)}, bf16[4,136,512]{2,1,0:T(8,128)(2,1)S(1)}, u32[]{:S(2)}, u32[]{:S(2)}) %collective-permute-start.16) | collective-permute-done | bytes 557088 | tf_op jit(solution)/shard_map/ppermute | solution.py:40
  240.8 4.3 %collective-permute-start.18 = (bf16[1,136,512]{2,1,0:T(8,128)(2,1)S(1)}, bf16[1,136,512]{2,1,0:T(8,128)(2,1)}, u32[]{:S(2)}, u32[]{:S(2)}) collective-permute-start(bf16[1,136,512]{2,1,0:T(8,128)(2,1)S(1)} %get-tuple-element.109), channel_id=1, source_target_pairs={{1,0},{2,1},{3,2},{4,3},{5,4},{6,5},{7,6},{8,7},{9,8},{10,9},{11,1... | collective-permute-start | bytes 417800 | tf_op jit(solution)/shard_map/ppermute | solution.py:15
  245.9 4.9 %collective-permute-done.18 = bf16[1,136,512]{2,1,0:T(8,128)(2,1)} collective-permute-done((bf16[1,136,512]{2,1,0:T(8,128)(2,1)S(1)}, bf16[1,136,512]{2,1,0:T(8,128)(2,1)}, u32[]{:S(2)}, u32[]{:S(2)}) %collective-permute-start.18) | collective-permute-done | bytes 139296 | tf_op jit(solution)/shard_map/ppermute | solution.py:15
  260.5 12.7 %collective-permute-done.19 = bf16[4,136,512]{2,1,0:T(8,128)(2,1)S(1)} collective-permute-done((bf16[4,136,512]{2,1,0:T(8,128)(2,1)S(1)}, bf16[4,136,512]{2,1,0:T(8,128)(2,1)S(1)}, u32[]{:S(2)}, u32[]{:S(2)}) %collective-permute-start.19) | collective-permute-done | bytes 557088 | tf_op jit(solution)/shard_map/ppermute | solution.py:40
  280.5 4.9 %collective-permute-done.21 = bf16[1,136,512]{2,1,0:T(8,128)(2,1)} collective-permute-done((bf16[1,136,512]{2,1,0:T(8,128)(2,1)S(1)}, bf16[1,136,512]{2,1,0:T(8,128)(2,1)}, u32[]{:S(2)}, u32[]{:S(2)}) %collective-permute-start.21) | collective-permute-done | bytes 139296 | tf_op jit(solution)/shard_map/ppermute | solution.py:15
  296.7 12.6 %collective-permute-done.22 = bf16[4,136,512]{2,1,0:T(8,128)(2,1)S(1)} collective-permute-done((bf16[4,136,512]{2,1,0:T(8,128)(2,1)}, bf16[4,136,512]{2,1,0:T(8,128)(2,1)S(1)}, u32[]{:S(2)}, u32[]{:S(2)}) %collective-permute-start.22) | collective-permute-done | bytes 557088 | tf_op jit(solution)/shard_map/ppermute | solution.py:40
  316.7 4.9 %collective-permute-done.24 = bf16[1,136,512]{2,1,0:T(8,128)(2,1)S(1)} collective-permute-done((bf16[1,136,512]{2,1,0:T(8,128)(2,1)S(1)}, bf16[1,136,512]{2,1,0:T(8,128)(2,1)S(1)}, u32[]{:S(2)}, u32[]{:S(2)}) %collective-permute-start.24) | collective-permute-done | bytes 139296 | tf_op jit(solution)/shard_map/ppermute | solution.py:15
  331.3 11.3 %collective-permute-done.25 = bf16[4,136,512]{2,1,0:T(8,128)(2,1)S(1)} collective-permute-done((bf16[4,136,512]{2,1,0:T(8,128)(2,1)S(1)}, bf16[4,136,512]{2,1,0:T(8,128)(2,1)S(1)}, u32[]{:S(2)}, u32[]{:S(2)}) %collective-permute-start.25) | collective-permute-done | bytes 557088 | tf_op jit(solution)/shard_map/ppermute | solution.py:40
  350.2 4.5 %collective-permute-done.27 = bf16[1,136,512]{2,1,0:T(8,128)(2,1)S(1)} collective-permute-done((bf16[1,136,512]{2,1,0:T(8,128)(2,1)S(1)}, bf16[1,136,512]{2,1,0:T(8,128)(2,1)S(1)}, u32[]{:S(2)}, u32[]{:S(2)}) %collective-permute-start.27) | collective-permute-done | bytes 139296 | tf_op jit(solution)/shard_map/ppermute | solution.py:15
  (259 shorter events, 145.4 us)
Async XLA Ops:
  0.7 7.1 %collective-permute-start = (bf16[2,1,16,256]{3,2,1,0:T(8,128)(2,1)S(1)}, bf16[2,1,16,256]{3,2,1,0:T(8,128)(2,1)S(1)}, u32[]{:S(2)}, u32[]{:S(2)}) collective-permute-start(bf16[2,1,16,256]{3,2,1,0:T(8,128)(2,1)S(1)} %get-tuple-element.38), channel_id=1, source_target_pairs={{0,32},{32,64},{64,96},{1,33},{33,65},{65,97},{2,34},{34,66},{66,9... | collective-permute-start | bytes 49160 | tf_op jit(solution)/shard_map/ppermute | solution.py:12
  14.3 9.3 %collective-permute-start.3 = (bf16[2,66,1,256]{3,1,2,0:T(8,128)(2,1)S(1)}, bf16[2,66,1,256]{3,1,2,0:T(8,128)(2,1)S(1)}, u32[]{:S(2)}, u32[]{:S(2)}) collective-permute-start(bf16[2,66,1,256]{3,1,2,0:T(8,128)(2,1)S(1)} %copy.31), channel_id=1, source_target_pairs={{1,0},{2,1},{3,2},{4,3},{5,4},{6,5},{7,6},{8,7},{9,8},{10,9},{11,1... | collective-permute-start | bytes 202760 | tf_op jit(solution)/shard_map/ppermute | solution.py:15
  32.5 7.1 %collective-permute-start.4 = (bf16[2,1,16,256]{3,2,1,0:T(8,128)(2,1)S(1)}, bf16[2,1,16,256]{3,2,1,0:T(8,128)(2,1)S(1)}, u32[]{:S(2)}, u32[]{:S(2)}) collective-permute-start(bf16[2,1,16,256]{3,2,1,0:T(8,128)(2,1)S(1)} %get-tuple-element.32), channel_id=1, source_target_pairs={{0,32},{32,64},{64,96},{1,33},{33,65},{65,97},{2,34},{34,66},{66,9... | collective-permute-start | bytes 49160 | tf_op jit(solution)/shard_map/ppermute | solution.py:12
  43.1 9.3 %collective-permute-start.7 = (bf16[2,66,1,256]{3,1,2,0:T(8,128)(2,1)S(1)}, bf16[2,66,1,256]{3,1,2,0:T(8,128)(2,1)S(1)}, u32[]{:S(2)}, u32[]{:S(2)}) collective-permute-start(bf16[2,66,1,256]{3,1,2,0:T(8,128)(2,1)S(1)} %copy.35), channel_id=1, source_target_pairs={{1,0},{2,1},{3,2},{4,3},{5,4},{6,5},{7,6},{8,7},{9,8},{10,9},{11,1... | collective-permute-start | bytes 202760 | tf_op jit(solution)/shard_map/ppermute | solution.py:15
  93.7 34.9 %all-to-all-start.1 = ((bf16[2,128,8,512]{3,2,0,1:T(8,128)(2,1)}), bf16[2,128,8,512]{3,2,0,1:T(8,128)(2,1)S(1)}, u32[]{:S(2)}, u32[]{:S(2)}) async-start(bf16[2,128,8,512]{3,2,0,1:T(8,128)(2,1)} %copy.43), calls=%async_computation.1 | async-start | bytes 4194304 | tf_op jit(solution)/shard_map/all_to_all | solution.py:94
  131.8 10.0 %collective-permute-start.8 = (bf16[1,136,512]{2,1,0:T(8,128)(2,1)S(1)}, bf16[1,136,512]{2,1,0:T(8,128)(2,1)S(1)}, u32[]{:S(2)}, u32[]{:S(2)}) collective-permute-start(bf16[1,136,512]{2,1,0:T(8,128)(2,1)S(1)} %get-tuple-element.114), channel_id=1, source_target_pairs={{0,1},{1,2},{2,3},{3,4},{4,5},{5,6},{6,7},{7,8},{8,9},{9,10},{10,1... | collective-permute-start | bytes 417800 | tf_op jit(solution)/shard_map/ppermute | solution.py:12
  138.3 10.0 %collective-permute-start.9 = (bf16[1,136,512]{2,1,0:T(8,128)(2,1)S(1)}, bf16[1,136,512]{2,1,0:T(8,128)(2,1)S(1)}, u32[]{:S(2)}, u32[]{:S(2)}) collective-permute-start(bf16[1,136,512]{2,1,0:T(8,128)(2,1)S(1)} %get-tuple-element.115), channel_id=1, source_target_pairs={{1,0},{2,1},{3,2},{4,3},{5,4},{6,5},{7,6},{8,7},{9,8},{10,9},{11,1... | collective-permute-start | bytes 417800 | tf_op jit(solution)/shard_map/ppermute | solution.py:15
  154.0 15.3 %collective-permute-start.10 = (bf16[4,136,512]{2,1,0:T(8,128)(2,1)S(1)}, bf16[4,136,512]{2,1,0:T(8,128)(2,1)S(1)}, u32[]{:S(2)}, u32[]{:S(2)}) collective-permute-start(bf16[4,136,512]{2,1,0:T(8,128)(2,1)S(1)} %fusion.5), channel_id=1, source_target_pairs={{0,32},{32,64},{64,96},{1,33},{33,65},{65,97},{2,34},{34,66},{66,9... | collective-permute-start | bytes 1671176 | tf_op jit(solution)/shard_map/ppermute | solution.py:40
  169.6 7.1 %collective-permute-start.11 = (bf16[1,136,512]{2,1,0:T(8,128)(2,1)S(1)}, bf16[1,136,512]{2,1,0:T(8,128)(2,1)}, u32[]{:S(2)}, u32[]{:S(2)}) collective-permute-start(bf16[1,136,512]{2,1,0:T(8,128)(2,1)S(1)} %get-tuple-element.112), channel_id=1, source_target_pairs={{0,1},{1,2},{2,3},{3,4},{4,5},{5,6},{6,7},{7,8},{8,9},{9,10},{10,1... | collective-permute-start | bytes 417800 | tf_op jit(solution)/shard_map/ppermute | solution.py:12
  171.5 10.1 %collective-permute-start.12 = (bf16[1,136,512]{2,1,0:T(8,128)(2,1)S(1)}, bf16[1,136,512]{2,1,0:T(8,128)(2,1)}, u32[]{:S(2)}, u32[]{:S(2)}) collective-permute-start(bf16[1,136,512]{2,1,0:T(8,128)(2,1)S(1)} %get-tuple-element.113), channel_id=1, source_target_pairs={{1,0},{2,1},{3,2},{4,3},{5,4},{6,5},{7,6},{8,7},{9,8},{10,9},{11,1... | collective-permute-start | bytes 417800 | tf_op jit(solution)/shard_map/ppermute | solution.py:15
  189.3 14.6 %collective-permute-start.13 = (bf16[4,136,512]{2,1,0:T(8,128)(2,1)S(1)}, bf16[4,136,512]{2,1,0:T(8,128)(2,1)S(1)}, u32[]{:S(2)}, u32[]{:S(2)}) collective-permute-start(bf16[4,136,512]{2,1,0:T(8,128)(2,1)S(1)} %select_convert_fusion.4), channel_id=1, source_target_pairs={{0,32},{32,64},{64,96},{1,33},{33,65},{65,97},{2,34},{34,66},{66,9... | collective-permute-start | bytes 1671176 | tf_op jit(solution)/shard_map/ppermute | solution.py:40
  204.2 7.1 %collective-permute-start.14 = (bf16[1,136,512]{2,1,0:T(8,128)(2,1)S(1)}, bf16[1,136,512]{2,1,0:T(8,128)(2,1)}, u32[]{:S(2)}, u32[]{:S(2)}) collective-permute-start(bf16[1,136,512]{2,1,0:T(8,128)(2,1)S(1)} %get-tuple-element.110), channel_id=1, source_target_pairs={{0,1},{1,2},{2,3},{3,4},{4,5},{5,6},{6,7},{7,8},{8,9},{9,10},{10,1... | collective-permute-start | bytes 417800 | tf_op jit(solution)/shard_map/ppermute | solution.py:12
  206.1 10.1 %collective-permute-start.15 = (bf16[1,136,512]{2,1,0:T(8,128)(2,1)S(1)}, bf16[1,136,512]{2,1,0:T(8,128)(2,1)}, u32[]{:S(2)}, u32[]{:S(2)}) collective-permute-start(bf16[1,136,512]{2,1,0:T(8,128)(2,1)S(1)} %get-tuple-element.111), channel_id=1, source_target_pairs={{1,0},{2,1},{3,2},{4,3},{5,4},{6,5},{7,6},{8,7},{9,8},{10,9},{11,1... | collective-permute-start | bytes 417800 | tf_op jit(solution)/shard_map/ppermute | solution.py:15
  224.0 14.6 %collective-permute-start.16 = (bf16[4,136,512]{2,1,0:T(8,128)(2,1)S(1)}, bf16[4,136,512]{2,1,0:T(8,128)(2,1)S(1)}, u32[]{:S(2)}, u32[]{:S(2)}) collective-permute-start(bf16[4,136,512]{2,1,0:T(8,128)(2,1)S(1)} %select_convert_fusion.3), channel_id=1, source_target_pairs={{0,32},{32,64},{64,96},{1,33},{33,65},{65,97},{2,34},{34,66},{66,9... | collective-permute-start | bytes 1671176 | tf_op jit(solution)/shard_map/ppermute | solution.py:40
  240.8 10.1 %collective-permute-start.18 = (bf16[1,136,512]{2,1,0:T(8,128)(2,1)S(1)}, bf16[1,136,512]{2,1,0:T(8,128)(2,1)}, u32[]{:S(2)}, u32[]{:S(2)}) collective-permute-start(bf16[1,136,512]{2,1,0:T(8,128)(2,1)S(1)} %get-tuple-element.109), channel_id=1, source_target_pairs={{1,0},{2,1},{3,2},{4,3},{5,4},{6,5},{7,6},{8,7},{9,8},{10,9},{11,1... | collective-permute-start | bytes 417800 | tf_op jit(solution)/shard_map/ppermute | solution.py:15
  258.6 14.6 %collective-permute-start.19 = (bf16[4,136,512]{2,1,0:T(8,128)(2,1)S(1)}, bf16[4,136,512]{2,1,0:T(8,128)(2,1)S(1)}, u32[]{:S(2)}, u32[]{:S(2)}) collective-permute-start(bf16[4,136,512]{2,1,0:T(8,128)(2,1)S(1)} %select_convert_fusion.2), channel_id=1, source_target_pairs={{0,32},{32,64},{64,96},{1,33},{33,65},{65,97},{2,34},{34,66},{66,9... | collective-permute-start | bytes 1671176 | tf_op jit(solution)/shard_map/ppermute | solution.py:40
  273.5 7.1 %collective-permute-start.20 = (bf16[1,136,512]{2,1,0:T(8,128)(2,1)S(1)}, bf16[1,136,512]{2,1,0:T(8,128)(2,1)}, u32[]{:S(2)}, u32[]{:S(2)}) collective-permute-start(bf16[1,136,512]{2,1,0:T(8,128)(2,1)S(1)} %get-tuple-element.106), channel_id=1, source_target_pairs={{0,1},{1,2},{2,3},{3,4},{4,5},{5,6},{6,7},{7,8},{8,9},{9,10},{10,1... | collective-permute-start | bytes 417800 | tf_op jit(solution)/shard_map/ppermute | solution.py:12
  275.4 10.1 %collective-permute-start.21 = (bf16[1,136,512]{2,1,0:T(8,128)(2,1)S(1)}, bf16[1,136,512]{2,1,0:T(8,128)(2,1)}, u32[]{:S(2)}, u32[]{:S(2)}) collective-permute-start(bf16[1,136,512]{2,1,0:T(8,128)(2,1)S(1)} %get-tuple-element.107), channel_id=1, source_target_pairs={{1,0},{2,1},{3,2},{4,3},{5,4},{6,5},{7,6},{8,7},{9,8},{10,9},{11,1... | collective-permute-start | bytes 417800 | tf_op jit(solution)/shard_map/ppermute | solution.py:15
  294.0 15.2 %collective-permute-start.22 = (bf16[4,136,512]{2,1,0:T(8,128)(2,1)}, bf16[4,136,512]{2,1,0:T(8,128)(2,1)S(1)}, u32[]{:S(2)}, u32[]{:S(2)}) collective-permute-start(bf16[4,136,512]{2,1,0:T(8,128)(2,1)} %select_convert_fusion.1), channel_id=1, source_target_pairs={{0,32},{32,64},{64,96},{1,33},{33,65},{65,97},{2,34},{34,66},{66,9... | collective-permute-start | bytes 1671176 | tf_op jit(solution)/shard_map/ppermute | solution.py:40
  309.5 7.2 %collective-permute-start.23 = (bf16[1,136,512]{2,1,0:T(8,128)(2,1)S(1)}, bf16[1,136,512]{2,1,0:T(8,128)(2,1)S(1)}, u32[]{:S(2)}, u32[]{:S(2)}) collective-permute-start(bf16[1,136,512]{2,1,0:T(8,128)(2,1)S(1)} %get-tuple-element.104), channel_id=1, source_target_pairs={{0,1},{1,2},{2,3},{3,4},{4,5},{5,6},{6,7},{7,8},{8,9},{9,10},{10,1... | collective-permute-start | bytes 417800 | tf_op jit(solution)/shard_map/ppermute | solution.py:12
  311.7 10.0 %collective-permute-start.24 = (bf16[1,136,512]{2,1,0:T(8,128)(2,1)S(1)}, bf16[1,136,512]{2,1,0:T(8,128)(2,1)S(1)}, u32[]{:S(2)}, u32[]{:S(2)}) collective-permute-start(bf16[1,136,512]{2,1,0:T(8,128)(2,1)S(1)} %get-tuple-element.105), channel_id=1, source_target_pairs={{1,0},{2,1},{3,2},{4,3},{5,4},{6,5},{7,6},{8,7},{9,8},{10,9},{11,1... | collective-permute-start | bytes 417800 | tf_op jit(solution)/shard_map/ppermute | solution.py:15
  327.3 15.3 %collective-permute-start.25 = (bf16[4,136,512]{2,1,0:T(8,128)(2,1)S(1)}, bf16[4,136,512]{2,1,0:T(8,128)(2,1)S(1)}, u32[]{:S(2)}, u32[]{:S(2)}) collective-permute-start(bf16[4,136,512]{2,1,0:T(8,128)(2,1)S(1)} %select_convert_fusion), channel_id=1, source_target_pairs={{0,32},{32,64},{64,96},{1,33},{33,65},{65,97},{2,34},{34,66},{66,9... | collective-permute-start | bytes 1671176 | tf_op jit(solution)/shard_map/ppermute | solution.py:40
  342.8 7.4 %collective-permute-start.26 = (bf16[1,136,512]{2,1,0:T(8,128)(2,1)S(1)}, bf16[1,136,512]{2,1,0:T(8,128)(2,1)S(1)}, u32[]{:S(2)}, u32[]{:S(2)}) collective-permute-start(bf16[1,136,512]{2,1,0:T(8,128)(2,1)S(1)} %get-tuple-element.102), channel_id=1, source_target_pairs={{0,1},{1,2},{2,3},{3,4},{4,5},{5,6},{6,7},{7,8},{8,9},{9,10},{10,1... | collective-permute-start | bytes 417800 | tf_op jit(solution)/shard_map/ppermute | solution.py:12
  344.7 10.0 %collective-permute-start.27 = (bf16[1,136,512]{2,1,0:T(8,128)(2,1)S(1)}, bf16[1,136,512]{2,1,0:T(8,128)(2,1)S(1)}, u32[]{:S(2)}, u32[]{:S(2)}) collective-permute-start(bf16[1,136,512]{2,1,0:T(8,128)(2,1)S(1)} %get-tuple-element.103), channel_id=1, source_target_pairs={{1,0},{2,1},{3,2},{4,3},{5,4},{6,5},{7,6},{8,7},{9,8},{10,9},{11,1... | collective-permute-start | bytes 417800 | tf_op jit(solution)/shard_map/ppermute | solution.py:15
  (30 other events, 217.0 us)
where the time goes:
time: 368 us; the launch traced here: 361 us
  waiting for transfers between devices  158 us (43%)
  starting transfers between devices  90.2 us (25%)
  matrix products  38.1 us (10%)
  blocking collectives  28.7 us (8%)
  local copies, waits for them, and re-layouts  23.9 us (6%)
  other arithmetic  20.8 us (6%)
    ppermute x6, waiting for transfers between devices, passed_along(): lax.ppermute(value, axis, [(source, source + steps) for source in range(f...  75.4 us
    ppermute x11, waiting for transfers between devices, padded_2(): lax.ppermute(lax.slice_in_dim(block, 0, width, axis=dim), axis, backward)  48.6 us
    ppermute x11, starting transfers between devices, padded_2(): lax.ppermute(lax.slice_in_dim(block, 0, width, axis=dim), axis, backward)  43.9 us
    dot_general x81, matrix products, conv_valid(): jnp.dot(window, weight[row_off, col_off], preferred_element_type=jnp.floa...  36.9 us
    all_to_all x1, blocking collectives, from_everyone(): lax.all_to_all(jnp.broadcast_to(shard[None], (devices, *shard.shape)), ax...  28.7 us
    all_to_all x1, waiting for transfers between devices, shards(): lax.all_to_all(banded, 'strip', split_axis=1, concat_axis=2, tiled=True)  26.9 us
    ppermute x11, starting transfers between devices, padded_2(): lax.ppermute(lax.slice_in_dim(block, block.shape[dim] - width, None, axis...  26.4 us
    ppermute x6, starting transfers between devices, passed_along(): lax.ppermute(value, axis, [(source, source + steps) for source in range(f...  11.9 us
  transfers between devices with their start and end apart: 29, of which 25 were waited for; matrix products, arithmetic and copies ran while one was open for 1% of the time, Pallas kernels for 0%

commit v1 on v0

v1 whole, which is shorter than its diff:
```python
import functools

import jax
import jax.numpy as jnp
from jax import lax
from jax.experimental import pallas as pl
from jax.experimental.pallas import tpu as pltpu
from jax.sharding import PartitionSpec as P

AXES = ("segment", "strip")
F32 = jnp.float32
BF16 = jnp.bfloat16
VMEM = pltpu.VMEM


def vmem_spec():
    return pl.BlockSpec(memory_space=pltpu.VMEM)


def smem_spec():
    return pl.BlockSpec(memory_space=pltpu.SMEM)


def any_spec():
    return pl.BlockSpec(memory_space=pl.ANY)


def stem_kernel(place, feat, up, down, left, right, w1, w2, wd, out, s1, x1, s2, x2, s3, dbuf):
    halo = 6
    rows = feat.shape[0]
    cols = feat.shape[1]
    ch = feat.shape[2]
    full = rows + 2 * halo
    row_base = place[0]
    total_rows = place[1]
    left_edge = place[2]
    right_edge = place[3]
    pitch = s1.shape[1] // full
    width = cols + 8
    lanes = s1.shape[2]

    s1d = s1.reshape(ch // lanes, full, pitch, lanes)
    for k in range(ch // lanes):
        at = slice(k * lanes, (k + 1) * lanes)
        s1d[k, 0:halo, 8 : 8 + cols, :] = up[:, :, at].astype(F32)
        s1d[k, halo : halo + rows, 8 : 8 + cols, :] = feat[:, :, at].astype(F32)
        s1d[k, halo + rows : full, 8 : 8 + cols, :] = down[:, :, at].astype(F32)
        for j in range(2):
            s1[k, pl.ds(6 + j, full, stride=pitch), :] = left[j, :, at].astype(F32)
            s1[k, pl.ds(8 + cols + j, full, stride=pitch), :] = right[j, :, at].astype(F32)

    step = 19

    def shift1(i, carry):
        r = i * step
        for c in range(3):
            for k in range(ch // lanes):
                x1[pl.ds(r, step), :, c * ch + k * lanes : c * ch + (k + 1) * lanes] = s1d[
                    k, pl.ds(r, step), 6 + c : 6 + c + width, :
                ].astype(BF16)
        return carry

    lax.fori_loop(0, full // step, shift1, 0)

    out1 = full - 2
    block1 = 37
    s2d = s2.reshape(out1, pitch, ch)

    def layer1(i, carry):
        r = i * block1
        acc = None
        for a in range(3):
            part = jnp.dot(
                x1[pl.ds(r + a, block1)].reshape(block1 * width, 3 * ch),
                w1[a],
                preferred_element_type=F32,
            )
            acc = part if acc is None else acc + part
        acc = acc.reshape(block1, width, ch)
        y = jnp.maximum(acc + x1[pl.ds(r + 1, block1), :, ch : 2 * ch].astype(F32), 0.0)
        row = row_base + 1 + r + lax.broadcasted_iota(jnp.int32, (block1, width, 1), 0)
        col = lax.broadcasted_iota(jnp.int32, (block1, width, 1), 1) - 1
        ok = (row >= 0) & (row < total_rows)
        ok = ok & ((col >= 0) | (left_edge == 0)) & ((col < cols) | (right_edge == 0))
        y = jnp.where(ok, y, 0.0)
        s2d[pl.ds(r, block1), 8 : 8 + width, :] = y.astype(BF16).astype(F32)
        return carry

    lax.fori_loop(0, out1 // block1, layer1, 0)

    def shift2(i, carry):
        r = i * block1
        for c in range(3):
            x2[pl.ds(r, block1), :, c * ch : (c + 1) * ch] = s2d[
                pl.ds(r, block1), 8 + c : 8 + c + cols, :
            ].astype(BF16)
        return carry

    lax.fori_loop(0, out1 // block1, shift2, 0)

    out2 = out1 - 2
    block2 = 36

    def layer2(i, carry):
        r = i * block2
        acc = None
        for a in range(3):
            part = jnp.dot(
                x2[pl.ds(r + a, block2)].reshape(block2 * cols, 3 * ch),
                w2[a],
                preferred_element_type=F32,
            )
            acc = part if acc is None else acc + part
        res = x2[pl.ds(r + 1, block2), :, ch : 2 * ch].reshape(block2 * cols, ch).astype(F32)
        y = jnp.maximum(acc + res, 0.0)
        y = y.astype(BF16).astype(F32)
        for k in range(ch // lanes):
            s3[k, pl.ds(i * (block2 * cols), block2 * cols), :] = y[:, k * lanes : (k + 1) * lanes]
        return carry

    lax.fori_loop(0, out2 // block2, layer2, 0)

    zrows = out2 // 2
    zcols = cols // 2

    for a in range(2):
        for c in range(2):
            for k in range(ch // lanes):
                at = (a * 2 + c) * ch + k * lanes
                for i in range(zrows):
                    dbuf[i * zcols : (i + 1) * zcols, at : at + lanes] = s3[
                        k, pl.ds((2 * i + a) * cols + c, zcols, stride=2), :
                    ].astype(BF16)
    z = jnp.maximum(jnp.dot(dbuf[...], wd[...], preferred_element_type=F32), 0.0)
    z = z.reshape(zrows, zcols, z.shape[-1])
    zrow = row_base // 2 + 1 + lax.broadcasted_iota(jnp.int32, (zrows, zcols, 1), 0)
    z = jnp.where((zrow >= 0) & (zrow < total_rows // 2), z, 0.0).astype(BF16)
    slots = out.shape[0]
    depth = out.shape[1]
    own = (zrows - 4) // slots
    for b in range(slots):
        out[b] = z[own * b : own * b + depth]


def stem(place, feat, up, down, left, right, w1, w2, wd, slots):
    rows, cols, ch = feat.shape
    full = rows + 12
    out_ch = wd.shape[1]
    own = rows // 2 // slots
    flops = 2 * (74 * 24 + 72 * 16) * 9 * ch * ch
    return pl.pallas_call(
        stem_kernel,
        out_shape=jax.ShapeDtypeStruct((slots, own + 4, cols // 2, out_ch), BF16),
        in_specs=[smem_spec()] + [vmem_spec()] * 8,
        out_specs=vmem_spec(),
        scratch_shapes=[
            VMEM((ch // 128, full * 32, 128), F32),
            VMEM((full, 24, 3 * ch), BF16),
            VMEM(((full - 2) * 32, ch), F32),
            VMEM((full - 2, 16, 3 * ch), BF16),
            VMEM((ch // 128, (full - 4) * 16, 128), F32),
            VMEM(((full - 4) // 2 * 8, 4 * ch), BF16),
        ],
        compiler_params=pltpu.CompilerParams(vmem_limit_bytes=48 * 2**20),
        cost_estimate=pl.CostEstimate(flops=flops, bytes_accessed=4 * 2**20, transcendentals=0),
        name="stem",
    )(place, feat, up, down, left, right, w1, w2, wd)


EDGE = 8


def duo_body(place, fill, own_w, peer_w, keep, send, full, scratch, window):
    s1, x1, s2, x2, wa, wb, za, zb, zf, sems = scratch
    core = place[1]
    row0, row_total, col0, col_total = place[2], place[3], place[4], place[5]
    rows_in, width, wide = x1.shape
    ch = wide // 3

    @pl.when(core == 0)
    def _():
        pltpu.make_async_copy(own_w, wa, sems.at[0]).start()
        pltpu.make_async_copy(peer_w, wb, sems.at[1]).start()

    @pl.when(core == 1)
    def _():
        pltpu.make_async_copy(peer_w, wa, sems.at[0]).start()
        pltpu.make_async_copy(own_w, wb, sems.at[1]).start()

    fill(s1)

    def shift(src, dst):
        def go(r, carry):
            for c in range(3):
                dst[r, :, c * ch : (c + 1) * ch] = src[
                    r, EDGE - 1 + c : EDGE - 1 + c + width, :
                ].astype(BF16)
            return carry

        lax.fori_loop(0, dst.shape[0], go, 0)

    def layer(x, w, r, first_row):
        acc = None
        for a in range(3):
            part = jnp.dot(
                x[pl.ds(r + a, 2)].reshape(2 * width, 3 * ch), w[a], preferred_element_type=F32
            )
            acc = part if acc is None else acc + part
        acc = acc.reshape(2, width, ch)
        y = jnp.maximum(acc + x[pl.ds(r + 1, 2), :, ch : 2 * ch].astype(F32), 0.0)
        row = first_row + r + lax.broadcasted_iota(jnp.int32, (2, width, 1), 0)
        col = col0 + lax.broadcasted_iota(jnp.int32, (2, width, 1), 1)
        ok = (row >= 0) & (row < row_total) & (col >= 0) & (col < col_total)
        return jnp.where(ok, y, 0.0).astype(BF16)

    shift(s1, x1)
    pltpu.make_async_copy(own_w, wa, sems.at[0]).wait()
    rows_mid = rows_in - 2

    def first(i, carry):
        r = 2 * i
        y = layer(x1, wa, r, row0 + 1)
        s2[pl.ds(r, 2), EDGE : EDGE + width, :] = y.astype(F32)
        return carry

    lax.fori_loop(0, rows_mid // 2, first, 0)
    shift(s2, x2)
    rows_out = rows_mid - 2
    za[...] = x2[1 : 1 + rows_out, EDGE : width - EDGE, ch : 2 * ch]
    pltpu.make_async_copy(own_w, wb, sems.at[1]).wait()

    def second(i, carry):
        r = 2 * i
        y = layer(x2, wb, r, row0 + 2)
        zf[pl.ds(r, 2)] = y
        return carry

    lax.fori_loop(0, rows_out // 2, second, 0)
    zb[...] = zf[:, EDGE : width - EDGE, :]

    half = width - 2 * EDGE

    @pl.when(core == 0)
    def _():
        pltpu.make_async_copy(za, keep.at[window, :, pl.ds(0, half), :], sems.at[2]).start()
        pltpu.make_async_copy(zb, send.at[window], sems.at[3]).start()

    @pl.when(core == 1)
    def _():
        pltpu.make_async_copy(zb, keep.at[window, :, pl.ds(half, half), :], sems.at[2]).start()
        pltpu.make_async_copy(za, send.at[window], sems.at[3]).start()

    if full is not None:
        copy = pltpu.make_async_copy(zf, full, sems.at[4])
        copy.start()
        copy.wait()
    pltpu.make_async_copy(za, keep.at[window, :, pl.ds(0, half), :], sems.at[2]).wait()
    pltpu.make_async_copy(zb, send.at[window], sems.at[3]).wait()


def clear_edges(s, width):
    rows = s.shape[0]
    s[:, 0:EDGE, :] = jnp.zeros((rows, EDGE, s.shape[2]), F32)
    s[:, EDGE + width :, :] = jnp.zeros((rows, EDGE, s.shape[2]), F32)


def early_kernel(window, chained, *refs):
    place, lo, hi, side, own_w, peer_w = refs[:6]
    refs = refs[6 + (2 if chained else 0) :]
    keep, send, full = refs[:3]
    scratch = refs[3:]
    s1, x1, s2 = scratch[0], scratch[1], scratch[2]
    width = x1.shape[1]
    block = lo.shape[2]

    def fill(s):
        clear_edges(s, width)
        clear_edges(s2, width)
        parts = lo.shape[0]

        def row(r, carry):
            for e in range(parts):
                at = 2 * EDGE + block * e
                s[r, at : at + block, :] = lo[e, r].astype(F32)
                at = at + block * parts
                s[r, at : at + block, :] = hi[e, r].astype(F32)
            on_left = place[1] == 1
            edge = side[r].astype(F32)
            s[r, EDGE : 2 * EDGE, :] = jnp.where(on_left, edge, 0.0)
            s[r, width : width + EDGE, :] = jnp.where(on_left, 0.0, edge)
            return carry

        lax.fori_loop(0, s.shape[0], row, 0)

    @pl.when(place[0] == 1)
    def _():
        duo_body(place, fill, own_w, peer_w, keep, send, full, scratch, window)


def late_kernel(window, *refs):
    place, above, main, below, own_w, peer_w, _, _ = refs[:8]
    keep, send = refs[8:10]
    scratch = refs[10:]
    x1, s2 = scratch[1], scratch[2]
    width = x1.shape[1]

    def fill(s):
        clear_edges(s, width)
        clear_edges(s2, width)
        rim = above.shape[0]
        mid = main.shape[0]
        s[0:rim, EDGE : EDGE + width, :] = above[...].astype(F32)
        s[rim : rim + mid, EDGE : EDGE + width, :] = main[...].astype(F32)
        s[rim + mid :, EDGE : EDGE + width, :] = below[...].astype(F32)

    @pl.when(place[0] == 1)
    def _():
        duo_body(place, fill, own_w, peer_w, keep, send, None, scratch, window)


def duo_scratch(rows, width, ch):
    return [
        VMEM((rows + 4, width + 2 * EDGE, ch), F32),
        VMEM((rows + 4, width, 3 * ch), BF16),
        VMEM((rows + 2, width + 2 * EDGE, ch), F32),
        VMEM((rows + 2, width, 3 * ch), BF16),
        VMEM((3, 3 * ch, ch), BF16),
        VMEM((3, 3 * ch, ch), BF16),
        VMEM((rows, width - 2 * EDGE, ch), BF16),
        VMEM((rows, width - 2 * EDGE, ch), BF16),
        VMEM((rows, width, ch), BF16),
        pltpu.SemaphoreType.DMA((5,)),
    ]


def duo_params(rows, width, ch):
    flops = 2 * (2 * rows + 2) * width * 9 * ch * ch
    return dict(
        compiler_params=pltpu.CompilerParams(vmem_limit_bytes=48 * 2**20),
        cost_estimate=pl.CostEstimate(flops=flops, bytes_accessed=12 * 2**20, transcendentals=0),
    )


def early(window, place, lo, hi, side, own_w, peer_w, buffers, windows, rows, half):
    ch = lo.shape[-1]
    width = half + 2 * EDGE
    chained = buffers is not None
    return pl.pallas_call(
        functools.partial(early_kernel, window, chained),
        out_shape=(
            jax.ShapeDtypeStruct((windows, rows, 2 * half, ch), BF16),
            jax.ShapeDtypeStruct((windows, rows, half, ch), BF16),
            jax.ShapeDtypeStruct((rows, width, ch), BF16),
        ),
        in_specs=[smem_spec()] + [vmem_spec()] * 3 + [any_spec()] * (4 if chained else 2),
        out_specs=(any_spec(), any_spec(), any_spec()),
        scratch_shapes=duo_scratch(rows, width, ch),
        input_output_aliases={6: 0, 7: 1} if chained else {},
        name=f"early{window}",
        **duo_params(rows, width, ch),
    )(place, lo, hi, side, own_w, peer_w, *(buffers or ()))


def late(window, place, above, main, below, own_w, peer_w, buffers):
    rows, width, ch = main.shape
    return pl.pallas_call(
        functools.partial(late_kernel, window),
        out_shape=tuple(jax.ShapeDtypeStruct(b.shape, b.dtype) for b in buffers),
        in_specs=[smem_spec()] + [vmem_spec()] * 3 + [any_spec()] * 4,
        out_specs=(any_spec(), any_spec()),
        scratch_shapes=duo_scratch(rows, width, ch),
        input_output_aliases={6: 0, 7: 1},
        name=f"late{window}",
        **duo_params(rows, width, ch),
    )(place, above, main, below, own_w, peer_w, *buffers)


def shards(features, weight_first, weight_second, weight_down, section_weights):
    segments = lax.axis_size("segment")
    strips = lax.axis_size("strip")
    seg = lax.axis_index("segment")
    strip = lax.axis_index("strip")
    windows, tile_rows, tile_cols, c1 = features.shape
    c2 = weight_down.shape[3]
    group = strips // segments
    strip_rows = segments * tile_rows // 2 // strips
    total_cols = strips * tile_cols // 2
    half = total_cols // 2
    core = lax.rem(seg, 2)
    far = seg // 2
    i32 = jnp.int32

    def device(s, c):
        return s * strips + c

    own_w = section_weights.reshape(3, 3 * c2, c2)
    peer_w = lax.ppermute(own_w, "segment", [(s, s ^ 1) for s in range(segments)])

    rim_r, rim_c = 6, 2
    ahead = [(s, s + 1) for s in range(segments - 1)]
    back = [(b, a) for a, b in ahead]
    up = lax.ppermute(features[:, tile_rows - rim_r :], "segment", ahead)
    down = lax.ppermute(features[:, :rim_r], "segment", back)

    def side(sl):
        piece = jnp.concatenate([up[:, :, sl], features[:, :, sl], down[:, :, sl]], axis=1)
        return jnp.swapaxes(piece, 1, 2)

    along = [(c, c + 1) for c in range(strips - 1)]
    against = [(b, a) for a, b in along]
    left = lax.ppermute(side(slice(tile_cols - rim_c, tile_cols)), "strip", along)
    right = lax.ppermute(side(slice(0, rim_c)), "strip", against)

    stem_place = jnp.stack(
        [
            seg * tile_rows - rim_r,
            i32(segments * tile_rows),
            (strip == 0).astype(i32),
            (strip == strips - 1).astype(i32),
        ]
    ).astype(i32)
    w1 = weight_first.reshape(3, 3 * c1, c1)
    w2 = weight_second.reshape(3, 3 * c1, c1)
    wd = weight_down.reshape(4 * c1, c2)

    groups = [[g * group + i for i in range(group)] for g in range(segments)]
    low, high, edge = [], [], []
    for s in range(segments):
        for d in range(segments):
            for b in range(group):
                src, dst = device(s, d * group + b), device(d // 2, s * group + b)
                (low if d % 2 == 0 else high).append((src, dst))
                if d == 2:
                    edge.append((src, device(0, s * group + b)))
                if d == 1:
                    edge.append((src, device(1, s * group + b)))
    quarter = strip // group

    tiles = []
    for w in range(windows):
        z = stem(stem_place, features[w], up[w], down[w], left[w], right[w], w1, w2, wd, group)
        shape = z.shape
        got = lax.all_to_all(
            z.reshape(-1, *shape[2:]), "strip", 0, 0, axis_index_groups=groups, tiled=True
        ).reshape(shape)
        lo = lax.ppermute(got, AXES, low)
        hi = lax.ppermute(got, AXES, high)
        pick = jnp.where(quarter == 2, got[0], got[group - 1])
        tiles.append((lo, hi, lax.ppermute(pick, AXES, edge)))

    common = [
        core,
        strip * strip_rows - 2,
        i32(segments * tile_rows // 2),
        core * half - EDGE,
        i32(total_cols),
    ]
    early_place = jnp.stack([(far == 0).astype(i32), *common]).astype(i32)
    late_place = jnp.stack([(far == 1).astype(i32), *common]).astype(i32)

    buffers = None
    passed = []
    across = [
        (device(h, t), device(h + 2, t)) for h in range(2) for t in range(strips)
    ]
    for w in range(windows):
        keep, send, full = early(
            w, early_place, *tiles[w], own_w, peer_w, buffers, windows, strip_rows, half
        )
        buffers = (keep, send)
        passed.append(lax.ppermute(full, AXES, across))
    later = [(device(s, a), device(s, b)) for s in (2, 3) for a, b in along]
    sooner = [(b, a) for a, b in later]
    for w in range(windows):
        main = passed[w]
        above = lax.ppermute(main[strip_rows - 2 :], AXES, later)
        below = lax.ppermute(main[:2], AXES, sooner)
        buffers = late(w, late_place, above, main, below, own_w, peer_w, buffers)
    keep, send = buffers
    other = lax.ppermute(send, "segment", [(s, s ^ 1) for s in range(segments)])
    zero = i32(0)
    result = lax.dynamic_update_slice(keep, other, (zero, zero, (1 - core) * half, zero))
    return result[None]


def solution(mesh):
    return jax.shard_map(
        shards,
        mesh=mesh,
        in_specs=(
            P(None, "segment", "strip", None),
            P(),
            P(),
            P(),
            P("segment", None, None, None, None),
        ),
        out_specs=P("segment", None, "strip", None, None),
        check_vma=False,
    )
```

time: 368 us -> 161 us (0.44)
  the two profiles are of different devices: /device:TPU:102 before, /device:TPU:29 now
where the time goes in v1:
time: 161 us; the launch traced here: 160 us
  starting transfers between devices  69 us (43%)
  waiting for transfers between devices  41 us (25%)
  Pallas kernels  39.7 us (25%)
  local copies, waits for them, and re-layouts  8.74 us (5%)
    pallas_call x2, Pallas kernels, late(): pl.pallas_call(functools.partial(late_kernel, window), out_shape=tuple((j...  24.2 us
    ppermute x2, starting transfers between devices, shards(): hi = lax.ppermute(got, AXES, high)  23.6 us
    ppermute x2, waiting for transfers between devices, shards(): passed.append(lax.ppermute(full, AXES, across))  23 us
    pallas_call x2, Pallas kernels, stem(): pl.pallas_call(stem_kernel, out_shape=jax.ShapeDtypeStruct((slots, own +...  14.4 us
    all_to_all x2, starting transfers between devices, shards(): lax.all_to_all(z.reshape(-1, *shape[2:]), 'strip', 0, 0, axis_index_group...  9.16 us
    ppermute x2, waiting for transfers between devices, shards(): hi = lax.ppermute(got, AXES, high)  8.65 us
    ppermute x2, starting transfers between devices, shards(): above = lax.ppermute(main[strip_rows - 2:], AXES, later)  8.4 us
    ppermute x2, starting transfers between devices, shards(): below = lax.ppermute(main[:2], AXES, sooner)  8.35 us
  transfers between devices with their start and end apart: 20, of which 6 were waited for; matrix products, arithmetic and copies ran while one was open for 5% of the time, Pallas kernels for 17%

profile of v1, /device:TPU:29, one launch (start us, length us, event | category | flops | bytes accessed | tf_op | source)
XLA Modules:
  0.0 160.0 jit_solution(6700834698379920986)
XLA Ops:
  4.3 3.0 %collective-permute-start.1 = (bf16[2,6,16,256]{3,1,2,0:T(8,128)(2,1)}, bf16[2,6,16,256]{3,1,2,0:T(8,128)(2,1)S(1)}, u32[]{:S(2)}, u32[]{:S(2)}) collective-permute-start(bf16[2,6,16,256]{3,1,2,0:T(8,128)(2,1)} %copy.21), channel_id=1, source_target_pairs={{32,0},{64,32},{96,64},{33,1},{65,33},{97,65},{34,2},{66,34},{98,6... | collective-permute-start | bytes 294920 | tf_op jit(solution)/shard_map/ppermute | solution.py:403
  7.4 1.4 fusion
  8.9 1.4 slice_bitcast_fusion
  10.5 6.5 %collective-permute-start.3 = (bf16[2,2,76,256]{3,2,1,0:T(8,128)(2,1)S(1)}, bf16[2,2,76,256]{3,2,1,0:T(8,128)(2,1)S(1)}, u32[]{:S(2)}, u32[]{:S(2)}) collective-permute-start(bf16[2,2,76,256]{3,2,1,0:T(8,128)(2,1)S(1)} %maximum_bitcast_fusion.1), channel_id=1, source_target_pairs={{1,0},{2,1},{3,2},{4,3},{5,4},{6,5},{7,6},{8,7},{9,8},{10,9},{11,1... | collective-permute-start | bytes 466952 | tf_op jit(solution)/shard_map/ppermute | solution.py:412
  17.0 1.9 %collective-permute-start.2 = (bf16[2,2,76,256]{3,2,1,0:T(8,128)(2,1)S(1)}, bf16[2,2,76,256]{3,2,1,0:T(8,128)(2,1)S(1)}, u32[]{:S(2)}, u32[]{:S(2)}) collective-permute-start(bf16[2,2,76,256]{3,2,1,0:T(8,128)(2,1)S(1)} %maximum_bitcast_fusion), channel_id=1, source_target_pairs={{0,1},{1,2},{2,3},{3,4},{4,5},{5,6},{6,7},{7,8},{8,9},{9,10},{10,1... | collective-permute-start | bytes 466952 | tf_op jit(solution)/shard_map/ppermute | solution.py:411
  19.2 6.9 %collective-permute-done.2 = bf16[2,2,76,256]{3,2,1,0:T(8,128)(2,1)S(1)} collective-permute-done((bf16[2,2,76,256]{3,2,1,0:T(8,128)(2,1)S(1)}, bf16[2,2,76,256]{3,2,1,0:T(8,128)(2,1)S(1)}, u32[]{:S(2)}, u32[]{:S(2)}) %collective-permute-start.2) | collective-permute-done | bytes 155680 | tf_op jit(solution)/shard_map/ppermute | solution.py:411
  26.1 7.2 %stem.3 = bf16[8,8,8,512]{3,2,1,0:T(8,128)(2,1)} custom-call(s32[4]{0:T(128)S(1)} %pad_add_fusion.place, bf16[64,16,256]{2,1,0:T(8,128)(2,1)S(1)} %get-tuple-element.25.feat, bf16[6,16,256]{2,1,0:T(8,128)(2,1)S(1)} %copy.18.up, bf16[6,16,256]{2,1,0:T(8,128)(2,1)S(1)} %copy.19.down, bf16[2,76,256]{2,1,0:T(8,128)(2,1)S(1)} %get-tuple-element.37.left, ...), custom_call_target="tpu_custom_call" | custom-call | flops 3454009344 | bytes 4194304 | tf_op jit(solution)/shard_map/stem/pallas_call | solution.py:151
  33.3 4.1 %all-to-all-start.1 = ((bf16[64,8,512]{2,1,0:T(8,128)(2,1)}), bf16[64,8,512]{2,1,0:T(8,128)(2,1)}, u32[]{:S(2)}, u32[]{:S(2)}) async-start(bf16[64,8,512]{2,1,0:T(8,128)(2,1)} %bitcast.26), calls=%async_computation.1 | async-start | bytes 1048576 | tf_op jit(solution)/shard_map/all_to_all | solution.py:443
  38.7 7.2 %stem.2 = bf16[8,8,8,512]{3,2,1,0:T(8,128)(2,1)} custom-call(s32[4]{0:T(128)S(1)} %pad_add_fusion.place, bf16[64,16,256]{2,1,0:T(8,128)(2,1)S(1)} %get-tuple-element.26.feat, bf16[6,16,256]{2,1,0:T(8,128)(2,1)S(1)} %copy.16.up, bf16[6,16,256]{2,1,0:T(8,128)(2,1)S(1)} %copy.17.down, bf16[2,76,256]{2,1,0:T(8,128)(2,1)S(1)} %get-tuple-element.38.left, ...), custom_call_target="tpu_custom_call" | custom-call | flops 3454009344 | bytes 4194304 | tf_op jit(solution)/shard_map/stem/pallas_call | solution.py:151
  45.9 5.0 %all-to-all-start = ((bf16[64,8,512]{2,1,0:T(8,128)(2,1)}), bf16[64,8,512]{2,1,0:T(8,128)(2,1)S(1)}, u32[]{:S(2)}, u32[]{:S(2)}) async-start(bf16[64,8,512]{2,1,0:T(8,128)(2,1)} %bitcast.18), calls=%async_computation | async-start | bytes 1048576 | tf_op jit(solution)/shard_map/all_to_all | solution.py:443
  51.6 7.3 %collective-permute-start.9 = (bf16[8,8,8,512]{3,2,1,0:T(8,128)(2,1)}, bf16[8,8,8,512]{3,2,1,0:T(8,128)(2,1)S(1)}, u32[]{:S(2)}, u32[]{:S(2)}) collective-permute-start(bf16[8,8,8,512]{3,2,1,0:T(8,128)(2,1)} %bitcast.27), channel_id=1, source_target_pairs={{8,0},{9,1},{10,2},{11,3},{12,4},{13,5},{14,6},{15,7},{24,32},{25,... | collective-permute-start | bytes 1572872 | tf_op jit(solution)/shard_map/ppermute | solution.py:447
  61.4 16.2 %collective-permute-start.5 = (bf16[8,8,8,512]{3,2,1,0:T(8,128)(2,1)S(1)}, bf16[8,8,8,512]{3,2,1,0:T(8,128)(2,1)S(1)}, u32[]{:S(2)}, u32[]{:S(2)}) collective-permute-start(bf16[8,8,8,512]{3,2,1,0:T(8,128)(2,1)S(1)} %bitcast.50), channel_id=1, source_target_pairs={{8,0},{9,1},{10,2},{11,3},{12,4},{13,5},{14,6},{15,7},{24,32},{25,... | collective-permute-start | bytes 1572872 | tf_op jit(solution)/shard_map/ppermute | solution.py:447
  78.9 1.3 collective-permute-start.14
  80.3 8.6 %collective-permute-done.5.refs_2_ = bf16[8,8,8,512]{3,2,1,0:T(8,128)(2,1)S(1)} collective-permute-done((bf16[8,8,8,512]{3,2,1,0:T(8,128)(2,1)S(1)}, bf16[8,8,8,512]{3,2,1,0:T(8,128)(2,1)S(1)}, u32[]{:S(2)}, u32[]{:S(2)}) %collective-permute-start.5) | collective-permute-done | bytes 524320 | tf_op jit(solution)/shard_map/ppermute | solution.py:447
  89.5 1.3 collective-permute-start.11
  90.8 15.0 %collective-permute-done.14.refs_2_ = bf16[4,144,512]{2,1,0:T(8,128)(2,1)S(1)} collective-permute-done((bf16[4,144,512]{2,1,0:T(8,128)(2,1)S(1)}, bf16[4,144,512]{2,1,0:T(8,128)(2,1)S(1)}, u32[]{:S(2)}, u32[]{:S(2)}) %collective-permute-start.14) | collective-permute-done | bytes 589856 | tf_op jit(solution)/shard_map/ppermute | solution.py:471
  106.7 4.4 %collective-permute-start.15 = (bf16[2,144,512]{2,1,0:T(8,128)(2,1)}, bf16[2,144,512]{2,1,0:T(8,128)(2,1)S(1)}, u32[]{:S(2)}, u32[]{:S(2)}) collective-permute-start(bf16[2,144,512]{2,1,0:T(8,128)(2,1)} %get-tuple-element.32), channel_id=1, source_target_pairs={{64,65},{65,66},{66,67},{67,68},{68,69},{69,70},{70,71},{71,72},{7... | collective-permute-start | bytes 884744 | tf_op jit(solution)/shard_map/ppermute | solution.py:476
  111.1 3.9 %collective-permute-start.16 = (bf16[2,144,512]{2,1,0:T(8,128)(2,1)}, bf16[2,144,512]{2,1,0:T(8,128)(2,1)S(1)}, u32[]{:S(2)}, u32[]{:S(2)}) collective-permute-start(bf16[2,144,512]{2,1,0:T(8,128)(2,1)} %get-tuple-element.31), channel_id=1, source_target_pairs={{65,64},{66,65},{67,66},{68,67},{69,68},{70,69},{71,70},{72,71},{7... | collective-permute-start | bytes 884744 | tf_op jit(solution)/shard_map/ppermute | solution.py:477
  115.0 8.0 %collective-permute-done.11.refs_2_ = bf16[4,144,512]{2,1,0:T(8,128)(2,1)S(1)} collective-permute-done((bf16[4,144,512]{2,1,0:T(8,128)(2,1)S(1)}, bf16[4,144,512]{2,1,0:T(8,128)(2,1)S(1)}, u32[]{:S(2)}, u32[]{:S(2)}) %collective-permute-start.11) | collective-permute-done | bytes 589856 | tf_op jit(solution)/shard_map/ppermute | solution.py:471
  123.1 4.0 %collective-permute-start.12 = (bf16[2,144,512]{2,1,0:T(8,128)(2,1)S(1)}, bf16[2,144,512]{2,1,0:T(8,128)(2,1)S(1)}, u32[]{:S(2)}, u32[]{:S(2)}) collective-permute-start(bf16[2,144,512]{2,1,0:T(8,128)(2,1)S(1)} %get-tuple-element.34), channel_id=1, source_target_pairs={{64,65},{65,66},{66,67},{67,68},{68,69},{69,70},{70,71},{71,72},{7... | collective-permute-start | bytes 884744 | tf_op jit(solution)/shard_map/ppermute | solution.py:476
  127.1 4.5 %collective-permute-start.13 = (bf16[2,144,512]{2,1,0:T(8,128)(2,1)S(1)}, bf16[2,144,512]{2,1,0:T(8,128)(2,1)S(1)}, u32[]{:S(2)}, u32[]{:S(2)}) collective-permute-start(bf16[2,144,512]{2,1,0:T(8,128)(2,1)S(1)} %get-tuple-element.33), channel_id=1, source_target_pairs={{65,64},{66,65},{67,66},{68,67},{69,68},{70,69},{71,70},{72,71},{7... | collective-permute-start | bytes 884744 | tf_op jit(solution)/shard_map/ppermute | solution.py:477
  131.6 12.1 %late0.1 = (bf16[2,4,256,512]{3,2,1,0:T(8,128)(2,1)}, bf16[2,4,128,512]{3,2,1,0:T(8,128)(2,1)S(1)}) custom-call(s32[6]{0:T(128)S(1)} %stack.53.refs_0_, bf16[2,144,512]{2,1,0:T(8,128)(2,1)S(1)} %collective-permute-done.15.refs_1_, bf16[4,144,512]{2,1,0:T(8,128)(2,1)S(1)} %collective-permute-done.14.refs_2_, ...), custom_call_target="tpu_custom_call", output_to_operand_aliasing={{0}: (6, {}), {1}: (7, {})} | custom-call | flops 6794772480 | bytes 12582912 | tf_op jit(solution)/shard_map/late0/pallas_call | solution.py:366
  143.7 12.1 %late1.1 = (bf16[2,4,256,512]{3,2,1,0:T(8,128)(2,1)}, bf16[2,4,128,512]{3,2,1,0:T(8,128)(2,1)S(1)}) custom-call(s32[6]{0:T(128)S(1)} %stack.53.refs_0_, bf16[2,144,512]{2,1,0:T(8,128)(2,1)S(1)} %collective-permute-done.12.refs_1_, bf16[4,144,512]{2,1,0:T(8,128)(2,1)S(1)} %collective-permute-done.11.refs_2_, ...), custom_call_target="tpu_custom_call", output_to_operand_aliasing={{0}: (6, {}), {1}: (7, {})} | custom-call | flops 6794772480 | bytes 12582912 | tf_op jit(solution)/shard_map/late1/pallas_call | solution.py:366
  156.7 2.3 %collective-permute-done.17 = bf16[2,4,128,512]{3,2,1,0:T(8,128)(2,1)S(1)} collective-permute-done((bf16[2,4,128,512]{3,2,1,0:T(8,128)(2,1)S(1)}, bf16[2,4,128,512]{3,2,1,0:T(8,128)(2,1)S(1)}, u32[]{:S(2)}, u32[]{:S(2)}) %collective-permute-start.17) | collective-permute-done | bytes 1048608 | tf_op jit(solution)/shard_map/ppermute | solution.py:480
  (57 shorter events, 13.9 us)
Async XLA Ops:
  0.0 78.3 %collective-permute-start.7 = (bf16[3,1536,512]{2,1,0:T(8,128)(2,1)}, bf16[3,1536,512]{2,1,0:T(8,128)(2,1)}, u32[]{:S(2)}, u32[]{:S(2)}) collective-permute-start(bf16[3,1536,512]{2,1,0:T(8,128)(2,1)} %bitcast.51), channel_id=1, source_target_pairs={{0,32},{32,0},{64,96},{96,64},{1,33},{33,1},{65,97},{97,65},{2,34}... | collective-permute-start | bytes 14155784 | tf_op jit(solution)/shard_map/ppermute | solution.py:397
  2.3 8.0 %collective-permute-start = (bf16[2,6,16,256]{3,1,2,0:T(8,128)(2,1)}, bf16[2,6,16,256]{3,1,2,0:T(8,128)(2,1)S(1)}, u32[]{:S(2)}, u32[]{:S(2)}) collective-permute-start(bf16[2,6,16,256]{3,1,2,0:T(8,128)(2,1)} %copy.20), channel_id=1, source_target_pairs={{0,32},{32,64},{64,96},{1,33},{33,65},{65,97},{2,34},{34,66},{66,9... | collective-permute-start | bytes 294920 | tf_op jit(solution)/shard_map/ppermute | solution.py:402
  4.3 6.1 %collective-permute-start.1 = (bf16[2,6,16,256]{3,1,2,0:T(8,128)(2,1)}, bf16[2,6,16,256]{3,1,2,0:T(8,128)(2,1)S(1)}, u32[]{:S(2)}, u32[]{:S(2)}) collective-permute-start(bf16[2,6,16,256]{3,1,2,0:T(8,128)(2,1)} %copy.21), channel_id=1, source_target_pairs={{32,0},{64,32},{96,64},{33,1},{65,33},{97,65},{34,2},{66,34},{98,6... | collective-permute-start | bytes 294920 | tf_op jit(solution)/shard_map/ppermute | solution.py:403
  8.8 17.3 %copy-start = (bf16[3,3,256,256]{3,2,1,0:T(8,128)(2,1)S(1)}, bf16[3,3,256,256]{3,2,1,0:T(8,128)(2,1)}, u32[]{:S(2)}) copy-start(bf16[3,3,256,256]{3,2,1,0:T(8,128)(2,1)} %param.6) | copy-start | bytes 3538948
  8.8 17.3 %copy-start.1 = (bf16[3,3,256,256]{3,2,1,0:T(8,128)(2,1)S(1)}, bf16[3,3,256,256]{3,2,1,0:T(8,128)(2,1)}, u32[]{:S(2)}) copy-start(bf16[3,3,256,256]{3,2,1,0:T(8,128)(2,1)} %param.7) | copy-start | bytes 3538948
  8.8 17.3 %copy-start.2 = (bf16[2,2,256,512]{3,2,1,0:T(8,128)(2,1)S(1)}, bf16[2,2,256,512]{3,2,1,0:T(8,128)(2,1)}, u32[]{:S(2)}) copy-start(bf16[2,2,256,512]{3,2,1,0:T(8,128)(2,1)} %param.8) | copy-start | bytes 3145732
  10.5 8.7 %collective-permute-start.3 = (bf16[2,2,76,256]{3,2,1,0:T(8,128)(2,1)S(1)}, bf16[2,2,76,256]{3,2,1,0:T(8,128)(2,1)S(1)}, u32[]{:S(2)}, u32[]{:S(2)}) collective-permute-start(bf16[2,2,76,256]{3,2,1,0:T(8,128)(2,1)S(1)} %maximum_bitcast_fusion.1), channel_id=1, source_target_pairs={{1,0},{2,1},{3,2},{4,3},{5,4},{6,5},{7,6},{8,7},{9,8},{10,9},{11,1... | collective-permute-start | bytes 466952 | tf_op jit(solution)/shard_map/ppermute | solution.py:412
  17.0 9.1 %collective-permute-start.2 = (bf16[2,2,76,256]{3,2,1,0:T(8,128)(2,1)S(1)}, bf16[2,2,76,256]{3,2,1,0:T(8,128)(2,1)S(1)}, u32[]{:S(2)}, u32[]{:S(2)}) collective-permute-start(bf16[2,2,76,256]{3,2,1,0:T(8,128)(2,1)S(1)} %maximum_bitcast_fusion), channel_id=1, source_target_pairs={{0,1},{1,2},{2,3},{3,4},{4,5},{5,6},{6,7},{7,8},{8,9},{9,10},{10,1... | collective-permute-start | bytes 466952 | tf_op jit(solution)/shard_map/ppermute | solution.py:411
  33.3 12.6 %all-to-all-start.1 = ((bf16[64,8,512]{2,1,0:T(8,128)(2,1)}), bf16[64,8,512]{2,1,0:T(8,128)(2,1)}, u32[]{:S(2)}, u32[]{:S(2)}) async-start(bf16[64,8,512]{2,1,0:T(8,128)(2,1)} %bitcast.26), calls=%async_computation.1 | async-start | bytes 1048576 | tf_op jit(solution)/shard_map/all_to_all | solution.py:443
  37.5 1.2 copy-start.3
  45.9 14.7 %all-to-all-start = ((bf16[64,8,512]{2,1,0:T(8,128)(2,1)}), bf16[64,8,512]{2,1,0:T(8,128)(2,1)S(1)}, u32[]{:S(2)}, u32[]{:S(2)}) async-start(bf16[64,8,512]{2,1,0:T(8,128)(2,1)} %bitcast.18), calls=%async_computation | async-start | bytes 1048576 | tf_op jit(solution)/shard_map/all_to_all | solution.py:443
  50.9 26.7 %collective-permute-start.8 = (bf16[8,8,8,512]{3,2,1,0:T(8,128)(2,1)}, bf16[8,8,8,512]{3,2,1,0:T(8,128)(2,1)S(1)}, u32[]{:S(2)}, u32[]{:S(2)}) collective-permute-start(bf16[8,8,8,512]{3,2,1,0:T(8,128)(2,1)} %bitcast.27), channel_id=1, source_target_pairs={{0,0},{1,1},{2,2},{3,3},{4,4},{5,5},{6,6},{7,7},{16,32},{17,33},{1... | collective-permute-start | bytes 1572872 | tf_op jit(solution)/shard_map/ppermute | solution.py:446
  51.6 26.7 %collective-permute-start.9 = (bf16[8,8,8,512]{3,2,1,0:T(8,128)(2,1)}, bf16[8,8,8,512]{3,2,1,0:T(8,128)(2,1)S(1)}, u32[]{:S(2)}, u32[]{:S(2)}) collective-permute-start(bf16[8,8,8,512]{3,2,1,0:T(8,128)(2,1)} %bitcast.27), channel_id=1, source_target_pairs={{8,0},{9,1},{10,2},{11,3},{12,4},{13,5},{14,6},{15,7},{24,32},{25,... | collective-permute-start | bytes 1572872 | tf_op jit(solution)/shard_map/ppermute | solution.py:447
  60.0 1.4 collective-permute-start.10
  60.7 19.6 %collective-permute-start.4 = (bf16[8,8,8,512]{3,2,1,0:T(8,128)(2,1)S(1)}, bf16[8,8,8,512]{3,2,1,0:T(8,128)(2,1)S(1)}, u32[]{:S(2)}, u32[]{:S(2)}) collective-permute-start(bf16[8,8,8,512]{3,2,1,0:T(8,128)(2,1)S(1)} %bitcast.49), channel_id=1, source_target_pairs={{0,0},{1,1},{2,2},{3,3},{4,4},{5,5},{6,6},{7,7},{16,32},{17,33},{1... | collective-permute-start | bytes 1572872 | tf_op jit(solution)/shard_map/ppermute | solution.py:446
  61.4 27.5 %collective-permute-start.5 = (bf16[8,8,8,512]{3,2,1,0:T(8,128)(2,1)S(1)}, bf16[8,8,8,512]{3,2,1,0:T(8,128)(2,1)S(1)}, u32[]{:S(2)}, u32[]{:S(2)}) collective-permute-start(bf16[8,8,8,512]{3,2,1,0:T(8,128)(2,1)S(1)} %bitcast.50), channel_id=1, source_target_pairs={{8,0},{9,1},{10,2},{11,3},{12,4},{13,5},{14,6},{15,7},{24,32},{25,... | collective-permute-start | bytes 1572872 | tf_op jit(solution)/shard_map/ppermute | solution.py:447
  77.6 2.6 %collective-permute-start.6 = (bf16[8,8,512]{2,1,0:T(8,128)(2,1)S(1)}, bf16[8,8,512]{2,1,0:T(8,128)(2,1)S(1)}, u32[]{:S(2)}, u32[]{:S(2)}) collective-permute-start(bf16[8,8,512]{2,1,0:T(8,128)(2,1)S(1)} %slice_select_fusion.1), channel_id=1, source_target_pairs={{8,32},{9,33},{10,34},{11,35},{12,36},{13,37},{14,38},{15,39},{16,... | collective-permute-start | bytes 196616 | tf_op jit(solution)/shard_map/ppermute | solution.py:449
  78.9 26.8 %collective-permute-start.14 = (bf16[4,144,512]{2,1,0:T(8,128)(2,1)S(1)}, bf16[4,144,512]{2,1,0:T(8,128)(2,1)S(1)}, u32[]{:S(2)}, u32[]{:S(2)}) collective-permute-start(bf16[4,144,512]{2,1,0:T(8,128)(2,1)S(1)} %get-tuple-element.18), channel_id=1, source_target_pairs={{0,64},{1,65},{2,66},{3,67},{4,68},{5,69},{6,70},{7,71},{8,72},{9,... | collective-permute-start | bytes 1769480 | tf_op jit(solution)/shard_map/ppermute | solution.py:471
  89.5 33.6 %collective-permute-start.11 = (bf16[4,144,512]{2,1,0:T(8,128)(2,1)S(1)}, bf16[4,144,512]{2,1,0:T(8,128)(2,1)S(1)}, u32[]{:S(2)}, u32[]{:S(2)}) collective-permute-start(bf16[4,144,512]{2,1,0:T(8,128)(2,1)S(1)} %get-tuple-element.17), channel_id=1, source_target_pairs={{0,64},{1,65},{2,66},{3,67},{4,68},{5,69},{6,70},{7,71},{8,72},{9,... | collective-permute-start | bytes 1769480 | tf_op jit(solution)/shard_map/ppermute | solution.py:471
  106.7 25.0 %collective-permute-start.15 = (bf16[2,144,512]{2,1,0:T(8,128)(2,1)}, bf16[2,144,512]{2,1,0:T(8,128)(2,1)S(1)}, u32[]{:S(2)}, u32[]{:S(2)}) collective-permute-start(bf16[2,144,512]{2,1,0:T(8,128)(2,1)} %get-tuple-element.32), channel_id=1, source_target_pairs={{64,65},{65,66},{66,67},{67,68},{68,69},{69,70},{70,71},{71,72},{7... | collective-permute-start | bytes 884744 | tf_op jit(solution)/shard_map/ppermute | solution.py:476
  111.1 20.5 %collective-permute-start.16 = (bf16[2,144,512]{2,1,0:T(8,128)(2,1)}, bf16[2,144,512]{2,1,0:T(8,128)(2,1)S(1)}, u32[]{:S(2)}, u32[]{:S(2)}) collective-permute-start(bf16[2,144,512]{2,1,0:T(8,128)(2,1)} %get-tuple-element.31), channel_id=1, source_target_pairs={{65,64},{66,65},{67,66},{68,67},{69,68},{70,69},{71,70},{72,71},{7... | collective-permute-start | bytes 884744 | tf_op jit(solution)/shard_map/ppermute | solution.py:477
  123.1 20.6 %collective-permute-start.12 = (bf16[2,144,512]{2,1,0:T(8,128)(2,1)S(1)}, bf16[2,144,512]{2,1,0:T(8,128)(2,1)S(1)}, u32[]{:S(2)}, u32[]{:S(2)}) collective-permute-start(bf16[2,144,512]{2,1,0:T(8,128)(2,1)S(1)} %get-tuple-element.34), channel_id=1, source_target_pairs={{64,65},{65,66},{66,67},{67,68},{68,69},{69,70},{70,71},{71,72},{7... | collective-permute-start | bytes 884744 | tf_op jit(solution)/shard_map/ppermute | solution.py:476
  127.1 16.6 %collective-permute-start.13 = (bf16[2,144,512]{2,1,0:T(8,128)(2,1)S(1)}, bf16[2,144,512]{2,1,0:T(8,128)(2,1)S(1)}, u32[]{:S(2)}, u32[]{:S(2)}) collective-permute-start(bf16[2,144,512]{2,1,0:T(8,128)(2,1)S(1)} %get-tuple-element.33), channel_id=1, source_target_pairs={{65,64},{66,65},{67,66},{68,67},{69,68},{70,69},{71,70},{72,71},{7... | collective-permute-start | bytes 884744 | tf_op jit(solution)/shard_map/ppermute | solution.py:477
  155.8 3.1 %collective-permute-start.17 = (bf16[2,4,128,512]{3,2,1,0:T(8,128)(2,1)S(1)}, bf16[2,4,128,512]{3,2,1,0:T(8,128)(2,1)S(1)}, u32[]{:S(2)}, u32[]{:S(2)}) collective-permute-start(bf16[2,4,128,512]{3,2,1,0:T(8,128)(2,1)S(1)} %get-tuple-element.24), channel_id=1, source_target_pairs={{0,32},{32,0},{64,96},{96,64},{1,33},{33,1},{65,97},{97,65},{2,34}... | collective-permute-start | bytes 3145736 | tf_op jit(solution)/shard_map/ppermute | solution.py:480

commit v2 on v1

--- a/solution.py
+++ b/solution.py
@@ -21,15 +21,55 @@
     return pl.BlockSpec(memory_space=pltpu.SMEM)
 
 
+def hbm_spec():
+    return pl.BlockSpec(memory_space=pltpu.HBM)
+
+
 def any_spec():
     return pl.BlockSpec(memory_space=pl.ANY)
 
 
-def stem_kernel(place, feat, up, down, left, right, w1, w2, wd, out, s1, x1, s2, x2, s3, dbuf):
+def pack_kernel(feat, top, bottom, first_cols, last_cols, wide):
+    windows, rows, cols, ch = feat.shape
+    rim_r, rim_c = top.shape[1], first_cols.shape[1]
+    lanes = wide.shape[2]
+    top[...] = feat[:, :rim_r]
+    bottom[...] = feat[:, rows - rim_r :]
+    for k in range(ch // lanes):
+        at = slice(k * lanes, (k + 1) * lanes)
+        wide[k] = feat[:, :, :, at].astype(F32).reshape(windows * rows * cols, lanes)
+        for w in range(windows):
+            for j in range(rim_c):
+                base = w * rows * cols
+                first_cols[w, j, :, at] = wide[k, pl.ds(base + j, rows, stride=cols), :].astype(BF16)
+                last_cols[w, j, :, at] = wide[
+                    k, pl.ds(base + cols - rim_c + j, rows, stride=cols), :
+                ].astype(BF16)
+
+
+def pack(features, rim_r, rim_c):
+    windows, rows, cols, ch = features.shape
+    row_shape = jax.ShapeDtypeStruct((windows, rim_r, cols, ch), BF16)
+    col_shape = jax.ShapeDtypeStruct((windows, rim_c, rows, ch), BF16)
+    return pl.pallas_call(
+        pack_kernel,
+        out_shape=(row_shape, row_shape, col_shape, col_shape),
+        in_specs=[vmem_spec()],
+        out_specs=(vmem_spec(),) * 4,
+        scratch_shapes=[VMEM((ch // 128, windows * rows * cols, 128), F32)],
+        compiler_params=pltpu.CompilerParams(vmem_limit_bytes=24 * 2**20),
+        name="pack",
+    )(features)
+
+
+def stem_kernel(window, place, feat, up, down, left, right, w1_in, w2_in, wd_in, out, *scratch):
+    s1, x1, s2, x2, s3, dbuf, w1, w2, wd, sems = scratch
+    pairs = ((w1_in, w1), (w2_in, w2), (wd_in, wd))
+    copies = [pltpu.make_async_copy(*pair, sems.at[i]) for i, pair in enumerate(pairs)]
+    for copy in copies:
+        copy.start()
     halo = 6
-    rows = feat.shape[0]
-    cols = feat.shape[1]
-    ch = feat.shape[2]
+    _, rows, cols, ch = feat.shape
     full = rows + 2 * halo
     row_base = place[0]
     total_rows = place[1]
@@ -42,12 +82,19 @@
     s1d = s1.reshape(ch // lanes, full, pitch, lanes)
     for k in range(ch // lanes):
         at = slice(k * lanes, (k + 1) * lanes)
-        s1d[k, 0:halo, 8 : 8 + cols, :] = up[:, :, at].astype(F32)
-        s1d[k, halo : halo + rows, 8 : 8 + cols, :] = feat[:, :, at].astype(F32)
-        s1d[k, halo + rows : full, 8 : 8 + cols, :] = down[:, :, at].astype(F32)
-        for j in range(2):
-            s1[k, pl.ds(6 + j, full, stride=pitch), :] = left[j, :, at].astype(F32)
-            s1[k, pl.ds(8 + cols + j, full, stride=pitch), :] = right[j, :, at].astype(F32)
+        s1d[k, 0:halo, 8 : 8 + cols, :] = up[window, :, :, at].astype(F32)
+        s1d[k, halo : halo + rows, 8 : 8 + cols, :] = feat[window, :, :, at].astype(F32)
+        s1d[k, halo + rows : full, 8 : 8 + cols, :] = down[window, :, :, at].astype(F32)
+        for src, to in ((left, 6), (right, 8 + cols)):
+            for j in range(2):
+                for take, put, count in (
+                    (0, halo, rows),
+                    (rows, 0, halo),
+                    (rows + halo, halo + rows, halo),
+                ):
+                    s1[k, pl.ds(put * pitch + to + j, count, stride=pitch), :] = src[
+                        window, j, take : take + count, at
+                    ].astype(F32)
 
     step = 19
 
@@ -61,6 +108,7 @@
         return carry
 
     lax.fori_loop(0, full // step, shift1, 0)
+    copies[0].wait()
 
     out1 = full - 2
     block1 = 37
@@ -97,6 +145,7 @@
         return carry
 
     lax.fori_loop(0, out1 // block1, shift2, 0)
+    copies[1].wait()
 
     out2 = out1 - 2
     block2 = 36
@@ -131,6 +180,7 @@
                     dbuf[i * zcols : (i + 1) * zcols, at : at + lanes] = s3[
                         k, pl.ds((2 * i + a) * cols + c, zcols, stride=2), :
                     ].astype(BF16)
+    copies[2].wait()
     z = jnp.maximum(jnp.dot(dbuf[...], wd[...], preferred_element_type=F32), 0.0)
     z = z.reshape(zrows, zcols, z.shape[-1])
     zrow = row_base // 2 + 1 + lax.broadcasted_iota(jnp.int32, (zrows, zcols, 1), 0)
@@ -142,16 +192,16 @@
         out[b] = z[own * b : own * b + depth]
 
 
-def stem(place, feat, up, down, left, right, w1, w2, wd, slots):
-    rows, cols, ch = feat.shape
+def stem(window, place, feat, up, down, left, right, w1, w2, wd, slots):
+    _, rows, cols, ch = feat.shape
     full = rows + 12
     out_ch = wd.shape[1]
     own = rows // 2 // slots
     flops = 2 * (74 * 24 + 72 * 16) * 9 * ch * ch
     return pl.pallas_call(
-        stem_kernel,
+        functools.partial(stem_kernel, window),
         out_shape=jax.ShapeDtypeStruct((slots, own + 4, cols // 2, out_ch), BF16),
-        in_specs=[smem_spec()] + [vmem_spec()] * 8,
+        in_specs=[smem_spec()] + [vmem_spec()] * 5 + [hbm_spec()] * 3,
         out_specs=vmem_spec(),
         scratch_shapes=[
             VMEM((ch // 128, full * 32, 128), F32),
@@ -160,10 +210,13 @@
             VMEM((full - 2, 16, 3 * ch), BF16),
             VMEM((ch // 128, (full - 4) * 16, 128), F32),
             VMEM(((full - 4) // 2 * 8, 4 * ch), BF16),
+            VMEM(w1.shape, BF16),
+            VMEM(w2.shape, BF16),
+            VMEM(wd.shape, BF16),
+            pltpu.SemaphoreType.DMA((3,)),
         ],
         compiler_params=pltpu.CompilerParams(vmem_limit_bytes=48 * 2**20),
         cost_estimate=pl.CostEstimate(flops=flops, bytes_accessed=4 * 2**20, transcendentals=0),
-        name="stem",
     )(place, feat, up, down, left, right, w1, w2, wd)
 
 
@@ -173,19 +226,20 @@
 def duo_body(place, fill, own_w, peer_w, keep, send, full, scratch, window):
     s1, x1, s2, x2, wa, wb, za, zb, zf, sems = scratch
     core = place[1]
+
+    def load(mine, dst, sem):
+        @pl.when(core == mine)
+        def _():
+            pltpu.make_async_copy(own_w, dst, sem).start()
+
+        @pl.when(core != mine)
+        def _():
+            pltpu.make_async_copy(peer_w, dst, sem).start()
+
+    load(0, wa, sems.at[3])
     row0, row_total, col0, col_total = place[2], place[3], place[4], place[5]
     rows_in, width, wide = x1.shape
     ch = wide // 3
-
-    @pl.when(core == 0)
-    def _():
-        pltpu.make_async_copy(own_w, wa, sems.at[0]).start()
-        pltpu.make_async_copy(peer_w, wb, sems.at[1]).start()
-
-    @pl.when(core == 1)
-    def _():
-        pltpu.make_async_copy(peer_w, wa, sems.at[0]).start()
-        pltpu.make_async_copy(own_w, wb, sems.at[1]).start()
 
     fill(s1)
 
@@ -214,7 +268,8 @@
         return jnp.where(ok, y, 0.0).astype(BF16)
 
     shift(s1, x1)
-    pltpu.make_async_copy(own_w, wa, sems.at[0]).wait()
+    pltpu.make_async_copy(own_w, wa, sems.at[3]).wait()
+    load(1, wb, sems.at[4])
     rows_mid = rows_in - 2
 
     def first(i, carry):
@@ -227,35 +282,43 @@
     shift(s2, x2)
     rows_out = rows_mid - 2
     za[...] = x2[1 : 1 + rows_out, EDGE : width - EDGE, ch : 2 * ch]
-    pltpu.make_async_copy(own_w, wb, sems.at[1]).wait()
+    half = width - 2 * EDGE
+
+    @pl.when(core == 0)
+    def _():
+        pltpu.make_async_copy(za, keep.at[window, :, pl.ds(0, half), :], sems.at[0]).start()
+
+    @pl.when(core == 1)
+    def _():
+        pltpu.make_async_copy(za, send, sems.at[0]).start()
+
+    pltpu.make_async_copy(own_w, wb, sems.at[4]).wait()
 
     def second(i, carry):
         r = 2 * i
-        y = layer(x2, wb, r, row0 + 2)
-        zf[pl.ds(r, 2)] = y
+        zf[pl.ds(r, 2)] = layer(x2, wb, r, row0 + 2)
         return carry
 
     lax.fori_loop(0, rows_out // 2, second, 0)
+
+    if full is not None:
+        pltpu.make_async_copy(zf, full, sems.at[2]).start()
     zb[...] = zf[:, EDGE : width - EDGE, :]
-
-    half = width - 2 * EDGE
 
     @pl.when(core == 0)
     def _():
-        pltpu.make_async_copy(za, keep.at[window, :, pl.ds(0, half), :], sems.at[2]).start()
-        pltpu.make_async_copy(zb, send.at[window], sems.at[3]).start()
+        pltpu.make_async_copy(zb, send, sems.at[1]).start()
+        pltpu.make_async_copy(za, keep.at[window, :, pl.ds(0, half), :], sems.at[0]).wait()
+        pltpu.make_async_copy(zb, send, sems.at[1]).wait()
 
     @pl.when(core == 1)
     def _():
-        pltpu.make_async_copy(zb, keep.at[window, :, pl.ds(half, half), :], sems.at[2]).start()
-        pltpu.make_async_copy(za, send.at[window], sems.at[3]).start()
+        pltpu.make_async_copy(zb, keep.at[window, :, pl.ds(half, half), :], sems.at[1]).start()
+        pltpu.make_async_copy(za, send, sems.at[0]).wait()
+        pltpu.make_async_copy(zb, keep.at[window, :, pl.ds(half, half), :], sems.at[1]).wait()
 
     if full is not None:
-        copy = pltpu.make_async_copy(zf, full, sems.at[4])
-        copy.start()
-        copy.wait()
-    pltpu.make_async_copy(za, keep.at[window, :, pl.ds(0, half), :], sems.at[2]).wait()
-    pltpu.make_async_copy(zb, send.at[window], sems.at[3]).wait()
+        pltpu.make_async_copy(zf, full, sems.at[2]).wait()
 
 
 def clear_edges(s, width):
@@ -266,10 +329,10 @@
 
 def early_kernel(window, chained, *refs):
     place, lo, hi, side, own_w, peer_w = refs[:6]
-    refs = refs[6 + (2 if chained else 0) :]
+    refs = refs[6 + (1 if chained else 0) :]
     keep, send, full = refs[:3]
     scratch = refs[3:]
-    s1, x1, s2 = scratch[0], scratch[1], scratch[2]
+    x1, s2 = scratch[1], scratch[2]
     width = x1.shape[1]
     block = lo.shape[2]
 
@@ -341,24 +404,26 @@
     )
 
 
-def early(window, place, lo, hi, side, own_w, peer_w, buffers, windows, rows, half):
+def early(window, place, lo, hi, side, own_w, peer_w, keep, windows, rows, half):
     ch = lo.shape[-1]
     width = half + 2 * EDGE
-    chained = buffers is not None
+    chained = keep is not None
     return pl.pallas_call(
         functools.partial(early_kernel, window, chained),
         out_shape=(
             jax.ShapeDtypeStruct((windows, rows, 2 * half, ch), BF16),
-            jax.ShapeDtypeStruct((windows, rows, half, ch), BF16),
+            jax.ShapeDtypeStruct((rows, half, ch), BF16),
             jax.ShapeDtypeStruct((rows, width, ch), BF16),
         ),
-        in_specs=[smem_spec()] + [vmem_spec()] * 3 + [any_spec()] * (4 if chained else 2),
+        in_specs=[smem_spec()]
+        + [vmem_spec()] * 3
+        + [hbm_spec()] * 2
+        + [any_spec()] * (1 if chained else 0),
         out_specs=(any_spec(), any_spec(), any_spec()),
         scratch_shapes=duo_scratch(rows, width, ch),
-        input_output_aliases={6: 0, 7: 1} if chained else {},
-        name=f"early{window}",
+        input_output_aliases={6: 0} if chained else {},
         **duo_params(rows, width, ch),
-    )(place, lo, hi, side, own_w, peer_w, *(buffers or ()))
+    )(place, lo, hi, side, own_w, peer_w, *([keep] if chained else []))
 
 
 def late(window, place, above, main, below, own_w, peer_w, buffers):
@@ -366,11 +431,10 @@
     return pl.pallas_call(
         functools.partial(late_kernel, window),
         out_shape=tuple(jax.ShapeDtypeStruct(b.shape, b.dtype) for b in buffers),
-        in_specs=[smem_spec()] + [vmem_spec()] * 3 + [any_spec()] * 4,
+        in_specs=[smem_spec()] + [vmem_spec()] * 3 + [hbm_spec()] * 2 + [any_spec()] * 2,
         out_specs=(any_spec(), any_spec()),
         scratch_shapes=duo_scratch(rows, width, ch),
         input_output_aliases={6: 0, 7: 1},
-        name=f"late{window}",
         **duo_params(rows, width, ch),
     )(place, above, main, below, own_w, peer_w, *buffers)
 
@@ -399,17 +463,20 @@
     rim_r, rim_c = 6, 2
     ahead = [(s, s + 1) for s in range(segments - 1)]
     back = [(b, a) for a, b in ahead]
-    up = lax.ppermute(features[:, tile_rows - rim_r :], "segment", ahead)
-    down = lax.ppermute(features[:, :rim_r], "segment", back)
-
-    def side(sl):
-        piece = jnp.concatenate([up[:, :, sl], features[:, :, sl], down[:, :, sl]], axis=1)
-        return jnp.swapaxes(piece, 1, 2)
+    top, bottom, first_cols, last_cols = pack(features, rim_r, rim_c)
+    up = lax.ppermute(bottom, "segment", ahead)
+    down = lax.ppermute(top, "segment", back)
+
+    def side(cols, sl):
+        ends = [jnp.swapaxes(rim[:, :, sl], 1, 2) for rim in (up, down)]
+        return jnp.concatenate([cols, *ends], axis=2)
 
     along = [(c, c + 1) for c in range(strips - 1)]
     against = [(b, a) for a, b in along]
-    left = lax.ppermute(side(slice(tile_cols - rim_c, tile_cols)), "strip", along)
-    right = lax.ppermute(side(slice(0, rim_c)), "strip", against)
+    left = lax.ppermute(
+        side(last_cols, slice(tile_cols - rim_c, tile_cols)), "strip", along
+    )
+    right = lax.ppermute(side(first_cols, slice(0, rim_c)), "strip", against)
 
     stem_place = jnp.stack(
         [
@@ -419,9 +486,14 @@
             (strip == strips - 1).astype(i32),
         ]
     ).astype(i32)
-    w1 = weight_first.reshape(3, 3 * c1, c1)
-    w2 = weight_second.reshape(3, 3 * c1, c1)
-    wd = weight_down.reshape(4 * c1, c2)
+    w1, w2, wd = (
+        pltpu.with_memory_space_constraint(w, pltpu.HBM)
+        for w in (
+            weight_first.reshape(3, 3 * c1, c1),
+            weight_second.reshape(3, 3 * c1, c1),
+            weight_down.reshape(4 * c1, c2),
+        )
+    )
 
     groups = [[g * group + i for i in range(group)] for g in range(segments)]
     low, high, edge = [], [], []
@@ -438,14 +510,14 @@
 
     tiles = []
     for w in range(windows):
-        z = stem(stem_place, features[w], up[w], down[w], left[w], right[w], w1, w2, wd, group)
+        z = stem(w, stem_place, features, up, down, left, right, w1, w2, wd, group)
         shape = z.shape
         got = lax.all_to_all(
             z.reshape(-1, *shape[2:]), "strip", 0, 0, axis_index_groups=groups, tiled=True
         ).reshape(shape)
         lo = lax.ppermute(got, AXES, low)
         hi = lax.ppermute(got, AXES, high)
-        pick = jnp.where(quarter == 2, got[0], got[group - 1])
+        pick = lax.dynamic_index_in_dim(got, jnp.where(quarter == 2, 0, group - 1), 0, False)
         tiles.append((lo, hi, lax.ppermute(pick, AXES, edge)))
 
     common = [
@@ -458,29 +530,34 @@
     early_place = jnp.stack([(far == 0).astype(i32), *common]).astype(i32)
     late_place = jnp.stack([(far == 1).astype(i32), *common]).astype(i32)
 
-    buffers = None
-    passed = []
-    across = [
-        (device(h, t), device(h + 2, t)) for h in range(2) for t in range(strips)
-    ]
+    keep = None
+    sends, passed = [], []
+    across = [(device(h, t), device(h + 2, t)) for h in range(2) for t in range(strips)]
     for w in range(windows):
         keep, send, full = early(
-            w, early_place, *tiles[w], own_w, peer_w, buffers, windows, strip_rows, half
+            w, early_place, *tiles[w], own_w, peer_w, keep, windows, strip_rows, half
         )
-        buffers = (keep, send)
+        sends.append(send)
         passed.append(lax.ppermute(full, AXES, across))
     later = [(device(s, a), device(s, b)) for s in (2, 3) for a, b in along]
     sooner = [(b, a) for a, b in later]
+    others = []
     for w in range(windows):
         main = passed[w]
         above = lax.ppermute(main[strip_rows - 2 :], AXES, later)
         below = lax.ppermute(main[:2], AXES, sooner)
-        buffers = late(w, late_place, above, main, below, own_w, peer_w, buffers)
-    keep, send = buffers
-    other = lax.ppermute(send, "segment", [(s, s ^ 1) for s in range(segments)])
+        keep, send = late(
+            w, late_place, above, main, below, own_w, peer_w, (keep, sends[w])
+        )
+        others.append(
+            lax.ppermute(send, "segment", [(s, s ^ 1) for s in range(segments)])
+        )
     zero = i32(0)
-    result = lax.dynamic_update_slice(keep, other, (zero, zero, (1 - core) * half, zero))
-    return result[None]
+    for w in range(windows):
+        keep = lax.dynamic_update_slice(
+            keep, others[w][None], (i32(w), zero, (1 - core) * half, zero)
+        )
+    return keep[None]
 
 
 def solution(mesh):

time: 161 us -> 157 us (0.975)
  local copies, waits for them, and re-layouts: 8.74 us -> 4.1 us
  Pallas kernels: 39.7 us -> 41.4 us
    slice x4 -> x0, local copies, waits for them, and re-layouts: 2.37 us -> none  [the longest x1 1.41 us: side(): features[:, :, sl]]
    pallas_call x2 -> x3, Pallas kernels: 14.4 us -> 16 us  [the longest x2 15.7 us: stem(): pl.pallas_call(functools.partial(stem_kernel, window), out_shape=jax.Shap...]
    ppermute x5 -> x6, waiting for transfers between devices: 9.34 us -> 10 us  [the longest x1 6.85 us: shards(): lax.ppermute(side(last_cols, slice(tile_cols - rim_c, tile_cols)), 'strip...]
    ppermute x5 -> x6, starting transfers between devices: 13.6 us -> 12.9 us  [the longest x1 6.48 us: shards(): right = lax.ppermute(side(first_cols, slice(0, rim_c)), 'strip', against)]
  transfers between devices with their start and end apart: 20 -> 21, of which waited for: 6 -> 8; matrix products, arithmetic and copies ran while one was open for 5% -> 1% of each run, Pallas kernels for 17% -> 26%
where the time goes in v2:
time: 157 us; the launch traced here: 156 us
  starting transfers between devices  69.1 us (44%)
  Pallas kernels  41.4 us (26%)
  waiting for transfers between devices  41.3 us (26%)
  local copies, waits for them, and re-layouts  4.1 us (3%)
    ppermute x2, starting transfers between devices, shards(): hi = lax.ppermute(got, AXES, high)  25 us
    pallas_call x2, Pallas kernels, late(): pl.pallas_call(functools.partial(late_kernel, window), out_shape=tuple((j...  24.3 us
    ppermute x2, waiting for transfers between devices, shards(): passed.append(lax.ppermute(full, AXES, across))  22.6 us
    pallas_call x2, Pallas kernels, stem(): pl.pallas_call(functools.partial(stem_kernel, window), out_shape=jax.Shap...  15.7 us
    ppermute x2, starting transfers between devices, shards(): below = lax.ppermute(main[:2], AXES, sooner)  9.31 us
    ppermute x2, waiting for transfers between devices, shards(): hi = lax.ppermute(got, AXES, high)  8.64 us
    all_to_all x2, starting transfers between devices, shards(): lax.all_to_all(z.reshape(-1, *shape[2:]), 'strip', 0, 0, axis_index_group...  8.58 us
    ppermute x2, starting transfers between devices, shards(): above = lax.ppermute(main[strip_rows - 2:], AXES, later)  7.44 us
  transfers between devices with their start and end apart: 21, of which 8 were waited for; matrix products, arithmetic and copies ran while one was open for 1% of the time, Pallas kernels for 26%

profile of v2, /device:TPU:29, one launch (start us, length us, event | category | flops | bytes accessed | tf_op | source)
XLA Modules:
  0.0 156.5 jit_solution(17310846593345870833)
XLA Ops:
  0.7 1.2 copy-done
  2.3 1.3 collective-permute-start
  3.6 3.0 %collective-permute-start.1 = (bf16[2,6,16,256]{3,1,2,0:T(8,128)(2,1)S(1)}, bf16[2,6,16,256]{3,1,2,0:T(8,128)(2,1)S(1)}, u32[]{:S(2)}, u32[]{:S(2)}) collective-permute-start(bf16[2,6,16,256]{3,1,2,0:T(8,128)(2,1)S(1)} %copy.12), channel_id=1, source_target_pairs={{32,0},{64,32},{96,64},{33,1},{65,33},{97,65},{34,2},{66,34},{98,6... | collective-permute-start | bytes 294920 | tf_op jit(solution)/shard_map/ppermute | solution.py:468
  6.6 1.8 %collective-permute-done = bf16[2,6,16,256]{3,1,2,0:T(8,128)(2,1)S(1)} collective-permute-done((bf16[2,6,16,256]{3,1,2,0:T(8,128)(2,1)S(1)}, bf16[2,6,16,256]{3,1,2,0:T(8,128)(2,1)S(1)}, u32[]{:S(2)}, u32[]{:S(2)}) %collective-permute-start) | collective-permute-done | bytes 98336 | tf_op jit(solution)/shard_map/ppermute | solution.py:467
  8.6 6.5 %collective-permute-start.3 = (bf16[2,2,76,256]{3,2,1,0:T(8,128)(2,1)S(1)}, bf16[2,2,76,256]{3,2,1,0:T(8,128)(2,1)S(1)}, u32[]{:S(2)}, u32[]{:S(2)}) collective-permute-start(bf16[2,2,76,256]{3,2,1,0:T(8,128)(2,1)S(1)} %pad_maximum_fusion.1), channel_id=1, source_target_pairs={{1,0},{2,1},{3,2},{4,3},{5,4},{6,5},{7,6},{8,7},{9,8},{10,9},{11,1... | collective-permute-start | bytes 466952 | tf_op jit(solution)/shard_map/ppermute | solution.py:479
  15.1 1.9 %collective-permute-start.2 = (bf16[2,2,76,256]{3,2,1,0:T(8,128)(2,1)S(1)}, bf16[2,2,76,256]{3,2,1,0:T(8,128)(2,1)S(1)}, u32[]{:S(2)}, u32[]{:S(2)}) collective-permute-start(bf16[2,2,76,256]{3,2,1,0:T(8,128)(2,1)S(1)} %pad_maximum_fusion), channel_id=1, source_target_pairs={{0,1},{1,2},{2,3},{3,4},{4,5},{5,6},{6,7},{7,8},{8,9},{9,10},{10,1... | collective-permute-start | bytes 466952 | tf_op jit(solution)/shard_map/ppermute | solution.py:476
  17.4 6.9 %collective-permute-done.2.left = bf16[2,2,76,256]{3,2,1,0:T(8,128)(2,1)S(1)} collective-permute-done((bf16[2,2,76,256]{3,2,1,0:T(8,128)(2,1)S(1)}, bf16[2,2,76,256]{3,2,1,0:T(8,128)(2,1)S(1)}, u32[]{:S(2)}, u32[]{:S(2)}) %collective-permute-start.2) | collective-permute-done | bytes 155680 | tf_op jit(solution)/shard_map/ppermute | solution.py:476
  24.2 7.8 %shard_map.56 = bf16[8,8,8,512]{3,2,1,0:T(8,128)(2,1)} custom-call(s32[4]{0:T(128)S(1)} %pad_add_fusion.place, bf16[2,64,16,256]{3,2,1,0:T(8,128)(2,1)S(1)} %copy-done.1, bf16[2,6,16,256]{3,2,1,0:T(8,128)(2,1)S(1)} %copy.13.up, bf16[2,6,16,256]{3,2,1,0:T(8,128)(2,1)S(1)} %copy.14.down, bf16[2,2,76,256]{3,2,1,0:T(8,128)(2,1)S(1)} %collective-permute-done.2.left, ...), custom_call_target="tpu_custom_call" | custom-call | flops 3454009344 | bytes 4194304 | tf_op jit(solution)/shard_map/pallas_call | solution.py:201
  32.1 3.5 %all-to-all-start.1 = ((bf16[64,8,512]{2,1,0:T(8,128)(2,1)}), bf16[64,8,512]{2,1,0:T(8,128)(2,1)S(1)}, u32[]{:S(2)}, u32[]{:S(2)}) async-start(bf16[64,8,512]{2,1,0:T(8,128)(2,1)} %bitcast.19), calls=%async_computation.1 | async-start | bytes 1048576 | tf_op jit(solution)/shard_map/all_to_all | solution.py:515
  35.6 7.8 %shard_map.55 = bf16[8,8,8,512]{3,2,1,0:T(8,128)(2,1)} custom-call(s32[4]{0:T(128)S(1)} %pad_add_fusion.place, bf16[2,64,16,256]{3,2,1,0:T(8,128)(2,1)S(1)} %copy-done.1, bf16[2,6,16,256]{3,2,1,0:T(8,128)(2,1)S(1)} %copy.13.up, bf16[2,6,16,256]{3,2,1,0:T(8,128)(2,1)S(1)} %copy.14.down, bf16[2,2,76,256]{3,2,1,0:T(8,128)(2,1)S(1)} %collective-permute-done.2.left, ...), custom_call_target="tpu_custom_call" | custom-call | flops 3454009344 | bytes 4194304 | tf_op jit(solution)/shard_map/pallas_call | solution.py:201
  43.4 5.1 %all-to-all-start = ((bf16[64,8,512]{2,1,0:T(8,128)(2,1)}), bf16[64,8,512]{2,1,0:T(8,128)(2,1)S(1)}, u32[]{:S(2)}, u32[]{:S(2)}) async-start(bf16[64,8,512]{2,1,0:T(8,128)(2,1)} %bitcast.15), calls=%async_computation | async-start | bytes 1048576 | tf_op jit(solution)/shard_map/all_to_all | solution.py:515
  49.2 8.2 %collective-permute-start.9 = (bf16[8,8,8,512]{3,2,1,0:T(8,128)(2,1)S(1)}, bf16[8,8,8,512]{3,2,1,0:T(8,128)(2,1)S(1)}, u32[]{:S(2)}, u32[]{:S(2)}) collective-permute-start(bf16[8,8,8,512]{3,2,1,0:T(8,128)(2,1)S(1)} %bitcast.37), channel_id=1, source_target_pairs={{8,0},{9,1},{10,2},{11,3},{12,4},{13,5},{14,6},{15,7},{24,32},{25,... | collective-permute-start | bytes 1572872 | tf_op jit(solution)/shard_map/ppermute | solution.py:519
  58.9 16.8 %collective-permute-start.5 = (bf16[8,8,8,512]{3,2,1,0:T(8,128)(2,1)S(1)}, bf16[8,8,8,512]{3,2,1,0:T(8,128)(2,1)S(1)}, u32[]{:S(2)}, u32[]{:S(2)}) collective-permute-start(bf16[8,8,8,512]{3,2,1,0:T(8,128)(2,1)S(1)} %bitcast.35), channel_id=1, source_target_pairs={{8,0},{9,1},{10,2},{11,3},{12,4},{13,5},{14,6},{15,7},{24,32},{25,... | collective-permute-start | bytes 1572872 | tf_op jit(solution)/shard_map/ppermute | solution.py:519
  77.0 1.3 collective-permute-start.14
  78.4 8.6 %collective-permute-done.5.refs_2_ = bf16[8,8,8,512]{3,2,1,0:T(8,128)(2,1)S(1)} collective-permute-done((bf16[8,8,8,512]{3,2,1,0:T(8,128)(2,1)S(1)}, bf16[8,8,8,512]{3,2,1,0:T(8,128)(2,1)S(1)}, u32[]{:S(2)}, u32[]{:S(2)}) %collective-permute-start.5) | collective-permute-done | bytes 524320 | tf_op jit(solution)/shard_map/ppermute | solution.py:519
  87.6 1.3 collective-permute-start.11
  88.9 15.2 %collective-permute-done.14.refs_2_ = bf16[4,144,512]{2,1,0:T(8,128)(2,1)S(1)} collective-permute-done((bf16[4,144,512]{2,1,0:T(8,128)(2,1)S(1)}, bf16[4,144,512]{2,1,0:T(8,128)(2,1)S(1)}, u32[]{:S(2)}, u32[]{:S(2)}) %collective-permute-start.14) | collective-permute-done | bytes 589856 | tf_op jit(solution)/shard_map/ppermute | solution.py:541
  104.9 3.9 %collective-permute-start.15 = (bf16[2,144,512]{2,1,0:T(8,128)(2,1)}, bf16[2,144,512]{2,1,0:T(8,128)(2,1)S(1)}, u32[]{:S(2)}, u32[]{:S(2)}) collective-permute-start(bf16[2,144,512]{2,1,0:T(8,128)(2,1)} %get-tuple-element.34), channel_id=1, source_target_pairs={{64,65},{65,66},{66,67},{67,68},{68,69},{69,70},{70,71},{71,72},{7... | collective-permute-start | bytes 884744 | tf_op jit(solution)/shard_map/ppermute | solution.py:547
  108.8 4.4 %collective-permute-start.16 = (bf16[2,144,512]{2,1,0:T(8,128)(2,1)}, bf16[2,144,512]{2,1,0:T(8,128)(2,1)S(1)}, u32[]{:S(2)}, u32[]{:S(2)}) collective-permute-start(bf16[2,144,512]{2,1,0:T(8,128)(2,1)} %get-tuple-element.33), channel_id=1, source_target_pairs={{65,64},{66,65},{67,66},{68,67},{69,68},{70,69},{71,70},{72,71},{7... | collective-permute-start | bytes 884744 | tf_op jit(solution)/shard_map/ppermute | solution.py:548
  113.3 7.4 %collective-permute-done.11.refs_2_ = bf16[4,144,512]{2,1,0:T(8,128)(2,1)S(1)} collective-permute-done((bf16[4,144,512]{2,1,0:T(8,128)(2,1)S(1)}, bf16[4,144,512]{2,1,0:T(8,128)(2,1)S(1)}, u32[]{:S(2)}, u32[]{:S(2)}) %collective-permute-start.11) | collective-permute-done | bytes 589856 | tf_op jit(solution)/shard_map/ppermute | solution.py:541
  120.8 3.6 %collective-permute-start.12 = (bf16[2,144,512]{2,1,0:T(8,128)(2,1)S(1)}, bf16[2,144,512]{2,1,0:T(8,128)(2,1)S(1)}, u32[]{:S(2)}, u32[]{:S(2)}) collective-permute-start(bf16[2,144,512]{2,1,0:T(8,128)(2,1)S(1)} %get-tuple-element.36), channel_id=1, source_target_pairs={{64,65},{65,66},{66,67},{67,68},{68,69},{69,70},{70,71},{71,72},{7... | collective-permute-start | bytes 884744 | tf_op jit(solution)/shard_map/ppermute | solution.py:547
  124.3 4.9 %collective-permute-start.13 = (bf16[2,144,512]{2,1,0:T(8,128)(2,1)S(1)}, bf16[2,144,512]{2,1,0:T(8,128)(2,1)S(1)}, u32[]{:S(2)}, u32[]{:S(2)}) collective-permute-start(bf16[2,144,512]{2,1,0:T(8,128)(2,1)S(1)} %get-tuple-element.35), channel_id=1, source_target_pairs={{65,64},{66,65},{67,66},{68,67},{69,68},{70,69},{71,70},{72,71},{7... | collective-permute-start | bytes 884744 | tf_op jit(solution)/shard_map/ppermute | solution.py:548
  129.3 12.1 %shard_map.59 = (bf16[2,4,256,512]{3,2,1,0:T(8,128)(2,1)}, bf16[4,128,512]{2,1,0:T(8,128)(2,1)S(1)}) custom-call(s32[6]{0:T(128)S(1)} %stack.53.refs_0_, bf16[2,144,512]{2,1,0:T(8,128)(2,1)S(1)} %collective-permute-done.15.refs_1_, bf16[4,144,512]{2,1,0:T(8,128)(2,1)S(1)} %collective-permute-done.14.refs_2_, ...), custom_call_target="tpu_custom_call", output_to_operand_aliasing={{0}: (6, {}), {1}: (7, {})} | custom-call | flops 6794772480 | bytes 12582912 | tf_op jit(solution)/shard_map/pallas_call | solution.py:431
  141.5 12.1 %shard_map.60 = (bf16[2,4,256,512]{3,2,1,0:T(8,128)(2,1)}, bf16[4,128,512]{2,1,0:T(8,128)(2,1)S(1)}) custom-call(s32[6]{0:T(128)S(1)} %stack.53.refs_0_, bf16[2,144,512]{2,1,0:T(8,128)(2,1)S(1)} %collective-permute-done.12.refs_1_, bf16[4,144,512]{2,1,0:T(8,128)(2,1)S(1)} %collective-permute-done.11.refs_2_, ...), custom_call_target="tpu_custom_call", output_to_operand_aliasing={{0}: (6, {}), {1}: (7, {})} | custom-call | flops 6794772480 | bytes 12582912 | tf_op jit(solution)/shard_map/pallas_call | solution.py:431
  (46 shorter events, 9.4 us)
Async XLA Ops:
  0.0 76.4 %collective-permute-start.7 = (bf16[3,1536,512]{2,1,0:T(8,128)(2,1)}, bf16[3,1536,512]{2,1,0:T(8,128)(2,1)}, u32[]{:S(2)}, u32[]{:S(2)}) collective-permute-start(bf16[3,1536,512]{2,1,0:T(8,128)(2,1)} %bitcast.39), channel_id=1, source_target_pairs={{0,32},{32,0},{64,96},{96,64},{1,33},{33,1},{65,97},{97,65},{2,34}... | collective-permute-start | bytes 14155784 | tf_op jit(solution)/shard_map/ppermute | solution.py:461
  0.7 1.2 copy-start
  1.9 22.3 %copy-start.1 = (bf16[2,64,16,256]{3,2,1,0:T(8,128)(2,1)S(1)}, bf16[2,64,16,256]{3,2,1,0:T(8,128)(2,1)}, u32[]{:S(2)}) copy-start(bf16[2,64,16,256]{3,2,1,0:T(8,128)(2,1)} %feat.5) | copy-start | bytes 3145732
  2.3 6.2 %collective-permute-start = (bf16[2,6,16,256]{3,1,2,0:T(8,128)(2,1)S(1)}, bf16[2,6,16,256]{3,1,2,0:T(8,128)(2,1)S(1)}, u32[]{:S(2)}, u32[]{:S(2)}) collective-permute-start(bf16[2,6,16,256]{3,1,2,0:T(8,128)(2,1)S(1)} %copy.11), channel_id=1, source_target_pairs={{0,32},{32,64},{64,96},{1,33},{33,65},{65,97},{2,34},{34,66},{66,9... | collective-permute-start | bytes 294920 | tf_op jit(solution)/shard_map/ppermute | solution.py:467
  3.6 5.0 %collective-permute-start.1 = (bf16[2,6,16,256]{3,1,2,0:T(8,128)(2,1)S(1)}, bf16[2,6,16,256]{3,1,2,0:T(8,128)(2,1)S(1)}, u32[]{:S(2)}, u32[]{:S(2)}) collective-permute-start(bf16[2,6,16,256]{3,1,2,0:T(8,128)(2,1)S(1)} %copy.12), channel_id=1, source_target_pairs={{32,0},{64,32},{96,64},{33,1},{65,33},{97,65},{34,2},{66,34},{98,6... | collective-permute-start | bytes 294920 | tf_op jit(solution)/shard_map/ppermute | solution.py:468
  8.6 8.7 %collective-permute-start.3 = (bf16[2,2,76,256]{3,2,1,0:T(8,128)(2,1)S(1)}, bf16[2,2,76,256]{3,2,1,0:T(8,128)(2,1)S(1)}, u32[]{:S(2)}, u32[]{:S(2)}) collective-permute-start(bf16[2,2,76,256]{3,2,1,0:T(8,128)(2,1)S(1)} %pad_maximum_fusion.1), channel_id=1, source_target_pairs={{1,0},{2,1},{3,2},{4,3},{5,4},{6,5},{7,6},{8,7},{9,8},{10,9},{11,1... | collective-permute-start | bytes 466952 | tf_op jit(solution)/shard_map/ppermute | solution.py:479
  15.1 9.1 %collective-permute-start.2 = (bf16[2,2,76,256]{3,2,1,0:T(8,128)(2,1)S(1)}, bf16[2,2,76,256]{3,2,1,0:T(8,128)(2,1)S(1)}, u32[]{:S(2)}, u32[]{:S(2)}) collective-permute-start(bf16[2,2,76,256]{3,2,1,0:T(8,128)(2,1)S(1)} %pad_maximum_fusion), channel_id=1, source_target_pairs={{0,1},{1,2},{2,3},{3,4},{4,5},{5,6},{6,7},{7,8},{8,9},{9,10},{10,1... | collective-permute-start | bytes 466952 | tf_op jit(solution)/shard_map/ppermute | solution.py:476
  32.1 11.4 %all-to-all-start.1 = ((bf16[64,8,512]{2,1,0:T(8,128)(2,1)}), bf16[64,8,512]{2,1,0:T(8,128)(2,1)S(1)}, u32[]{:S(2)}, u32[]{:S(2)}) async-start(bf16[64,8,512]{2,1,0:T(8,128)(2,1)} %bitcast.19), calls=%async_computation.1 | async-start | bytes 1048576 | tf_op jit(solution)/shard_map/all_to_all | solution.py:515
  43.4 14.8 %all-to-all-start = ((bf16[64,8,512]{2,1,0:T(8,128)(2,1)}), bf16[64,8,512]{2,1,0:T(8,128)(2,1)S(1)}, u32[]{:S(2)}, u32[]{:S(2)}) async-start(bf16[64,8,512]{2,1,0:T(8,128)(2,1)} %bitcast.15), calls=%async_computation | async-start | bytes 1048576 | tf_op jit(solution)/shard_map/all_to_all | solution.py:515
  48.5 27.2 %collective-permute-start.8 = (bf16[8,8,8,512]{3,2,1,0:T(8,128)(2,1)S(1)}, bf16[8,8,8,512]{3,2,1,0:T(8,128)(2,1)S(1)}, u32[]{:S(2)}, u32[]{:S(2)}) collective-permute-start(bf16[8,8,8,512]{3,2,1,0:T(8,128)(2,1)S(1)} %bitcast.36), channel_id=1, source_target_pairs={{0,0},{1,1},{2,2},{3,3},{4,4},{5,5},{6,6},{7,7},{16,32},{17,33},{1... | collective-permute-start | bytes 1572872 | tf_op jit(solution)/shard_map/ppermute | solution.py:518
  49.2 27.2 %collective-permute-start.9 = (bf16[8,8,8,512]{3,2,1,0:T(8,128)(2,1)S(1)}, bf16[8,8,8,512]{3,2,1,0:T(8,128)(2,1)S(1)}, u32[]{:S(2)}, u32[]{:S(2)}) collective-permute-start(bf16[8,8,8,512]{3,2,1,0:T(8,128)(2,1)S(1)} %bitcast.37), channel_id=1, source_target_pairs={{8,0},{9,1},{10,2},{11,3},{12,4},{13,5},{14,6},{15,7},{24,32},{25,... | collective-permute-start | bytes 1572872 | tf_op jit(solution)/shard_map/ppermute | solution.py:519
  57.5 1.4 collective-permute-start.10
  58.2 20.1 %collective-permute-start.4 = (bf16[8,8,8,512]{3,2,1,0:T(8,128)(2,1)S(1)}, bf16[8,8,8,512]{3,2,1,0:T(8,128)(2,1)S(1)}, u32[]{:S(2)}, u32[]{:S(2)}) collective-permute-start(bf16[8,8,8,512]{3,2,1,0:T(8,128)(2,1)S(1)} %bitcast.33), channel_id=1, source_target_pairs={{0,0},{1,1},{2,2},{3,3},{4,4},{5,5},{6,6},{7,7},{16,32},{17,33},{1... | collective-permute-start | bytes 1572872 | tf_op jit(solution)/shard_map/ppermute | solution.py:518
  58.9 28.0 %collective-permute-start.5 = (bf16[8,8,8,512]{3,2,1,0:T(8,128)(2,1)S(1)}, bf16[8,8,8,512]{3,2,1,0:T(8,128)(2,1)S(1)}, u32[]{:S(2)}, u32[]{:S(2)}) collective-permute-start(bf16[8,8,8,512]{3,2,1,0:T(8,128)(2,1)S(1)} %bitcast.35), channel_id=1, source_target_pairs={{8,0},{9,1},{10,2},{11,3},{12,4},{13,5},{14,6},{15,7},{24,32},{25,... | collective-permute-start | bytes 1572872 | tf_op jit(solution)/shard_map/ppermute | solution.py:519
  75.7 2.6 %collective-permute-start.6 = (bf16[8,8,512]{2,1,0:T(8,128)(2,1)S(1)}, bf16[8,8,512]{2,1,0:T(8,128)(2,1)S(1)}, u32[]{:S(2)}, u32[]{:S(2)}) collective-permute-start(bf16[8,8,512]{2,1,0:T(8,128)(2,1)S(1)} %dynamic-slice_bitcast_fusion.1), channel_id=1, source_target_pairs={{8,32},{9,33},{10,34},{11,35},{12,36},{13,37},{14,38},{15,39},{16,... | collective-permute-start | bytes 196616 | tf_op jit(solution)/shard_map/ppermute | solution.py:521
  77.0 27.0 %collective-permute-start.14 = (bf16[4,144,512]{2,1,0:T(8,128)(2,1)S(1)}, bf16[4,144,512]{2,1,0:T(8,128)(2,1)S(1)}, u32[]{:S(2)}, u32[]{:S(2)}) collective-permute-start(bf16[4,144,512]{2,1,0:T(8,128)(2,1)S(1)} %get-tuple-element.25), channel_id=1, source_target_pairs={{0,64},{1,65},{2,66},{3,67},{4,68},{5,69},{6,70},{7,71},{8,72},{9,... | collective-permute-start | bytes 1769480 | tf_op jit(solution)/shard_map/ppermute | solution.py:541
  87.6 33.1 %collective-permute-start.11 = (bf16[4,144,512]{2,1,0:T(8,128)(2,1)S(1)}, bf16[4,144,512]{2,1,0:T(8,128)(2,1)S(1)}, u32[]{:S(2)}, u32[]{:S(2)}) collective-permute-start(bf16[4,144,512]{2,1,0:T(8,128)(2,1)S(1)} %get-tuple-element.24), channel_id=1, source_target_pairs={{0,64},{1,65},{2,66},{3,67},{4,68},{5,69},{6,70},{7,71},{8,72},{9,... | collective-permute-start | bytes 1769480 | tf_op jit(solution)/shard_map/ppermute | solution.py:541
  104.9 24.3 %collective-permute-start.15 = (bf16[2,144,512]{2,1,0:T(8,128)(2,1)}, bf16[2,144,512]{2,1,0:T(8,128)(2,1)S(1)}, u32[]{:S(2)}, u32[]{:S(2)}) collective-permute-start(bf16[2,144,512]{2,1,0:T(8,128)(2,1)} %get-tuple-element.34), channel_id=1, source_target_pairs={{64,65},{65,66},{66,67},{67,68},{68,69},{69,70},{70,71},{71,72},{7... | collective-permute-start | bytes 884744 | tf_op jit(solution)/shard_map/ppermute | solution.py:547
  108.8 20.5 %collective-permute-start.16 = (bf16[2,144,512]{2,1,0:T(8,128)(2,1)}, bf16[2,144,512]{2,1,0:T(8,128)(2,1)S(1)}, u32[]{:S(2)}, u32[]{:S(2)}) collective-permute-start(bf16[2,144,512]{2,1,0:T(8,128)(2,1)} %get-tuple-element.33), channel_id=1, source_target_pairs={{65,64},{66,65},{67,66},{68,67},{69,68},{70,69},{71,70},{72,71},{7... | collective-permute-start | bytes 884744 | tf_op jit(solution)/shard_map/ppermute | solution.py:548
  120.8 20.7 %collective-permute-start.12 = (bf16[2,144,512]{2,1,0:T(8,128)(2,1)S(1)}, bf16[2,144,512]{2,1,0:T(8,128)(2,1)S(1)}, u32[]{:S(2)}, u32[]{:S(2)}) collective-permute-start(bf16[2,144,512]{2,1,0:T(8,128)(2,1)S(1)} %get-tuple-element.36), channel_id=1, source_target_pairs={{64,65},{65,66},{66,67},{67,68},{68,69},{69,70},{70,71},{71,72},{7... | collective-permute-start | bytes 884744 | tf_op jit(solution)/shard_map/ppermute | solution.py:547
  124.3 17.2 %collective-permute-start.13 = (bf16[2,144,512]{2,1,0:T(8,128)(2,1)S(1)}, bf16[2,144,512]{2,1,0:T(8,128)(2,1)S(1)}, u32[]{:S(2)}, u32[]{:S(2)}) collective-permute-start(bf16[2,144,512]{2,1,0:T(8,128)(2,1)S(1)} %get-tuple-element.35), channel_id=1, source_target_pairs={{65,64},{66,65},{67,66},{68,67},{69,68},{70,69},{71,70},{72,71},{7... | collective-permute-start | bytes 884744 | tf_op jit(solution)/shard_map/ppermute | solution.py:548
  141.4 12.4 %collective-permute-start.17 = (bf16[4,128,512]{2,1,0:T(8,128)(2,1)S(1)}, bf16[4,128,512]{2,1,0:T(8,128)(2,1)S(1)}, u32[]{:S(2)}, u32[]{:S(2)}) collective-permute-start(bf16[4,128,512]{2,1,0:T(8,128)(2,1)S(1)} %get-tuple-element.31), channel_id=1, source_target_pairs={{0,32},{32,0},{64,96},{96,64},{1,33},{33,1},{65,97},{97,65},{2,34}... | collective-permute-start | bytes 1572872 | tf_op jit(solution)/shard_map/ppermute | solution.py:553
  153.7 2.0 %collective-permute-start.18 = (bf16[4,128,512]{2,1,0:T(8,128)(2,1)S(1)}, bf16[4,128,512]{2,1,0:T(8,128)(2,1)S(1)}, u32[]{:S(2)}, u32[]{:S(2)}) collective-permute-start(bf16[4,128,512]{2,1,0:T(8,128)(2,1)S(1)} %get-tuple-element.32), channel_id=1, source_target_pairs={{0,32},{32,0},{64,96},{96,64},{1,33},{33,1},{65,97},{97,65},{2,34}... | collective-permute-start | bytes 1572872 | tf_op jit(solution)/shard_map/ppermute | solution.py:553

commit v3 on v2

--- a/solution.py
+++ b/solution.py
@@ -227,20 +227,24 @@
     s1, x1, s2, x2, wa, wb, za, zb, zf, sems = scratch
     core = place[1]
 
-    def load(mine, dst, sem):
+    def load(mine, dst, taps, sem):
         @pl.when(core == mine)
         def _():
-            pltpu.make_async_copy(own_w, dst, sem).start()
+            pltpu.make_async_copy(own_w.at[taps], dst.at[taps], sem).start()
 
         @pl.when(core != mine)
         def _():
-            pltpu.make_async_copy(peer_w, dst, sem).start()
-
-    load(0, wa, sems.at[3])
+            pltpu.make_async_copy(peer_w.at[taps], dst.at[taps], sem).start()
+
+    def tap_ready(a):
+        pltpu.make_async_copy(own_w.at[pl.ds(a, 1)], wa.at[pl.ds(a, 1)], sems.at[3 + a]).wait()
+
+    for a in range(3):
+        load(0, wa, pl.ds(a, 1), sems.at[3 + a])
+    inner = pl.multiple_of(core * EDGE, EDGE)
     row0, row_total, col0, col_total = place[2], place[3], place[4], place[5]
     rows_in, width, wide = x1.shape
     ch = wide // 3
-
     fill(s1)
 
     def shift(src, dst):
@@ -253,9 +257,11 @@
 
         lax.fori_loop(0, dst.shape[0], go, 0)
 
-    def layer(x, w, r, first_row):
+    def layer(x, w, r, first_row, ready=None):
         acc = None
         for a in range(3):
+            if ready is not None:
+                ready(a)
             part = jnp.dot(
                 x[pl.ds(r + a, 2)].reshape(2 * width, 3 * ch), w[a], preferred_element_type=F32
             )
@@ -268,54 +274,64 @@
         return jnp.where(ok, y, 0.0).astype(BF16)
 
     shift(s1, x1)
-    pltpu.make_async_copy(own_w, wa, sems.at[3]).wait()
-    load(1, wb, sems.at[4])
     rows_mid = rows_in - 2
 
-    def first(i, carry):
+    def first(i, carry, ready=None):
         r = 2 * i
-        y = layer(x1, wa, r, row0 + 1)
+        y = layer(x1, wa, r, row0 + 1, ready)
         s2[pl.ds(r, 2), EDGE : EDGE + width, :] = y.astype(F32)
         return carry
 
-    lax.fori_loop(0, rows_mid // 2, first, 0)
+    first(0, 0, tap_ready)
+    load(1, wb, pl.ds(0, 3), sems.at[6])
+    lax.fori_loop(1, rows_mid // 2, first, 0)
     shift(s2, x2)
     rows_out = rows_mid - 2
-    za[...] = x2[1 : 1 + rows_out, EDGE : width - EDGE, ch : 2 * ch]
-    half = width - 2 * EDGE
+    half = width - EDGE
+    left_half, right_half = pl.ds(0, half), pl.ds(half, half)
+    za[...] = x2[1 : 1 + rows_out, pl.ds(inner, half), ch : 2 * ch]
 
     @pl.when(core == 0)
     def _():
-        pltpu.make_async_copy(za, keep.at[window, :, pl.ds(0, half), :], sems.at[0]).start()
+        pltpu.make_async_copy(za, keep.at[window, :, left_half, :], sems.at[0]).start()
 
     @pl.when(core == 1)
     def _():
         pltpu.make_async_copy(za, send, sems.at[0]).start()
 
-    pltpu.make_async_copy(own_w, wb, sems.at[4]).wait()
+    pltpu.make_async_copy(own_w, wb, sems.at[6]).wait()
 
     def second(i, carry):
         r = 2 * i
-        zf[pl.ds(r, 2)] = layer(x2, wb, r, row0 + 2)
+        two = pl.ds(r, 2)
+        zf[two] = layer(x2, wb, r, row0 + 2)
+        if full is not None:
+            pltpu.make_async_copy(zf.at[two], full.at[two], sems.at[2]).start()
+        zb[two] = zf[two, pl.ds(inner, half), :]
+
+        @pl.when(core == 0)
+        def _():
+            pltpu.make_async_copy(zb.at[two], send.at[two], sems.at[1]).start()
+
+        @pl.when(core == 1)
+        def _():
+            pltpu.make_async_copy(
+                zb.at[two], keep.at[window, two, right_half, :], sems.at[1]
+            ).start()
+
         return carry
 
     lax.fori_loop(0, rows_out // 2, second, 0)
-
-    if full is not None:
-        pltpu.make_async_copy(zf, full, sems.at[2]).start()
-    zb[...] = zf[:, EDGE : width - EDGE, :]
 
     @pl.when(core == 0)
     def _():
-        pltpu.make_async_copy(zb, send, sems.at[1]).start()
-        pltpu.make_async_copy(za, keep.at[window, :, pl.ds(0, half), :], sems.at[0]).wait()
+        pltpu.make_async_copy(za, keep.at[window, :, left_half, :], sems.at[0]).wait()
         pltpu.make_async_copy(zb, send, sems.at[1]).wait()
 
     @pl.when(core == 1)
     def _():
-        pltpu.make_async_copy(zb, keep.at[window, :, pl.ds(half, half), :], sems.at[1]).start()
         pltpu.make_async_copy(za, send, sems.at[0]).wait()
-        pltpu.make_async_copy(zb, keep.at[window, :, pl.ds(half, half), :], sems.at[1]).wait()
+        pltpu.make_async_copy(zb, keep.at[window, :, right_half, :], sems.at[1]).wait()
 
     if full is not None:
         pltpu.make_async_copy(zf, full, sems.at[2]).wait()
@@ -341,16 +357,17 @@
         clear_edges(s2, width)
         parts = lo.shape[0]
 
+        core = place[1]
+        base = EDGE + core * EDGE
+        rim = pl.ds(pl.multiple_of(EDGE + (1 - core) * 2 * parts * block, EDGE), EDGE)
+
         def row(r, carry):
             for e in range(parts):
-                at = 2 * EDGE + block * e
-                s[r, at : at + block, :] = lo[e, r].astype(F32)
-                at = at + block * parts
-                s[r, at : at + block, :] = hi[e, r].astype(F32)
-            on_left = place[1] == 1
-            edge = side[r].astype(F32)
-            s[r, EDGE : 2 * EDGE, :] = jnp.where(on_left, edge, 0.0)
-            s[r, width : width + EDGE, :] = jnp.where(on_left, 0.0, edge)
+                at = pl.multiple_of(base + block * e, EDGE)
+                s[r, pl.ds(at, block), :] = lo[e, r].astype(F32)
+                at = pl.multiple_of(base + block * (e + parts), EDGE)
+                s[r, pl.ds(at, block), :] = hi[e, r].astype(F32)
+            s[r, rim, :] = side[r].astype(F32)
             return carry
 
         lax.fori_loop(0, s.shape[0], row, 0)
@@ -389,10 +406,10 @@
         VMEM((rows + 2, width, 3 * ch), BF16),
         VMEM((3, 3 * ch, ch), BF16),
         VMEM((3, 3 * ch, ch), BF16),
-        VMEM((rows, width - 2 * EDGE, ch), BF16),
-        VMEM((rows, width - 2 * EDGE, ch), BF16),
+        VMEM((rows, width - EDGE, ch), BF16),
+        VMEM((rows, width - EDGE, ch), BF16),
         VMEM((rows, width, ch), BF16),
-        pltpu.SemaphoreType.DMA((5,)),
+        pltpu.SemaphoreType.DMA((7,)),
     ]
 
 
@@ -406,7 +423,7 @@
 
 def early(window, place, lo, hi, side, own_w, peer_w, keep, windows, rows, half):
     ch = lo.shape[-1]
-    width = half + 2 * EDGE
+    width = half + EDGE
     chained = keep is not None
     return pl.pallas_call(
         functools.partial(early_kernel, window, chained),
@@ -524,7 +541,7 @@
         core,
         strip * strip_rows - 2,
         i32(segments * tile_rows // 2),
-        core * half - EDGE,
+        core * (half - EDGE),
         i32(total_cols),
     ]
     early_place = jnp.stack([(far == 0).astype(i32), *common]).astype(i32)

time: 157 us -> 154 us (0.981)
    pallas_call x2, Pallas kernels: 24.3 us -> 22.4 us  [late(): pl.pallas_call(functools.partial(late_kernel, window), out_shape=tuple((j...]
where the time goes in v3:
time: 154 us; the launch traced here: 153 us
  starting transfers between devices  69 us (45%)
  Pallas kernels  39.9 us (26%)
  waiting for transfers between devices  39.8 us (26%)
  local copies, waits for them, and re-layouts  4.1 us (3%)
    ppermute x2, starting transfers between devices, shards(): hi = lax.ppermute(got, AXES, high)  25 us
    pallas_call x2, Pallas kernels, late(): pl.pallas_call(functools.partial(late_kernel, window), out_shape=tuple((j...  22.4 us
    ppermute x2, waiting for transfers between devices, shards(): passed.append(lax.ppermute(full, AXES, across))  21.2 us
    pallas_call x2, Pallas kernels, stem(): pl.pallas_call(functools.partial(stem_kernel, window), out_shape=jax.Shap...  15.7 us
    ppermute x2, starting transfers between devices, shards(): below = lax.ppermute(main[:2], AXES, sooner)  9.23 us
    ppermute x2, waiting for transfers between devices, shards(): hi = lax.ppermute(got, AXES, high)  8.62 us
    all_to_all x2, starting transfers between devices, shards(): lax.all_to_all(z.reshape(-1, *shape[2:]), 'strip', 0, 0, axis_index_group...  8.58 us
    ppermute x2, starting transfers between devices, shards(): above = lax.ppermute(main[strip_rows - 2:], AXES, later)  7.34 us
  transfers between devices with their start and end apart: 21, of which 8 were waited for; matrix products, arithmetic and copies ran while one was open for 1% of the time, Pallas kernels for 26%

profile of v3, /device:TPU:29, one launch (start us, length us, event | category | flops | bytes accessed | tf_op | source)
XLA Modules:
  0.0 153.3 jit_solution(6984136091406099965)
XLA Ops:
  0.7 1.2 copy-done
  2.3 1.3 collective-permute-start
  3.6 3.0 %collective-permute-start.1 = (bf16[2,6,16,256]{3,1,2,0:T(8,128)(2,1)S(1)}, bf16[2,6,16,256]{3,1,2,0:T(8,128)(2,1)S(1)}, u32[]{:S(2)}, u32[]{:S(2)}) collective-permute-start(bf16[2,6,16,256]{3,1,2,0:T(8,128)(2,1)S(1)} %copy.12), channel_id=1, source_target_pairs={{32,0},{64,32},{96,64},{33,1},{65,33},{97,65},{34,2},{66,34},{98,6... | collective-permute-start | bytes 294920 | tf_op jit(solution)/shard_map/ppermute | solution.py:485
  6.6 1.8 %collective-permute-done = bf16[2,6,16,256]{3,1,2,0:T(8,128)(2,1)S(1)} collective-permute-done((bf16[2,6,16,256]{3,1,2,0:T(8,128)(2,1)S(1)}, bf16[2,6,16,256]{3,1,2,0:T(8,128)(2,1)S(1)}, u32[]{:S(2)}, u32[]{:S(2)}) %collective-permute-start) | collective-permute-done | bytes 98336 | tf_op jit(solution)/shard_map/ppermute | solution.py:484
  8.6 6.5 %collective-permute-start.3 = (bf16[2,2,76,256]{3,2,1,0:T(8,128)(2,1)S(1)}, bf16[2,2,76,256]{3,2,1,0:T(8,128)(2,1)S(1)}, u32[]{:S(2)}, u32[]{:S(2)}) collective-permute-start(bf16[2,2,76,256]{3,2,1,0:T(8,128)(2,1)S(1)} %pad_maximum_fusion.1), channel_id=1, source_target_pairs={{1,0},{2,1},{3,2},{4,3},{5,4},{6,5},{7,6},{8,7},{9,8},{10,9},{11,1... | collective-permute-start | bytes 466952 | tf_op jit(solution)/shard_map/ppermute | solution.py:496
  15.1 1.9 %collective-permute-start.2 = (bf16[2,2,76,256]{3,2,1,0:T(8,128)(2,1)S(1)}, bf16[2,2,76,256]{3,2,1,0:T(8,128)(2,1)S(1)}, u32[]{:S(2)}, u32[]{:S(2)}) collective-permute-start(bf16[2,2,76,256]{3,2,1,0:T(8,128)(2,1)S(1)} %pad_maximum_fusion), channel_id=1, source_target_pairs={{0,1},{1,2},{2,3},{3,4},{4,5},{5,6},{6,7},{7,8},{8,9},{9,10},{10,1... | collective-permute-start | bytes 466952 | tf_op jit(solution)/shard_map/ppermute | solution.py:493
  17.4 6.9 %collective-permute-done.2.left = bf16[2,2,76,256]{3,2,1,0:T(8,128)(2,1)S(1)} collective-permute-done((bf16[2,2,76,256]{3,2,1,0:T(8,128)(2,1)S(1)}, bf16[2,2,76,256]{3,2,1,0:T(8,128)(2,1)S(1)}, u32[]{:S(2)}, u32[]{:S(2)}) %collective-permute-start.2) | collective-permute-done | bytes 155680 | tf_op jit(solution)/shard_map/ppermute | solution.py:493
  24.2 7.8 %shard_map.56 = bf16[8,8,8,512]{3,2,1,0:T(8,128)(2,1)} custom-call(s32[4]{0:T(128)S(1)} %pad_add_fusion.place, bf16[2,64,16,256]{3,2,1,0:T(8,128)(2,1)S(1)} %copy-done.1, bf16[2,6,16,256]{3,2,1,0:T(8,128)(2,1)S(1)} %copy.13.up, bf16[2,6,16,256]{3,2,1,0:T(8,128)(2,1)S(1)} %copy.14.down, bf16[2,2,76,256]{3,2,1,0:T(8,128)(2,1)S(1)} %collective-permute-done.2.left, ...), custom_call_target="tpu_custom_call" | custom-call | flops 3454009344 | bytes 4194304 | tf_op jit(solution)/shard_map/pallas_call | solution.py:201
  32.1 3.5 %all-to-all-start.1 = ((bf16[64,8,512]{2,1,0:T(8,128)(2,1)}), bf16[64,8,512]{2,1,0:T(8,128)(2,1)S(1)}, u32[]{:S(2)}, u32[]{:S(2)}) async-start(bf16[64,8,512]{2,1,0:T(8,128)(2,1)} %bitcast.19), calls=%async_computation.1 | async-start | bytes 1048576 | tf_op jit(solution)/shard_map/all_to_all | solution.py:532
  35.6 7.8 %shard_map.55 = bf16[8,8,8,512]{3,2,1,0:T(8,128)(2,1)} custom-call(s32[4]{0:T(128)S(1)} %pad_add_fusion.place, bf16[2,64,16,256]{3,2,1,0:T(8,128)(2,1)S(1)} %copy-done.1, bf16[2,6,16,256]{3,2,1,0:T(8,128)(2,1)S(1)} %copy.13.up, bf16[2,6,16,256]{3,2,1,0:T(8,128)(2,1)S(1)} %copy.14.down, bf16[2,2,76,256]{3,2,1,0:T(8,128)(2,1)S(1)} %collective-permute-done.2.left, ...), custom_call_target="tpu_custom_call" | custom-call | flops 3454009344 | bytes 4194304 | tf_op jit(solution)/shard_map/pallas_call | solution.py:201
  43.4 5.1 %all-to-all-start = ((bf16[64,8,512]{2,1,0:T(8,128)(2,1)}), bf16[64,8,512]{2,1,0:T(8,128)(2,1)S(1)}, u32[]{:S(2)}, u32[]{:S(2)}) async-start(bf16[64,8,512]{2,1,0:T(8,128)(2,1)} %bitcast.15), calls=%async_computation | async-start | bytes 1048576 | tf_op jit(solution)/shard_map/all_to_all | solution.py:532
  49.2 8.2 %collective-permute-start.9 = (bf16[8,8,8,512]{3,2,1,0:T(8,128)(2,1)S(1)}, bf16[8,8,8,512]{3,2,1,0:T(8,128)(2,1)S(1)}, u32[]{:S(2)}, u32[]{:S(2)}) collective-permute-start(bf16[8,8,8,512]{3,2,1,0:T(8,128)(2,1)S(1)} %bitcast.37), channel_id=1, source_target_pairs={{8,0},{9,1},{10,2},{11,3},{12,4},{13,5},{14,6},{15,7},{24,32},{25,... | collective-permute-start | bytes 1572872 | tf_op jit(solution)/shard_map/ppermute | solution.py:536
  58.9 16.8 %collective-permute-start.5 = (bf16[8,8,8,512]{3,2,1,0:T(8,128)(2,1)S(1)}, bf16[8,8,8,512]{3,2,1,0:T(8,128)(2,1)S(1)}, u32[]{:S(2)}, u32[]{:S(2)}) collective-permute-start(bf16[8,8,8,512]{3,2,1,0:T(8,128)(2,1)S(1)} %bitcast.35), channel_id=1, source_target_pairs={{8,0},{9,1},{10,2},{11,3},{12,4},{13,5},{14,6},{15,7},{24,32},{25,... | collective-permute-start | bytes 1572872 | tf_op jit(solution)/shard_map/ppermute | solution.py:536
  77.1 1.3 collective-permute-start.14
  78.4 8.6 %collective-permute-done.5.refs_2_ = bf16[8,8,8,512]{3,2,1,0:T(8,128)(2,1)S(1)} collective-permute-done((bf16[8,8,8,512]{3,2,1,0:T(8,128)(2,1)S(1)}, bf16[8,8,8,512]{3,2,1,0:T(8,128)(2,1)S(1)}, u32[]{:S(2)}, u32[]{:S(2)}) %collective-permute-start.5) | collective-permute-done | bytes 524320 | tf_op jit(solution)/shard_map/ppermute | solution.py:536
  87.8 1.3 collective-permute-start.11
  89.1 13.5 %collective-permute-done.14.refs_2_ = bf16[4,136,512]{2,1,0:T(8,128)(2,1)S(1)} collective-permute-done((bf16[4,136,512]{2,1,0:T(8,128)(2,1)S(1)}, bf16[4,136,512]{2,1,0:T(8,128)(2,1)S(1)}, u32[]{:S(2)}, u32[]{:S(2)}) %collective-permute-start.14) | collective-permute-done | bytes 557088 | tf_op jit(solution)/shard_map/ppermute | solution.py:558
  103.5 3.8 %collective-permute-start.15 = (bf16[2,136,512]{2,1,0:T(8,128)(2,1)}, bf16[2,136,512]{2,1,0:T(8,128)(2,1)S(1)}, u32[]{:S(2)}, u32[]{:S(2)}) collective-permute-start(bf16[2,136,512]{2,1,0:T(8,128)(2,1)} %get-tuple-element.34), channel_id=1, source_target_pairs={{64,65},{65,66},{66,67},{67,68},{68,69},{69,70},{70,71},{71,72},{7... | collective-permute-start | bytes 835592 | tf_op jit(solution)/shard_map/ppermute | solution.py:564
  107.2 4.5 %collective-permute-start.16 = (bf16[2,136,512]{2,1,0:T(8,128)(2,1)}, bf16[2,136,512]{2,1,0:T(8,128)(2,1)S(1)}, u32[]{:S(2)}, u32[]{:S(2)}) collective-permute-start(bf16[2,136,512]{2,1,0:T(8,128)(2,1)} %get-tuple-element.33), channel_id=1, source_target_pairs={{65,64},{66,65},{67,66},{68,67},{69,68},{70,69},{71,70},{72,71},{7... | collective-permute-start | bytes 835592 | tf_op jit(solution)/shard_map/ppermute | solution.py:565
  111.8 7.7 %collective-permute-done.11.refs_2_ = bf16[4,136,512]{2,1,0:T(8,128)(2,1)S(1)} collective-permute-done((bf16[4,136,512]{2,1,0:T(8,128)(2,1)S(1)}, bf16[4,136,512]{2,1,0:T(8,128)(2,1)S(1)}, u32[]{:S(2)}, u32[]{:S(2)}) %collective-permute-start.11) | collective-permute-done | bytes 557088 | tf_op jit(solution)/shard_map/ppermute | solution.py:558
  119.6 3.6 %collective-permute-start.12 = (bf16[2,136,512]{2,1,0:T(8,128)(2,1)S(1)}, bf16[2,136,512]{2,1,0:T(8,128)(2,1)S(1)}, u32[]{:S(2)}, u32[]{:S(2)}) collective-permute-start(bf16[2,136,512]{2,1,0:T(8,128)(2,1)S(1)} %get-tuple-element.36), channel_id=1, source_target_pairs={{64,65},{65,66},{66,67},{67,68},{68,69},{69,70},{70,71},{71,72},{7... | collective-permute-start | bytes 835592 | tf_op jit(solution)/shard_map/ppermute | solution.py:564
  123.2 4.7 %collective-permute-start.13 = (bf16[2,136,512]{2,1,0:T(8,128)(2,1)S(1)}, bf16[2,136,512]{2,1,0:T(8,128)(2,1)S(1)}, u32[]{:S(2)}, u32[]{:S(2)}) collective-permute-start(bf16[2,136,512]{2,1,0:T(8,128)(2,1)S(1)} %get-tuple-element.35), channel_id=1, source_target_pairs={{65,64},{66,65},{67,66},{68,67},{69,68},{70,69},{71,70},{72,71},{7... | collective-permute-start | bytes 835592 | tf_op jit(solution)/shard_map/ppermute | solution.py:565
  127.9 11.2 %shard_map.59 = (bf16[2,4,256,512]{3,2,1,0:T(8,128)(2,1)}, bf16[4,128,512]{2,1,0:T(8,128)(2,1)S(1)}) custom-call(s32[6]{0:T(128)S(1)} %stack.53.refs_0_, bf16[2,136,512]{2,1,0:T(8,128)(2,1)S(1)} %collective-permute-done.15.refs_1_, bf16[4,136,512]{2,1,0:T(8,128)(2,1)S(1)} %collective-permute-done.14.refs_2_, ...), custom_call_target="tpu_custom_call", output_to_operand_aliasing={{0}: (6, {}), {1}: (7, {})} | custom-call | flops 6417285120 | bytes 12582912 | tf_op jit(solution)/shard_map/pallas_call | solution.py:448
  139.3 11.2 %shard_map.60 = (bf16[2,4,256,512]{3,2,1,0:T(8,128)(2,1)}, bf16[4,128,512]{2,1,0:T(8,128)(2,1)S(1)}) custom-call(s32[6]{0:T(128)S(1)} %stack.53.refs_0_, bf16[2,136,512]{2,1,0:T(8,128)(2,1)S(1)} %collective-permute-done.12.refs_1_, bf16[4,136,512]{2,1,0:T(8,128)(2,1)S(1)} %collective-permute-done.11.refs_2_, ...), custom_call_target="tpu_custom_call", output_to_operand_aliasing={{0}: (6, {}), {1}: (7, {})} | custom-call | flops 6417285120 | bytes 12582912 | tf_op jit(solution)/shard_map/pallas_call | solution.py:448
  (46 shorter events, 9.7 us)
Async XLA Ops:
  0.0 76.4 %collective-permute-start.7 = (bf16[3,1536,512]{2,1,0:T(8,128)(2,1)}, bf16[3,1536,512]{2,1,0:T(8,128)(2,1)}, u32[]{:S(2)}, u32[]{:S(2)}) collective-permute-start(bf16[3,1536,512]{2,1,0:T(8,128)(2,1)} %bitcast.39), channel_id=1, source_target_pairs={{0,32},{32,0},{64,96},{96,64},{1,33},{33,1},{65,97},{97,65},{2,34}... | collective-permute-start | bytes 14155784 | tf_op jit(solution)/shard_map/ppermute | solution.py:478
  0.7 1.2 copy-start
  1.9 22.3 %copy-start.1 = (bf16[2,64,16,256]{3,2,1,0:T(8,128)(2,1)S(1)}, bf16[2,64,16,256]{3,2,1,0:T(8,128)(2,1)}, u32[]{:S(2)}) copy-start(bf16[2,64,16,256]{3,2,1,0:T(8,128)(2,1)} %feat.5) | copy-start | bytes 3145732
  2.3 6.2 %collective-permute-start = (bf16[2,6,16,256]{3,1,2,0:T(8,128)(2,1)S(1)}, bf16[2,6,16,256]{3,1,2,0:T(8,128)(2,1)S(1)}, u32[]{:S(2)}, u32[]{:S(2)}) collective-permute-start(bf16[2,6,16,256]{3,1,2,0:T(8,128)(2,1)S(1)} %copy.11), channel_id=1, source_target_pairs={{0,32},{32,64},{64,96},{1,33},{33,65},{65,97},{2,34},{34,66},{66,9... | collective-permute-start | bytes 294920 | tf_op jit(solution)/shard_map/ppermute | solution.py:484
  3.6 5.0 %collective-permute-start.1 = (bf16[2,6,16,256]{3,1,2,0:T(8,128)(2,1)S(1)}, bf16[2,6,16,256]{3,1,2,0:T(8,128)(2,1)S(1)}, u32[]{:S(2)}, u32[]{:S(2)}) collective-permute-start(bf16[2,6,16,256]{3,1,2,0:T(8,128)(2,1)S(1)} %copy.12), channel_id=1, source_target_pairs={{32,0},{64,32},{96,64},{33,1},{65,33},{97,65},{34,2},{66,34},{98,6... | collective-permute-start | bytes 294920 | tf_op jit(solution)/shard_map/ppermute | solution.py:485
  8.6 8.7 %collective-permute-start.3 = (bf16[2,2,76,256]{3,2,1,0:T(8,128)(2,1)S(1)}, bf16[2,2,76,256]{3,2,1,0:T(8,128)(2,1)S(1)}, u32[]{:S(2)}, u32[]{:S(2)}) collective-permute-start(bf16[2,2,76,256]{3,2,1,0:T(8,128)(2,1)S(1)} %pad_maximum_fusion.1), channel_id=1, source_target_pairs={{1,0},{2,1},{3,2},{4,3},{5,4},{6,5},{7,6},{8,7},{9,8},{10,9},{11,1... | collective-permute-start | bytes 466952 | tf_op jit(solution)/shard_map/ppermute | solution.py:496
  15.1 9.1 %collective-permute-start.2 = (bf16[2,2,76,256]{3,2,1,0:T(8,128)(2,1)S(1)}, bf16[2,2,76,256]{3,2,1,0:T(8,128)(2,1)S(1)}, u32[]{:S(2)}, u32[]{:S(2)}) collective-permute-start(bf16[2,2,76,256]{3,2,1,0:T(8,128)(2,1)S(1)} %pad_maximum_fusion), channel_id=1, source_target_pairs={{0,1},{1,2},{2,3},{3,4},{4,5},{5,6},{6,7},{7,8},{8,9},{9,10},{10,1... | collective-permute-start | bytes 466952 | tf_op jit(solution)/shard_map/ppermute | solution.py:493
  32.1 11.4 %all-to-all-start.1 = ((bf16[64,8,512]{2,1,0:T(8,128)(2,1)}), bf16[64,8,512]{2,1,0:T(8,128)(2,1)S(1)}, u32[]{:S(2)}, u32[]{:S(2)}) async-start(bf16[64,8,512]{2,1,0:T(8,128)(2,1)} %bitcast.19), calls=%async_computation.1 | async-start | bytes 1048576 | tf_op jit(solution)/shard_map/all_to_all | solution.py:532
  43.4 14.8 %all-to-all-start = ((bf16[64,8,512]{2,1,0:T(8,128)(2,1)}), bf16[64,8,512]{2,1,0:T(8,128)(2,1)S(1)}, u32[]{:S(2)}, u32[]{:S(2)}) async-start(bf16[64,8,512]{2,1,0:T(8,128)(2,1)} %bitcast.15), calls=%async_computation | async-start | bytes 1048576 | tf_op jit(solution)/shard_map/all_to_all | solution.py:532
  48.5 27.2 %collective-permute-start.8 = (bf16[8,8,8,512]{3,2,1,0:T(8,128)(2,1)S(1)}, bf16[8,8,8,512]{3,2,1,0:T(8,128)(2,1)S(1)}, u32[]{:S(2)}, u32[]{:S(2)}) collective-permute-start(bf16[8,8,8,512]{3,2,1,0:T(8,128)(2,1)S(1)} %bitcast.36), channel_id=1, source_target_pairs={{0,0},{1,1},{2,2},{3,3},{4,4},{5,5},{6,6},{7,7},{16,32},{17,33},{1... | collective-permute-start | bytes 1572872 | tf_op jit(solution)/shard_map/ppermute | solution.py:535
  49.2 27.2 %collective-permute-start.9 = (bf16[8,8,8,512]{3,2,1,0:T(8,128)(2,1)S(1)}, bf16[8,8,8,512]{3,2,1,0:T(8,128)(2,1)S(1)}, u32[]{:S(2)}, u32[]{:S(2)}) collective-permute-start(bf16[8,8,8,512]{3,2,1,0:T(8,128)(2,1)S(1)} %bitcast.37), channel_id=1, source_target_pairs={{8,0},{9,1},{10,2},{11,3},{12,4},{13,5},{14,6},{15,7},{24,32},{25,... | collective-permute-start | bytes 1572872 | tf_op jit(solution)/shard_map/ppermute | solution.py:536
  57.5 1.4 collective-permute-start.10
  58.2 20.2 %collective-permute-start.4 = (bf16[8,8,8,512]{3,2,1,0:T(8,128)(2,1)S(1)}, bf16[8,8,8,512]{3,2,1,0:T(8,128)(2,1)S(1)}, u32[]{:S(2)}, u32[]{:S(2)}) collective-permute-start(bf16[8,8,8,512]{3,2,1,0:T(8,128)(2,1)S(1)} %bitcast.33), channel_id=1, source_target_pairs={{0,0},{1,1},{2,2},{3,3},{4,4},{5,5},{6,6},{7,7},{16,32},{17,33},{1... | collective-permute-start | bytes 1572872 | tf_op jit(solution)/shard_map/ppermute | solution.py:535
  58.9 28.0 %collective-permute-start.5 = (bf16[8,8,8,512]{3,2,1,0:T(8,128)(2,1)S(1)}, bf16[8,8,8,512]{3,2,1,0:T(8,128)(2,1)S(1)}, u32[]{:S(2)}, u32[]{:S(2)}) collective-permute-start(bf16[8,8,8,512]{3,2,1,0:T(8,128)(2,1)S(1)} %bitcast.35), channel_id=1, source_target_pairs={{8,0},{9,1},{10,2},{11,3},{12,4},{13,5},{14,6},{15,7},{24,32},{25,... | collective-permute-start | bytes 1572872 | tf_op jit(solution)/shard_map/ppermute | solution.py:536
  75.7 2.6 %collective-permute-start.6 = (bf16[8,8,512]{2,1,0:T(8,128)(2,1)S(1)}, bf16[8,8,512]{2,1,0:T(8,128)(2,1)S(1)}, u32[]{:S(2)}, u32[]{:S(2)}) collective-permute-start(bf16[8,8,512]{2,1,0:T(8,128)(2,1)S(1)} %dynamic-slice_bitcast_fusion.1), channel_id=1, source_target_pairs={{8,32},{9,33},{10,34},{11,35},{12,36},{13,37},{14,38},{15,39},{16,... | collective-permute-start | bytes 196616 | tf_op jit(solution)/shard_map/ppermute | solution.py:538
  77.1 25.5 %collective-permute-start.14 = (bf16[4,136,512]{2,1,0:T(8,128)(2,1)S(1)}, bf16[4,136,512]{2,1,0:T(8,128)(2,1)S(1)}, u32[]{:S(2)}, u32[]{:S(2)}) collective-permute-start(bf16[4,136,512]{2,1,0:T(8,128)(2,1)S(1)} %get-tuple-element.25), channel_id=1, source_target_pairs={{0,64},{1,65},{2,66},{3,67},{4,68},{5,69},{6,70},{7,71},{8,72},{9,... | collective-permute-start | bytes 1671176 | tf_op jit(solution)/shard_map/ppermute | solution.py:558
  87.8 31.7 %collective-permute-start.11 = (bf16[4,136,512]{2,1,0:T(8,128)(2,1)S(1)}, bf16[4,136,512]{2,1,0:T(8,128)(2,1)S(1)}, u32[]{:S(2)}, u32[]{:S(2)}) collective-permute-start(bf16[4,136,512]{2,1,0:T(8,128)(2,1)S(1)} %get-tuple-element.24), channel_id=1, source_target_pairs={{0,64},{1,65},{2,66},{3,67},{4,68},{5,69},{6,70},{7,71},{8,72},{9,... | collective-permute-start | bytes 1671176 | tf_op jit(solution)/shard_map/ppermute | solution.py:558
  103.5 24.5 %collective-permute-start.15 = (bf16[2,136,512]{2,1,0:T(8,128)(2,1)}, bf16[2,136,512]{2,1,0:T(8,128)(2,1)S(1)}, u32[]{:S(2)}, u32[]{:S(2)}) collective-permute-start(bf16[2,136,512]{2,1,0:T(8,128)(2,1)} %get-tuple-element.34), channel_id=1, source_target_pairs={{64,65},{65,66},{66,67},{67,68},{68,69},{69,70},{70,71},{71,72},{7... | collective-permute-start | bytes 835592 | tf_op jit(solution)/shard_map/ppermute | solution.py:564
  107.2 20.7 %collective-permute-start.16 = (bf16[2,136,512]{2,1,0:T(8,128)(2,1)}, bf16[2,136,512]{2,1,0:T(8,128)(2,1)S(1)}, u32[]{:S(2)}, u32[]{:S(2)}) collective-permute-start(bf16[2,136,512]{2,1,0:T(8,128)(2,1)} %get-tuple-element.33), channel_id=1, source_target_pairs={{65,64},{66,65},{67,66},{68,67},{69,68},{70,69},{71,70},{72,71},{7... | collective-permute-start | bytes 835592 | tf_op jit(solution)/shard_map/ppermute | solution.py:565
  119.6 19.6 %collective-permute-start.12 = (bf16[2,136,512]{2,1,0:T(8,128)(2,1)S(1)}, bf16[2,136,512]{2,1,0:T(8,128)(2,1)S(1)}, u32[]{:S(2)}, u32[]{:S(2)}) collective-permute-start(bf16[2,136,512]{2,1,0:T(8,128)(2,1)S(1)} %get-tuple-element.36), channel_id=1, source_target_pairs={{64,65},{65,66},{66,67},{67,68},{68,69},{69,70},{70,71},{71,72},{7... | collective-permute-start | bytes 835592 | tf_op jit(solution)/shard_map/ppermute | solution.py:564
  123.2 16.1 %collective-permute-start.13 = (bf16[2,136,512]{2,1,0:T(8,128)(2,1)S(1)}, bf16[2,136,512]{2,1,0:T(8,128)(2,1)S(1)}, u32[]{:S(2)}, u32[]{:S(2)}) collective-permute-start(bf16[2,136,512]{2,1,0:T(8,128)(2,1)S(1)} %get-tuple-element.35), channel_id=1, source_target_pairs={{65,64},{66,65},{67,66},{68,67},{69,68},{70,69},{71,70},{72,71},{7... | collective-permute-start | bytes 835592 | tf_op jit(solution)/shard_map/ppermute | solution.py:565
  139.2 11.4 %collective-permute-start.17 = (bf16[4,128,512]{2,1,0:T(8,128)(2,1)S(1)}, bf16[4,128,512]{2,1,0:T(8,128)(2,1)S(1)}, u32[]{:S(2)}, u32[]{:S(2)}) collective-permute-start(bf16[4,128,512]{2,1,0:T(8,128)(2,1)S(1)} %get-tuple-element.31), channel_id=1, source_target_pairs={{0,32},{32,0},{64,96},{96,64},{1,33},{33,1},{65,97},{97,65},{2,34}... | collective-permute-start | bytes 1572872 | tf_op jit(solution)/shard_map/ppermute | solution.py:570
  150.5 2.0 %collective-permute-start.18 = (bf16[4,128,512]{2,1,0:T(8,128)(2,1)S(1)}, bf16[4,128,512]{2,1,0:T(8,128)(2,1)S(1)}, u32[]{:S(2)}, u32[]{:S(2)}) collective-permute-start(bf16[4,128,512]{2,1,0:T(8,128)(2,1)S(1)} %get-tuple-element.32), channel_id=1, source_target_pairs={{0,32},{32,0},{64,96},{96,64},{1,33},{33,1},{65,97},{97,65},{2,34}... | collective-permute-start | bytes 1572872 | tf_op jit(solution)/shard_map/ppermute | solution.py:570

commit v4 on v3

--- a/solution.py
+++ b/solution.py
@@ -305,8 +305,12 @@
         r = 2 * i
         two = pl.ds(r, 2)
         zf[two] = layer(x2, wb, r, row0 + 2)
-        if full is not None:
-            pltpu.make_async_copy(zf.at[two], full.at[two], sems.at[2]).start()
+        for k, part in enumerate(full):
+
+            @pl.when(i == k)
+            def _(part=part):
+                pltpu.make_async_copy(zf.at[two], part, sems.at[2]).start()
+
         zb[two] = zf[two, pl.ds(inner, half), :]
 
         @pl.when(core == 0)
@@ -333,8 +337,8 @@
         pltpu.make_async_copy(za, send, sems.at[0]).wait()
         pltpu.make_async_copy(zb, keep.at[window, :, right_half, :], sems.at[1]).wait()
 
-    if full is not None:
-        pltpu.make_async_copy(zf, full, sems.at[2]).wait()
+    for k, part in enumerate(full):
+        pltpu.make_async_copy(zf.at[pl.ds(2 * k, 2)], part, sems.at[2]).wait()
 
 
 def clear_edges(s, width):
@@ -346,8 +350,8 @@
 def early_kernel(window, chained, *refs):
     place, lo, hi, side, own_w, peer_w = refs[:6]
     refs = refs[6 + (1 if chained else 0) :]
-    keep, send, full = refs[:3]
-    scratch = refs[3:]
+    keep, send, *full = refs[:4]
+    scratch = refs[4:]
     x1, s2 = scratch[1], scratch[2]
     width = x1.shape[1]
     block = lo.shape[2]
@@ -378,24 +382,23 @@
 
 
 def late_kernel(window, *refs):
-    place, above, main, below, own_w, peer_w, _, _ = refs[:8]
-    keep, send = refs[8:10]
-    scratch = refs[10:]
+    place, above, upper, lower, below, own_w, peer_w, _, _ = refs[:9]
+    keep, send = refs[9:11]
+    scratch = refs[11:]
     x1, s2 = scratch[1], scratch[2]
     width = x1.shape[1]
 
     def fill(s):
         clear_edges(s, width)
         clear_edges(s2, width)
-        rim = above.shape[0]
-        mid = main.shape[0]
-        s[0:rim, EDGE : EDGE + width, :] = above[...].astype(F32)
-        s[rim : rim + mid, EDGE : EDGE + width, :] = main[...].astype(F32)
-        s[rim + mid :, EDGE : EDGE + width, :] = below[...].astype(F32)
+        at = 0
+        for piece in (above, upper, lower, below):
+            s[at : at + piece.shape[0], EDGE : EDGE + width, :] = piece[...].astype(F32)
+            at += piece.shape[0]
 
     @pl.when(place[0] == 1)
     def _():
-        duo_body(place, fill, own_w, peer_w, keep, send, None, scratch, window)
+        duo_body(place, fill, own_w, peer_w, keep, send, (), scratch, window)
 
 
 def duo_scratch(rows, width, ch):
@@ -430,30 +433,32 @@
         out_shape=(
             jax.ShapeDtypeStruct((windows, rows, 2 * half, ch), BF16),
             jax.ShapeDtypeStruct((rows, half, ch), BF16),
-            jax.ShapeDtypeStruct((rows, width, ch), BF16),
+            jax.ShapeDtypeStruct((rows // 2, width, ch), BF16),
+            jax.ShapeDtypeStruct((rows // 2, width, ch), BF16),
         ),
         in_specs=[smem_spec()]
         + [vmem_spec()] * 3
         + [hbm_spec()] * 2
         + [any_spec()] * (1 if chained else 0),
-        out_specs=(any_spec(), any_spec(), any_spec()),
+        out_specs=(any_spec(),) * 4,
         scratch_shapes=duo_scratch(rows, width, ch),
         input_output_aliases={6: 0} if chained else {},
         **duo_params(rows, width, ch),
     )(place, lo, hi, side, own_w, peer_w, *([keep] if chained else []))
 
 
-def late(window, place, above, main, below, own_w, peer_w, buffers):
-    rows, width, ch = main.shape
+def late(window, place, above, upper, lower, below, own_w, peer_w, buffers):
+    rows, width, ch = upper.shape
+    rows *= 2
     return pl.pallas_call(
         functools.partial(late_kernel, window),
         out_shape=tuple(jax.ShapeDtypeStruct(b.shape, b.dtype) for b in buffers),
-        in_specs=[smem_spec()] + [vmem_spec()] * 3 + [hbm_spec()] * 2 + [any_spec()] * 2,
+        in_specs=[smem_spec()] + [vmem_spec()] * 4 + [hbm_spec()] * 2 + [any_spec()] * 2,
         out_specs=(any_spec(), any_spec()),
         scratch_shapes=duo_scratch(rows, width, ch),
-        input_output_aliases={6: 0, 7: 1},
+        input_output_aliases={7: 0, 8: 1},
         **duo_params(rows, width, ch),
-    )(place, above, main, below, own_w, peer_w, *buffers)
+    )(place, above, upper, lower, below, own_w, peer_w, *buffers)
 
 
 def shards(features, weight_first, weight_second, weight_down, section_weights):
@@ -551,20 +556,20 @@
     sends, passed = [], []
     across = [(device(h, t), device(h + 2, t)) for h in range(2) for t in range(strips)]
     for w in range(windows):
-        keep, send, full = early(
+        keep, send, *full = early(
             w, early_place, *tiles[w], own_w, peer_w, keep, windows, strip_rows, half
         )
         sends.append(send)
-        passed.append(lax.ppermute(full, AXES, across))
+        passed.append([lax.ppermute(part, AXES, across) for part in full])
     later = [(device(s, a), device(s, b)) for s in (2, 3) for a, b in along]
     sooner = [(b, a) for a, b in later]
     others = []
     for w in range(windows):
-        main = passed[w]
-        above = lax.ppermute(main[strip_rows - 2 :], AXES, later)
-        below = lax.ppermute(main[:2], AXES, sooner)
+        upper, lower = passed[w]
+        above = lax.ppermute(lower, AXES, later)
+        below = lax.ppermute(upper, AXES, sooner)
         keep, send = late(
-            w, late_place, above, main, below, own_w, peer_w, (keep, sends[w])
+            w, late_place, above, upper, lower, below, own_w, peer_w, (keep, sends[w])
         )
         others.append(
             lax.ppermute(send, "segment", [(s, s ^ 1) for s in range(segments)])

time: 154 us -> 149 us (0.968)
  waiting for transfers between devices: 39.8 us -> 33.7 us
  starting transfers between devices: 69 us -> 70.9 us
    ppermute x6 -> x8, waiting for transfers between devices: 21.2 us -> 16.4 us  [the longest x4 16.4 us: shards(): passed.append([lax.ppermute(part, AXES, across) for part in full])]
    ppermute x6 -> x8, starting transfers between devices: 19.2 us -> 21.1 us  [the longest x2 8.31 us: shards(): below = lax.ppermute(upper, AXES, sooner)]
  transfers between devices with their start and end apart: 21 -> 23, of which waited for: 8 -> 10; matrix products, arithmetic and copies ran while one was open for 1% -> 1% of each run, Pallas kernels for 26% -> 27%
where the time goes in v4:
time: 149 us; the launch traced here: 148 us
  starting transfers between devices  70.9 us (48%)
  Pallas kernels  39.9 us (27%)
  waiting for transfers between devices  33.7 us (23%)
  local copies, waits for them, and re-layouts  3.19 us (2%)
    ppermute x2, starting transfers between devices, shards(): hi = lax.ppermute(got, AXES, high)  25 us
    pallas_call x2, Pallas kernels, late(): pl.pallas_call(functools.partial(late_kernel, window), out_shape=tuple((j...  22.4 us
    ppermute x4, waiting for transfers between devices, shards(): passed.append([lax.ppermute(part, AXES, across) for part in full])  16.4 us
    pallas_call x2, Pallas kernels, stem(): pl.pallas_call(functools.partial(stem_kernel, window), out_shape=jax.Shap...  15.7 us
    all_to_all x2, starting transfers between devices, shards(): lax.all_to_all(z.reshape(-1, *shape[2:]), 'strip', 0, 0, axis_index_group...  8.58 us
    ppermute x2, starting transfers between devices, shards(): below = lax.ppermute(upper, AXES, sooner)  8.31 us
    ppermute x2, starting transfers between devices, shards(): above = lax.ppermute(lower, AXES, later)  7.6 us
    ppermute x2, waiting for transfers between devices, shards(): hi = lax.ppermute(got, AXES, high)  7.32 us
  transfers between devices with their start and end apart: 23, of which 10 were waited for; matrix products, arithmetic and copies ran while one was open for 1% of the time, Pallas kernels for 27%

profile of v4, /device:TPU:29, one launch (start us, length us, event | category | flops | bytes accessed | tf_op | source)
XLA Modules:
  0.0 148.2 jit_solution(16094372673163345420)
XLA Ops:
  2.3 1.3 collective-permute-start
  3.6 3.0 %collective-permute-start.1 = (bf16[2,6,16,256]{3,1,2,0:T(8,128)(2,1)S(1)}, bf16[2,6,16,256]{3,1,2,0:T(8,128)(2,1)S(1)}, u32[]{:S(2)}, u32[]{:S(2)}) collective-permute-start(bf16[2,6,16,256]{3,1,2,0:T(8,128)(2,1)S(1)} %copy.12), channel_id=1, source_target_pairs={{32,0},{64,32},{96,64},{33,1},{65,33},{97,65},{34,2},{66,34},{98,6... | collective-permute-start | bytes 294920 | tf_op jit(solution)/shard_map/ppermute | solution.py:490
  6.6 1.8 %collective-permute-done = bf16[2,6,16,256]{3,1,2,0:T(8,128)(2,1)S(1)} collective-permute-done((bf16[2,6,16,256]{3,1,2,0:T(8,128)(2,1)S(1)}, bf16[2,6,16,256]{3,1,2,0:T(8,128)(2,1)S(1)}, u32[]{:S(2)}, u32[]{:S(2)}) %collective-permute-start) | collective-permute-done | bytes 98336 | tf_op jit(solution)/shard_map/ppermute | solution.py:489
  8.6 6.5 %collective-permute-start.3 = (bf16[2,2,76,256]{3,2,1,0:T(8,128)(2,1)S(1)}, bf16[2,2,76,256]{3,2,1,0:T(8,128)(2,1)S(1)}, u32[]{:S(2)}, u32[]{:S(2)}) collective-permute-start(bf16[2,2,76,256]{3,2,1,0:T(8,128)(2,1)S(1)} %pad_maximum_fusion.1), channel_id=1, source_target_pairs={{1,0},{2,1},{3,2},{4,3},{5,4},{6,5},{7,6},{8,7},{9,8},{10,9},{11,1... | collective-permute-start | bytes 466952 | tf_op jit(solution)/shard_map/ppermute | solution.py:501
  15.1 1.9 %collective-permute-start.2 = (bf16[2,2,76,256]{3,2,1,0:T(8,128)(2,1)S(1)}, bf16[2,2,76,256]{3,2,1,0:T(8,128)(2,1)S(1)}, u32[]{:S(2)}, u32[]{:S(2)}) collective-permute-start(bf16[2,2,76,256]{3,2,1,0:T(8,128)(2,1)S(1)} %pad_maximum_fusion), channel_id=1, source_target_pairs={{0,1},{1,2},{2,3},{3,4},{4,5},{5,6},{6,7},{7,8},{8,9},{9,10},{10,1... | collective-permute-start | bytes 466952 | tf_op jit(solution)/shard_map/ppermute | solution.py:498
  17.4 6.9 %collective-permute-done.2.left = bf16[2,2,76,256]{3,2,1,0:T(8,128)(2,1)S(1)} collective-permute-done((bf16[2,2,76,256]{3,2,1,0:T(8,128)(2,1)S(1)}, bf16[2,2,76,256]{3,2,1,0:T(8,128)(2,1)S(1)}, u32[]{:S(2)}, u32[]{:S(2)}) %collective-permute-start.2) | collective-permute-done | bytes 155680 | tf_op jit(solution)/shard_map/ppermute | solution.py:498
  24.2 7.8 %shard_map.56 = bf16[8,8,8,512]{3,2,1,0:T(8,128)(2,1)} custom-call(s32[4]{0:T(128)S(1)} %pad_add_fusion.place, bf16[2,64,16,256]{3,2,1,0:T(8,128)(2,1)S(1)} %copy-done.1, bf16[2,6,16,256]{3,2,1,0:T(8,128)(2,1)S(1)} %copy.13.up, bf16[2,6,16,256]{3,2,1,0:T(8,128)(2,1)S(1)} %copy.14.down, bf16[2,2,76,256]{3,2,1,0:T(8,128)(2,1)S(1)} %collective-permute-done.2.left, ...), custom_call_target="tpu_custom_call" | custom-call | flops 3454009344 | bytes 4194304 | tf_op jit(solution)/shard_map/pallas_call | solution.py:201
  32.1 3.5 %all-to-all-start.1 = ((bf16[64,8,512]{2,1,0:T(8,128)(2,1)}), bf16[64,8,512]{2,1,0:T(8,128)(2,1)S(1)}, u32[]{:S(2)}, u32[]{:S(2)}) async-start(bf16[64,8,512]{2,1,0:T(8,128)(2,1)} %bitcast.19), calls=%async_computation.1 | async-start | bytes 1048576 | tf_op jit(solution)/shard_map/all_to_all | solution.py:537
  35.6 7.8 %shard_map.55 = bf16[8,8,8,512]{3,2,1,0:T(8,128)(2,1)} custom-call(s32[4]{0:T(128)S(1)} %pad_add_fusion.place, bf16[2,64,16,256]{3,2,1,0:T(8,128)(2,1)S(1)} %copy-done.1, bf16[2,6,16,256]{3,2,1,0:T(8,128)(2,1)S(1)} %copy.13.up, bf16[2,6,16,256]{3,2,1,0:T(8,128)(2,1)S(1)} %copy.14.down, bf16[2,2,76,256]{3,2,1,0:T(8,128)(2,1)S(1)} %collective-permute-done.2.left, ...), custom_call_target="tpu_custom_call" | custom-call | flops 3454009344 | bytes 4194304 | tf_op jit(solution)/shard_map/pallas_call | solution.py:201
  43.4 5.1 %all-to-all-start = ((bf16[64,8,512]{2,1,0:T(8,128)(2,1)}), bf16[64,8,512]{2,1,0:T(8,128)(2,1)S(1)}, u32[]{:S(2)}, u32[]{:S(2)}) async-start(bf16[64,8,512]{2,1,0:T(8,128)(2,1)} %bitcast.15), calls=%async_computation | async-start | bytes 1048576 | tf_op jit(solution)/shard_map/all_to_all | solution.py:537
  49.2 8.2 %collective-permute-start.9 = (bf16[8,8,8,512]{3,2,1,0:T(8,128)(2,1)S(1)}, bf16[8,8,8,512]{3,2,1,0:T(8,128)(2,1)S(1)}, u32[]{:S(2)}, u32[]{:S(2)}) collective-permute-start(bf16[8,8,8,512]{3,2,1,0:T(8,128)(2,1)S(1)} %bitcast.37), channel_id=1, source_target_pairs={{8,0},{9,1},{10,2},{11,3},{12,4},{13,5},{14,6},{15,7},{24,32},{25,... | collective-permute-start | bytes 1572872 | tf_op jit(solution)/shard_map/ppermute | solution.py:541
  58.9 16.8 %collective-permute-start.5 = (bf16[8,8,8,512]{3,2,1,0:T(8,128)(2,1)S(1)}, bf16[8,8,8,512]{3,2,1,0:T(8,128)(2,1)S(1)}, u32[]{:S(2)}, u32[]{:S(2)}) collective-permute-start(bf16[8,8,8,512]{3,2,1,0:T(8,128)(2,1)S(1)} %bitcast.35), channel_id=1, source_target_pairs={{8,0},{9,1},{10,2},{11,3},{12,4},{13,5},{14,6},{15,7},{24,32},{25,... | collective-permute-start | bytes 1572872 | tf_op jit(solution)/shard_map/ppermute | solution.py:541
  77.1 1.3 collective-permute-start.15
  79.7 7.3 %collective-permute-done.5.refs_2_ = bf16[8,8,8,512]{3,2,1,0:T(8,128)(2,1)S(1)} collective-permute-done((bf16[8,8,8,512]{3,2,1,0:T(8,128)(2,1)S(1)}, bf16[8,8,8,512]{3,2,1,0:T(8,128)(2,1)S(1)}, u32[]{:S(2)}, u32[]{:S(2)}) %collective-permute-start.5) | collective-permute-done | bytes 524320 | tf_op jit(solution)/shard_map/ppermute | solution.py:541
  90.4 6.4 %collective-permute-done.15.refs_3_ = bf16[2,136,512]{2,1,0:T(8,128)(2,1)S(1)} collective-permute-done((bf16[2,136,512]{2,1,0:T(8,128)(2,1)S(1)}, bf16[2,136,512]{2,1,0:T(8,128)(2,1)S(1)}, u32[]{:S(2)}, u32[]{:S(2)}) %collective-permute-start.15) | collective-permute-done | bytes 278560 | tf_op jit(solution)/shard_map/ppermute | solution.py:563
  96.9 4.3 %collective-permute-start.16 = (bf16[2,136,512]{2,1,0:T(8,128)(2,1)S(1)}, bf16[2,136,512]{2,1,0:T(8,128)(2,1)S(1)}, u32[]{:S(2)}, u32[]{:S(2)}) collective-permute-start(bf16[2,136,512]{2,1,0:T(8,128)(2,1)S(1)} %collective-permute-done.15.refs_3_), channel_id=1, source_target_pairs={{64,65},{65,66},{66,67},{67,68},{68,69},{69,70},{70,71},{71,72},{7... | collective-permute-start | bytes 835592 | tf_op jit(solution)/shard_map/ppermute | solution.py:569
  101.2 1.4 collective-permute-done.17.refs_2_
  102.6 5.1 %collective-permute-start.18 = (bf16[2,136,512]{2,1,0:T(8,128)(2,1)S(1)}, bf16[2,136,512]{2,1,0:T(8,128)(2,1)S(1)}, u32[]{:S(2)}, u32[]{:S(2)}) collective-permute-start(bf16[2,136,512]{2,1,0:T(8,128)(2,1)S(1)} %collective-permute-done.17.refs_2_), channel_id=1, source_target_pairs={{65,64},{66,65},{67,66},{68,67},{69,68},{70,69},{71,70},{72,71},{7... | collective-permute-start | bytes 835592 | tf_op jit(solution)/shard_map/ppermute | solution.py:570
  107.8 6.7 %collective-permute-done.11.refs_3_ = bf16[2,136,512]{2,1,0:T(8,128)(2,1)S(1)} collective-permute-done((bf16[2,136,512]{2,1,0:T(8,128)(2,1)S(1)}, bf16[2,136,512]{2,1,0:T(8,128)(2,1)S(1)}, u32[]{:S(2)}, u32[]{:S(2)}) %collective-permute-start.11) | collective-permute-done | bytes 278560 | tf_op jit(solution)/shard_map/ppermute | solution.py:563
  114.5 3.3 %collective-permute-start.12 = (bf16[2,136,512]{2,1,0:T(8,128)(2,1)S(1)}, bf16[2,136,512]{2,1,0:T(8,128)(2,1)S(1)}, u32[]{:S(2)}, u32[]{:S(2)}) collective-permute-start(bf16[2,136,512]{2,1,0:T(8,128)(2,1)S(1)} %collective-permute-done.11.refs_3_), channel_id=1, source_target_pairs={{64,65},{65,66},{66,67},{67,68},{68,69},{69,70},{70,71},{71,72},{7... | collective-permute-start | bytes 835592 | tf_op jit(solution)/shard_map/ppermute | solution.py:569
  117.8 1.8 %collective-permute-done.13.refs_2_ = bf16[2,136,512]{2,1,0:T(8,128)(2,1)S(1)} collective-permute-done((bf16[2,136,512]{2,1,0:T(8,128)(2,1)S(1)}, bf16[2,136,512]{2,1,0:T(8,128)(2,1)S(1)}, u32[]{:S(2)}, u32[]{:S(2)}) %collective-permute-start.13) | collective-permute-done | bytes 278560 | tf_op jit(solution)/shard_map/ppermute | solution.py:563
  119.6 3.2 %collective-permute-start.14 = (bf16[2,136,512]{2,1,0:T(8,128)(2,1)S(1)}, bf16[2,136,512]{2,1,0:T(8,128)(2,1)S(1)}, u32[]{:S(2)}, u32[]{:S(2)}) collective-permute-start(bf16[2,136,512]{2,1,0:T(8,128)(2,1)S(1)} %collective-permute-done.13.refs_2_), channel_id=1, source_target_pairs={{65,64},{66,65},{67,66},{68,67},{69,68},{70,69},{71,70},{72,71},{7... | collective-permute-start | bytes 835592 | tf_op jit(solution)/shard_map/ppermute | solution.py:570
  122.8 11.2 %shard_map.59 = (bf16[2,4,256,512]{3,2,1,0:T(8,128)(2,1)}, bf16[4,128,512]{2,1,0:T(8,128)(2,1)S(1)}) custom-call(s32[6]{0:T(128)S(1)} %stack.53.refs_0_, bf16[2,136,512]{2,1,0:T(8,128)(2,1)S(1)} %collective-permute-done.16.refs_1_, bf16[2,136,512]{2,1,0:T(8,128)(2,1)S(1)} %collective-permute-done.17.refs_2_, ...), custom_call_target="tpu_custom_call", output_to_operand_aliasing={{0}: (7, {}), {1}: (8, {})} | custom-call | flops 6417285120 | bytes 12582912 | tf_op jit(solution)/shard_map/pallas_call | solution.py:453
  134.2 11.2 %shard_map.60 = (bf16[2,4,256,512]{3,2,1,0:T(8,128)(2,1)}, bf16[4,128,512]{2,1,0:T(8,128)(2,1)S(1)}) custom-call(s32[6]{0:T(128)S(1)} %stack.53.refs_0_, bf16[2,136,512]{2,1,0:T(8,128)(2,1)S(1)} %collective-permute-done.12.refs_1_, bf16[2,136,512]{2,1,0:T(8,128)(2,1)S(1)} %collective-permute-done.13.refs_2_, ...), custom_call_target="tpu_custom_call", output_to_operand_aliasing={{0}: (7, {}), {1}: (8, {})} | custom-call | flops 6417285120 | bytes 12582912 | tf_op jit(solution)/shard_map/pallas_call | solution.py:453
  (48 shorter events, 13.9 us)
Async XLA Ops:
  0.0 76.4 %collective-permute-start.7 = (bf16[3,1536,512]{2,1,0:T(8,128)(2,1)}, bf16[3,1536,512]{2,1,0:T(8,128)(2,1)}, u32[]{:S(2)}, u32[]{:S(2)}) collective-permute-start(bf16[3,1536,512]{2,1,0:T(8,128)(2,1)} %bitcast.39), channel_id=1, source_target_pairs={{0,32},{32,0},{64,96},{96,64},{1,33},{33,1},{65,97},{97,65},{2,34}... | collective-permute-start | bytes 14155784 | tf_op jit(solution)/shard_map/ppermute | solution.py:483
  1.9 22.3 %copy-start.1 = (bf16[2,64,16,256]{3,2,1,0:T(8,128)(2,1)S(1)}, bf16[2,64,16,256]{3,2,1,0:T(8,128)(2,1)}, u32[]{:S(2)}) copy-start(bf16[2,64,16,256]{3,2,1,0:T(8,128)(2,1)} %feat.5) | copy-start | bytes 3145732
  2.3 6.2 %collective-permute-start = (bf16[2,6,16,256]{3,1,2,0:T(8,128)(2,1)S(1)}, bf16[2,6,16,256]{3,1,2,0:T(8,128)(2,1)S(1)}, u32[]{:S(2)}, u32[]{:S(2)}) collective-permute-start(bf16[2,6,16,256]{3,1,2,0:T(8,128)(2,1)S(1)} %copy.11), channel_id=1, source_target_pairs={{0,32},{32,64},{64,96},{1,33},{33,65},{65,97},{2,34},{34,66},{66,9... | collective-permute-start | bytes 294920 | tf_op jit(solution)/shard_map/ppermute | solution.py:489
  3.6 5.0 %collective-permute-start.1 = (bf16[2,6,16,256]{3,1,2,0:T(8,128)(2,1)S(1)}, bf16[2,6,16,256]{3,1,2,0:T(8,128)(2,1)S(1)}, u32[]{:S(2)}, u32[]{:S(2)}) collective-permute-start(bf16[2,6,16,256]{3,1,2,0:T(8,128)(2,1)S(1)} %copy.12), channel_id=1, source_target_pairs={{32,0},{64,32},{96,64},{33,1},{65,33},{97,65},{34,2},{66,34},{98,6... | collective-permute-start | bytes 294920 | tf_op jit(solution)/shard_map/ppermute | solution.py:490
  8.6 8.7 %collective-permute-start.3 = (bf16[2,2,76,256]{3,2,1,0:T(8,128)(2,1)S(1)}, bf16[2,2,76,256]{3,2,1,0:T(8,128)(2,1)S(1)}, u32[]{:S(2)}, u32[]{:S(2)}) collective-permute-start(bf16[2,2,76,256]{3,2,1,0:T(8,128)(2,1)S(1)} %pad_maximum_fusion.1), channel_id=1, source_target_pairs={{1,0},{2,1},{3,2},{4,3},{5,4},{6,5},{7,6},{8,7},{9,8},{10,9},{11,1... | collective-permute-start | bytes 466952 | tf_op jit(solution)/shard_map/ppermute | solution.py:501
  15.1 9.1 %collective-permute-start.2 = (bf16[2,2,76,256]{3,2,1,0:T(8,128)(2,1)S(1)}, bf16[2,2,76,256]{3,2,1,0:T(8,128)(2,1)S(1)}, u32[]{:S(2)}, u32[]{:S(2)}) collective-permute-start(bf16[2,2,76,256]{3,2,1,0:T(8,128)(2,1)S(1)} %pad_maximum_fusion), channel_id=1, source_target_pairs={{0,1},{1,2},{2,3},{3,4},{4,5},{5,6},{6,7},{7,8},{8,9},{9,10},{10,1... | collective-permute-start | bytes 466952 | tf_op jit(solution)/shard_map/ppermute | solution.py:498
  32.1 11.4 %all-to-all-start.1 = ((bf16[64,8,512]{2,1,0:T(8,128)(2,1)}), bf16[64,8,512]{2,1,0:T(8,128)(2,1)S(1)}, u32[]{:S(2)}, u32[]{:S(2)}) async-start(bf16[64,8,512]{2,1,0:T(8,128)(2,1)} %bitcast.19), calls=%async_computation.1 | async-start | bytes 1048576 | tf_op jit(solution)/shard_map/all_to_all | solution.py:537
  43.4 14.8 %all-to-all-start = ((bf16[64,8,512]{2,1,0:T(8,128)(2,1)}), bf16[64,8,512]{2,1,0:T(8,128)(2,1)S(1)}, u32[]{:S(2)}, u32[]{:S(2)}) async-start(bf16[64,8,512]{2,1,0:T(8,128)(2,1)} %bitcast.15), calls=%async_computation | async-start | bytes 1048576 | tf_op jit(solution)/shard_map/all_to_all | solution.py:537
  48.5 27.2 %collective-permute-start.8 = (bf16[8,8,8,512]{3,2,1,0:T(8,128)(2,1)S(1)}, bf16[8,8,8,512]{3,2,1,0:T(8,128)(2,1)S(1)}, u32[]{:S(2)}, u32[]{:S(2)}) collective-permute-start(bf16[8,8,8,512]{3,2,1,0:T(8,128)(2,1)S(1)} %bitcast.36), channel_id=1, source_target_pairs={{0,0},{1,1},{2,2},{3,3},{4,4},{5,5},{6,6},{7,7},{16,32},{17,33},{1... | collective-permute-start | bytes 1572872 | tf_op jit(solution)/shard_map/ppermute | solution.py:540
  49.2 27.2 %collective-permute-start.9 = (bf16[8,8,8,512]{3,2,1,0:T(8,128)(2,1)S(1)}, bf16[8,8,8,512]{3,2,1,0:T(8,128)(2,1)S(1)}, u32[]{:S(2)}, u32[]{:S(2)}) collective-permute-start(bf16[8,8,8,512]{3,2,1,0:T(8,128)(2,1)S(1)} %bitcast.37), channel_id=1, source_target_pairs={{8,0},{9,1},{10,2},{11,3},{12,4},{13,5},{14,6},{15,7},{24,32},{25,... | collective-permute-start | bytes 1572872 | tf_op jit(solution)/shard_map/ppermute | solution.py:541
  57.5 1.4 collective-permute-start.10
  58.2 21.5 %collective-permute-start.4 = (bf16[8,8,8,512]{3,2,1,0:T(8,128)(2,1)S(1)}, bf16[8,8,8,512]{3,2,1,0:T(8,128)(2,1)S(1)}, u32[]{:S(2)}, u32[]{:S(2)}) collective-permute-start(bf16[8,8,8,512]{3,2,1,0:T(8,128)(2,1)S(1)} %bitcast.33), channel_id=1, source_target_pairs={{0,0},{1,1},{2,2},{3,3},{4,4},{5,5},{6,6},{7,7},{16,32},{17,33},{1... | collective-permute-start | bytes 1572872 | tf_op jit(solution)/shard_map/ppermute | solution.py:540
  58.9 28.0 %collective-permute-start.5 = (bf16[8,8,8,512]{3,2,1,0:T(8,128)(2,1)S(1)}, bf16[8,8,8,512]{3,2,1,0:T(8,128)(2,1)S(1)}, u32[]{:S(2)}, u32[]{:S(2)}) collective-permute-start(bf16[8,8,8,512]{3,2,1,0:T(8,128)(2,1)S(1)} %bitcast.35), channel_id=1, source_target_pairs={{8,0},{9,1},{10,2},{11,3},{12,4},{13,5},{14,6},{15,7},{24,32},{25,... | collective-permute-start | bytes 1572872 | tf_op jit(solution)/shard_map/ppermute | solution.py:541
  75.7 3.9 %collective-permute-start.6 = (bf16[8,8,512]{2,1,0:T(8,128)(2,1)S(1)}, bf16[8,8,512]{2,1,0:T(8,128)(2,1)S(1)}, u32[]{:S(2)}, u32[]{:S(2)}) collective-permute-start(bf16[8,8,512]{2,1,0:T(8,128)(2,1)S(1)} %dynamic-slice_bitcast_fusion.1), channel_id=1, source_target_pairs={{8,32},{9,33},{10,34},{11,35},{12,36},{13,37},{14,38},{15,39},{16,... | collective-permute-start | bytes 196616 | tf_op jit(solution)/shard_map/ppermute | solution.py:543
  77.1 19.8 %collective-permute-start.15 = (bf16[2,136,512]{2,1,0:T(8,128)(2,1)S(1)}, bf16[2,136,512]{2,1,0:T(8,128)(2,1)S(1)}, u32[]{:S(2)}, u32[]{:S(2)}) collective-permute-start(bf16[2,136,512]{2,1,0:T(8,128)(2,1)S(1)} %get-tuple-element.28), channel_id=1, source_target_pairs={{0,64},{1,65},{2,66},{3,67},{4,68},{5,69},{6,70},{7,71},{8,72},{9,... | collective-permute-start | bytes 835592 | tf_op jit(solution)/shard_map/ppermute | solution.py:563
  78.4 24.2 %collective-permute-start.17 = (bf16[2,136,512]{2,1,0:T(8,128)(2,1)S(1)}, bf16[2,136,512]{2,1,0:T(8,128)(2,1)S(1)}, u32[]{:S(2)}, u32[]{:S(2)}) collective-permute-start(bf16[2,136,512]{2,1,0:T(8,128)(2,1)S(1)} %get-tuple-element.29), channel_id=1, source_target_pairs={{0,64},{1,65},{2,66},{3,67},{4,68},{5,69},{6,70},{7,71},{8,72},{9,... | collective-permute-start | bytes 835592 | tf_op jit(solution)/shard_map/ppermute | solution.py:563
  87.8 26.7 %collective-permute-start.11 = (bf16[2,136,512]{2,1,0:T(8,128)(2,1)S(1)}, bf16[2,136,512]{2,1,0:T(8,128)(2,1)S(1)}, u32[]{:S(2)}, u32[]{:S(2)}) collective-permute-start(bf16[2,136,512]{2,1,0:T(8,128)(2,1)S(1)} %get-tuple-element.26), channel_id=1, source_target_pairs={{0,64},{1,65},{2,66},{3,67},{4,68},{5,69},{6,70},{7,71},{8,72},{9,... | collective-permute-start | bytes 835592 | tf_op jit(solution)/shard_map/ppermute | solution.py:563
  89.1 30.4 %collective-permute-start.13 = (bf16[2,136,512]{2,1,0:T(8,128)(2,1)S(1)}, bf16[2,136,512]{2,1,0:T(8,128)(2,1)S(1)}, u32[]{:S(2)}, u32[]{:S(2)}) collective-permute-start(bf16[2,136,512]{2,1,0:T(8,128)(2,1)S(1)} %get-tuple-element.27), channel_id=1, source_target_pairs={{0,64},{1,65},{2,66},{3,67},{4,68},{5,69},{6,70},{7,71},{8,72},{9,... | collective-permute-start | bytes 835592 | tf_op jit(solution)/shard_map/ppermute | solution.py:563
  96.9 26.0 %collective-permute-start.16 = (bf16[2,136,512]{2,1,0:T(8,128)(2,1)S(1)}, bf16[2,136,512]{2,1,0:T(8,128)(2,1)S(1)}, u32[]{:S(2)}, u32[]{:S(2)}) collective-permute-start(bf16[2,136,512]{2,1,0:T(8,128)(2,1)S(1)} %collective-permute-done.15.refs_3_), channel_id=1, source_target_pairs={{64,65},{65,66},{66,67},{67,68},{68,69},{69,70},{70,71},{71,72},{7... | collective-permute-start | bytes 835592 | tf_op jit(solution)/shard_map/ppermute | solution.py:569
  102.6 20.2 %collective-permute-start.18 = (bf16[2,136,512]{2,1,0:T(8,128)(2,1)S(1)}, bf16[2,136,512]{2,1,0:T(8,128)(2,1)S(1)}, u32[]{:S(2)}, u32[]{:S(2)}) collective-permute-start(bf16[2,136,512]{2,1,0:T(8,128)(2,1)S(1)} %collective-permute-done.17.refs_2_), channel_id=1, source_target_pairs={{65,64},{66,65},{67,66},{68,67},{69,68},{70,69},{71,70},{72,71},{7... | collective-permute-start | bytes 835592 | tf_op jit(solution)/shard_map/ppermute | solution.py:570
  114.5 19.6 %collective-permute-start.12 = (bf16[2,136,512]{2,1,0:T(8,128)(2,1)S(1)}, bf16[2,136,512]{2,1,0:T(8,128)(2,1)S(1)}, u32[]{:S(2)}, u32[]{:S(2)}) collective-permute-start(bf16[2,136,512]{2,1,0:T(8,128)(2,1)S(1)} %collective-permute-done.11.refs_3_), channel_id=1, source_target_pairs={{64,65},{65,66},{66,67},{67,68},{68,69},{69,70},{70,71},{71,72},{7... | collective-permute-start | bytes 835592 | tf_op jit(solution)/shard_map/ppermute | solution.py:569
  119.6 14.6 %collective-permute-start.14 = (bf16[2,136,512]{2,1,0:T(8,128)(2,1)S(1)}, bf16[2,136,512]{2,1,0:T(8,128)(2,1)S(1)}, u32[]{:S(2)}, u32[]{:S(2)}) collective-permute-start(bf16[2,136,512]{2,1,0:T(8,128)(2,1)S(1)} %collective-permute-done.13.refs_2_), channel_id=1, source_target_pairs={{65,64},{66,65},{67,66},{68,67},{69,68},{70,69},{71,70},{72,71},{7... | collective-permute-start | bytes 835592 | tf_op jit(solution)/shard_map/ppermute | solution.py:570
  134.1 11.4 %collective-permute-start.19 = (bf16[4,128,512]{2,1,0:T(8,128)(2,1)S(1)}, bf16[4,128,512]{2,1,0:T(8,128)(2,1)S(1)}, u32[]{:S(2)}, u32[]{:S(2)}) collective-permute-start(bf16[4,128,512]{2,1,0:T(8,128)(2,1)S(1)} %get-tuple-element.35), channel_id=1, source_target_pairs={{0,32},{32,0},{64,96},{96,64},{1,33},{33,1},{65,97},{97,65},{2,34}... | collective-permute-start | bytes 1572872 | tf_op jit(solution)/shard_map/ppermute | solution.py:575
  145.4 2.0 %collective-permute-start.20 = (bf16[4,128,512]{2,1,0:T(8,128)(2,1)S(1)}, bf16[4,128,512]{2,1,0:T(8,128)(2,1)S(1)}, u32[]{:S(2)}, u32[]{:S(2)}) collective-permute-start(bf16[4,128,512]{2,1,0:T(8,128)(2,1)S(1)} %get-tuple-element.36), channel_id=1, source_target_pairs={{0,32},{32,0},{64,96},{96,64},{1,33},{33,1},{65,97},{97,65},{2,34}... | collective-permute-start | bytes 1572872 | tf_op jit(solution)/shard_map/ppermute | solution.py:575
  (1 other events, 1.2 us)

commit v5 on v4

--- a/solution.py
+++ b/solution.py
@@ -257,19 +257,23 @@
 
         lax.fori_loop(0, dst.shape[0], go, 0)
 
-    def layer(x, w, r, first_row, ready=None):
+    def layer(x, w, r, first_row, ready=None, cols=None):
+        start, span = cols or (0, width)
+        keep_cols = pl.ds(start, span)
         acc = None
         for a in range(3):
             if ready is not None:
                 ready(a)
             part = jnp.dot(
-                x[pl.ds(r + a, 2)].reshape(2 * width, 3 * ch), w[a], preferred_element_type=F32
+                x[pl.ds(r + a, 2), keep_cols].reshape(2 * span, 3 * ch),
+                w[a],
+                preferred_element_type=F32,
             )
             acc = part if acc is None else acc + part
-        acc = acc.reshape(2, width, ch)
-        y = jnp.maximum(acc + x[pl.ds(r + 1, 2), :, ch : 2 * ch].astype(F32), 0.0)
-        row = first_row + r + lax.broadcasted_iota(jnp.int32, (2, width, 1), 0)
-        col = col0 + lax.broadcasted_iota(jnp.int32, (2, width, 1), 1)
+        acc = acc.reshape(2, span, ch)
+        y = jnp.maximum(acc + x[pl.ds(r + 1, 2), keep_cols, ch : 2 * ch].astype(F32), 0.0)
+        row = first_row + r + lax.broadcasted_iota(jnp.int32, (2, span, 1), 0)
+        col = col0 + start + lax.broadcasted_iota(jnp.int32, (2, span, 1), 1)
         ok = (row >= 0) & (row < row_total) & (col >= 0) & (col < col_total)
         return jnp.where(ok, y, 0.0).astype(BF16)
 
@@ -304,14 +308,18 @@
     def second(i, carry):
         r = 2 * i
         two = pl.ds(r, 2)
-        zf[two] = layer(x2, wb, r, row0 + 2)
+        if full:
+            zf[two] = layer(x2, wb, r, row0 + 2)
         for k, part in enumerate(full):
 
             @pl.when(i == k)
             def _(part=part):
                 pltpu.make_async_copy(zf.at[two], part, sems.at[2]).start()
 
-        zb[two] = zf[two, pl.ds(inner, half), :]
+        if full:
+            zb[two] = zf[two, pl.ds(inner, half), :]
+        else:
+            zb[two] = layer(x2, wb, r, row0 + 2, cols=(inner, half))
 
         @pl.when(core == 0)
         def _():

time: 149 us -> 148 us (level)
  no operation moved by 1% of the time
where the time goes in v5:
time: 148 us
  starting transfers between devices  70.9 us (48%)
  Pallas kernels  39.5 us (27%)
  waiting for transfers between devices  33.7 us (23%)
  local copies, waits for them, and re-layouts  3.19 us (2%)
    ppermute x2, starting transfers between devices, shards(): hi = lax.ppermute(got, AXES, high)  25 us
    pallas_call x2, Pallas kernels, late(): pl.pallas_call(functools.partial(late_kernel, window), out_shape=tuple((j...  22 us
    ppermute x4, waiting for transfers between devices, shards(): passed.append([lax.ppermute(part, AXES, across) for part in full])  16.4 us
    pallas_call x2, Pallas kernels, stem(): pl.pallas_call(functools.partial(stem_kernel, window), out_shape=jax.Shap...  15.7 us
    all_to_all x2, starting transfers between devices, shards(): lax.all_to_all(z.reshape(-1, *shape[2:]), 'strip', 0, 0, axis_index_group...  8.58 us
    ppermute x2, starting transfers between devices, shards(): below = lax.ppermute(upper, AXES, sooner)  8.31 us
    ppermute x2, starting transfers between devices, shards(): above = lax.ppermute(lower, AXES, later)  7.6 us
    ppermute x2, waiting for transfers between devices, shards(): hi = lax.ppermute(got, AXES, high)  7.32 us
  transfers between devices with their start and end apart: 23, of which 10 were waited for; matrix products, arithmetic and copies ran while one was open for 1% of the time, Pallas kernels for 27%

profile of v5, /device:TPU:29, one launch (start us, length us, event | category | flops | bytes accessed | tf_op | source)
XLA Modules:
  0.0 147.8 jit_solution(11673324166996853614)
XLA Ops:
  2.3 1.3 collective-permute-start
  3.6 3.0 %collective-permute-start.1 = (bf16[2,6,16,256]{3,1,2,0:T(8,128)(2,1)S(1)}, bf16[2,6,16,256]{3,1,2,0:T(8,128)(2,1)S(1)}, u32[]{:S(2)}, u32[]{:S(2)}) collective-permute-start(bf16[2,6,16,256]{3,1,2,0:T(8,128)(2,1)S(1)} %copy.12), channel_id=1, source_target_pairs={{32,0},{64,32},{96,64},{33,1},{65,33},{97,65},{34,2},{66,34},{98,6... | collective-permute-start | bytes 294920 | tf_op jit(solution)/shard_map/ppermute | solution.py:498
  6.6 1.8 %collective-permute-done = bf16[2,6,16,256]{3,1,2,0:T(8,128)(2,1)S(1)} collective-permute-done((bf16[2,6,16,256]{3,1,2,0:T(8,128)(2,1)S(1)}, bf16[2,6,16,256]{3,1,2,0:T(8,128)(2,1)S(1)}, u32[]{:S(2)}, u32[]{:S(2)}) %collective-permute-start) | collective-permute-done | bytes 98336 | tf_op jit(solution)/shard_map/ppermute | solution.py:497
  8.6 6.5 %collective-permute-start.3 = (bf16[2,2,76,256]{3,2,1,0:T(8,128)(2,1)S(1)}, bf16[2,2,76,256]{3,2,1,0:T(8,128)(2,1)S(1)}, u32[]{:S(2)}, u32[]{:S(2)}) collective-permute-start(bf16[2,2,76,256]{3,2,1,0:T(8,128)(2,1)S(1)} %pad_maximum_fusion.1), channel_id=1, source_target_pairs={{1,0},{2,1},{3,2},{4,3},{5,4},{6,5},{7,6},{8,7},{9,8},{10,9},{11,1... | collective-permute-start | bytes 466952 | tf_op jit(solution)/shard_map/ppermute | solution.py:509
  15.1 1.9 %collective-permute-start.2 = (bf16[2,2,76,256]{3,2,1,0:T(8,128)(2,1)S(1)}, bf16[2,2,76,256]{3,2,1,0:T(8,128)(2,1)S(1)}, u32[]{:S(2)}, u32[]{:S(2)}) collective-permute-start(bf16[2,2,76,256]{3,2,1,0:T(8,128)(2,1)S(1)} %pad_maximum_fusion), channel_id=1, source_target_pairs={{0,1},{1,2},{2,3},{3,4},{4,5},{5,6},{6,7},{7,8},{8,9},{9,10},{10,1... | collective-permute-start | bytes 466952 | tf_op jit(solution)/shard_map/ppermute | solution.py:506
  17.4 6.9 %collective-permute-done.2.left = bf16[2,2,76,256]{3,2,1,0:T(8,128)(2,1)S(1)} collective-permute-done((bf16[2,2,76,256]{3,2,1,0:T(8,128)(2,1)S(1)}, bf16[2,2,76,256]{3,2,1,0:T(8,128)(2,1)S(1)}, u32[]{:S(2)}, u32[]{:S(2)}) %collective-permute-start.2) | collective-permute-done | bytes 155680 | tf_op jit(solution)/shard_map/ppermute | solution.py:506
  24.2 7.8 %shard_map.56 = bf16[8,8,8,512]{3,2,1,0:T(8,128)(2,1)} custom-call(s32[4]{0:T(128)S(1)} %pad_add_fusion.place, bf16[2,64,16,256]{3,2,1,0:T(8,128)(2,1)S(1)} %copy-done.1, bf16[2,6,16,256]{3,2,1,0:T(8,128)(2,1)S(1)} %copy.13.up, bf16[2,6,16,256]{3,2,1,0:T(8,128)(2,1)S(1)} %copy.14.down, bf16[2,2,76,256]{3,2,1,0:T(8,128)(2,1)S(1)} %collective-permute-done.2.left, ...), custom_call_target="tpu_custom_call" | custom-call | flops 3454009344 | bytes 4194304 | tf_op jit(solution)/shard_map/pallas_call | solution.py:201
  32.1 3.5 %all-to-all-start.1 = ((bf16[64,8,512]{2,1,0:T(8,128)(2,1)}), bf16[64,8,512]{2,1,0:T(8,128)(2,1)S(1)}, u32[]{:S(2)}, u32[]{:S(2)}) async-start(bf16[64,8,512]{2,1,0:T(8,128)(2,1)} %bitcast.19), calls=%async_computation.1 | async-start | bytes 1048576 | tf_op jit(solution)/shard_map/all_to_all | solution.py:545
  35.6 7.8 %shard_map.55 = bf16[8,8,8,512]{3,2,1,0:T(8,128)(2,1)} custom-call(s32[4]{0:T(128)S(1)} %pad_add_fusion.place, bf16[2,64,16,256]{3,2,1,0:T(8,128)(2,1)S(1)} %copy-done.1, bf16[2,6,16,256]{3,2,1,0:T(8,128)(2,1)S(1)} %copy.13.up, bf16[2,6,16,256]{3,2,1,0:T(8,128)(2,1)S(1)} %copy.14.down, bf16[2,2,76,256]{3,2,1,0:T(8,128)(2,1)S(1)} %collective-permute-done.2.left, ...), custom_call_target="tpu_custom_call" | custom-call | flops 3454009344 | bytes 4194304 | tf_op jit(solution)/shard_map/pallas_call | solution.py:201
  43.4 5.1 %all-to-all-start = ((bf16[64,8,512]{2,1,0:T(8,128)(2,1)}), bf16[64,8,512]{2,1,0:T(8,128)(2,1)S(1)}, u32[]{:S(2)}, u32[]{:S(2)}) async-start(bf16[64,8,512]{2,1,0:T(8,128)(2,1)} %bitcast.15), calls=%async_computation | async-start | bytes 1048576 | tf_op jit(solution)/shard_map/all_to_all | solution.py:545
  49.2 8.2 %collective-permute-start.9 = (bf16[8,8,8,512]{3,2,1,0:T(8,128)(2,1)S(1)}, bf16[8,8,8,512]{3,2,1,0:T(8,128)(2,1)S(1)}, u32[]{:S(2)}, u32[]{:S(2)}) collective-permute-start(bf16[8,8,8,512]{3,2,1,0:T(8,128)(2,1)S(1)} %bitcast.37), channel_id=1, source_target_pairs={{8,0},{9,1},{10,2},{11,3},{12,4},{13,5},{14,6},{15,7},{24,32},{25,... | collective-permute-start | bytes 1572872 | tf_op jit(solution)/shard_map/ppermute | solution.py:549
  58.9 16.8 %collective-permute-start.5 = (bf16[8,8,8,512]{3,2,1,0:T(8,128)(2,1)S(1)}, bf16[8,8,8,512]{3,2,1,0:T(8,128)(2,1)S(1)}, u32[]{:S(2)}, u32[]{:S(2)}) collective-permute-start(bf16[8,8,8,512]{3,2,1,0:T(8,128)(2,1)S(1)} %bitcast.35), channel_id=1, source_target_pairs={{8,0},{9,1},{10,2},{11,3},{12,4},{13,5},{14,6},{15,7},{24,32},{25,... | collective-permute-start | bytes 1572872 | tf_op jit(solution)/shard_map/ppermute | solution.py:549
  77.1 1.3 collective-permute-start.15
  79.7 7.3 %collective-permute-done.5.refs_2_ = bf16[8,8,8,512]{3,2,1,0:T(8,128)(2,1)S(1)} collective-permute-done((bf16[8,8,8,512]{3,2,1,0:T(8,128)(2,1)S(1)}, bf16[8,8,8,512]{3,2,1,0:T(8,128)(2,1)S(1)}, u32[]{:S(2)}, u32[]{:S(2)}) %collective-permute-start.5) | collective-permute-done | bytes 524320 | tf_op jit(solution)/shard_map/ppermute | solution.py:549
  90.4 6.4 %collective-permute-done.15.refs_3_ = bf16[2,136,512]{2,1,0:T(8,128)(2,1)S(1)} collective-permute-done((bf16[2,136,512]{2,1,0:T(8,128)(2,1)S(1)}, bf16[2,136,512]{2,1,0:T(8,128)(2,1)S(1)}, u32[]{:S(2)}, u32[]{:S(2)}) %collective-permute-start.15) | collective-permute-done | bytes 278560 | tf_op jit(solution)/shard_map/ppermute | solution.py:571
  96.9 4.3 %collective-permute-start.16 = (bf16[2,136,512]{2,1,0:T(8,128)(2,1)S(1)}, bf16[2,136,512]{2,1,0:T(8,128)(2,1)S(1)}, u32[]{:S(2)}, u32[]{:S(2)}) collective-permute-start(bf16[2,136,512]{2,1,0:T(8,128)(2,1)S(1)} %collective-permute-done.15.refs_3_), channel_id=1, source_target_pairs={{64,65},{65,66},{66,67},{67,68},{68,69},{69,70},{70,71},{71,72},{7... | collective-permute-start | bytes 835592 | tf_op jit(solution)/shard_map/ppermute | solution.py:577
  101.2 1.4 collective-permute-done.17.refs_2_
  102.6 5.1 %collective-permute-start.18 = (bf16[2,136,512]{2,1,0:T(8,128)(2,1)S(1)}, bf16[2,136,512]{2,1,0:T(8,128)(2,1)S(1)}, u32[]{:S(2)}, u32[]{:S(2)}) collective-permute-start(bf16[2,136,512]{2,1,0:T(8,128)(2,1)S(1)} %collective-permute-done.17.refs_2_), channel_id=1, source_target_pairs={{65,64},{66,65},{67,66},{68,67},{69,68},{70,69},{71,70},{72,71},{7... | collective-permute-start | bytes 835592 | tf_op jit(solution)/shard_map/ppermute | solution.py:578
  107.8 6.7 %collective-permute-done.11.refs_3_ = bf16[2,136,512]{2,1,0:T(8,128)(2,1)S(1)} collective-permute-done((bf16[2,136,512]{2,1,0:T(8,128)(2,1)S(1)}, bf16[2,136,512]{2,1,0:T(8,128)(2,1)S(1)}, u32[]{:S(2)}, u32[]{:S(2)}) %collective-permute-start.11) | collective-permute-done | bytes 278560 | tf_op jit(solution)/shard_map/ppermute | solution.py:571
  114.5 3.3 %collective-permute-start.12 = (bf16[2,136,512]{2,1,0:T(8,128)(2,1)S(1)}, bf16[2,136,512]{2,1,0:T(8,128)(2,1)S(1)}, u32[]{:S(2)}, u32[]{:S(2)}) collective-permute-start(bf16[2,136,512]{2,1,0:T(8,128)(2,1)S(1)} %collective-permute-done.11.refs_3_), channel_id=1, source_target_pairs={{64,65},{65,66},{66,67},{67,68},{68,69},{69,70},{70,71},{71,72},{7... | collective-permute-start | bytes 835592 | tf_op jit(solution)/shard_map/ppermute | solution.py:577
  117.8 1.8 %collective-permute-done.13.refs_2_ = bf16[2,136,512]{2,1,0:T(8,128)(2,1)S(1)} collective-permute-done((bf16[2,136,512]{2,1,0:T(8,128)(2,1)S(1)}, bf16[2,136,512]{2,1,0:T(8,128)(2,1)S(1)}, u32[]{:S(2)}, u32[]{:S(2)}) %collective-permute-start.13) | collective-permute-done | bytes 278560 | tf_op jit(solution)/shard_map/ppermute | solution.py:571
  119.6 3.2 %collective-permute-start.14 = (bf16[2,136,512]{2,1,0:T(8,128)(2,1)S(1)}, bf16[2,136,512]{2,1,0:T(8,128)(2,1)S(1)}, u32[]{:S(2)}, u32[]{:S(2)}) collective-permute-start(bf16[2,136,512]{2,1,0:T(8,128)(2,1)S(1)} %collective-permute-done.13.refs_2_), channel_id=1, source_target_pairs={{65,64},{66,65},{67,66},{68,67},{69,68},{70,69},{71,70},{72,71},{7... | collective-permute-start | bytes 835592 | tf_op jit(solution)/shard_map/ppermute | solution.py:578
  122.8 11.0 %shard_map.59 = (bf16[2,4,256,512]{3,2,1,0:T(8,128)(2,1)}, bf16[4,128,512]{2,1,0:T(8,128)(2,1)S(1)}) custom-call(s32[6]{0:T(128)S(1)} %stack.53.refs_0_, bf16[2,136,512]{2,1,0:T(8,128)(2,1)S(1)} %collective-permute-done.16.refs_1_, bf16[2,136,512]{2,1,0:T(8,128)(2,1)S(1)} %collective-permute-done.17.refs_2_, ...), custom_call_target="tpu_custom_call", output_to_operand_aliasing={{0}: (7, {}), {1}: (8, {})} | custom-call | flops 6417285120 | bytes 12582912 | tf_op jit(solution)/shard_map/pallas_call | solution.py:461
  134.0 11.0 %shard_map.60 = (bf16[2,4,256,512]{3,2,1,0:T(8,128)(2,1)}, bf16[4,128,512]{2,1,0:T(8,128)(2,1)S(1)}) custom-call(s32[6]{0:T(128)S(1)} %stack.53.refs_0_, bf16[2,136,512]{2,1,0:T(8,128)(2,1)S(1)} %collective-permute-done.12.refs_1_, bf16[2,136,512]{2,1,0:T(8,128)(2,1)S(1)} %collective-permute-done.13.refs_2_, ...), custom_call_target="tpu_custom_call", output_to_operand_aliasing={{0}: (7, {}), {1}: (8, {})} | custom-call | flops 6417285120 | bytes 12582912 | tf_op jit(solution)/shard_map/pallas_call | solution.py:461
  (48 shorter events, 13.9 us)
Async XLA Ops:
  0.0 76.4 %collective-permute-start.7 = (bf16[3,1536,512]{2,1,0:T(8,128)(2,1)}, bf16[3,1536,512]{2,1,0:T(8,128)(2,1)}, u32[]{:S(2)}, u32[]{:S(2)}) collective-permute-start(bf16[3,1536,512]{2,1,0:T(8,128)(2,1)} %bitcast.39), channel_id=1, source_target_pairs={{0,32},{32,0},{64,96},{96,64},{1,33},{33,1},{65,97},{97,65},{2,34}... | collective-permute-start | bytes 14155784 | tf_op jit(solution)/shard_map/ppermute | solution.py:491
  1.9 22.3 %copy-start.1 = (bf16[2,64,16,256]{3,2,1,0:T(8,128)(2,1)S(1)}, bf16[2,64,16,256]{3,2,1,0:T(8,128)(2,1)}, u32[]{:S(2)}) copy-start(bf16[2,64,16,256]{3,2,1,0:T(8,128)(2,1)} %feat.5) | copy-start | bytes 3145732
  2.3 6.2 %collective-permute-start = (bf16[2,6,16,256]{3,1,2,0:T(8,128)(2,1)S(1)}, bf16[2,6,16,256]{3,1,2,0:T(8,128)(2,1)S(1)}, u32[]{:S(2)}, u32[]{:S(2)}) collective-permute-start(bf16[2,6,16,256]{3,1,2,0:T(8,128)(2,1)S(1)} %copy.11), channel_id=1, source_target_pairs={{0,32},{32,64},{64,96},{1,33},{33,65},{65,97},{2,34},{34,66},{66,9... | collective-permute-start | bytes 294920 | tf_op jit(solution)/shard_map/ppermute | solution.py:497
  3.6 5.0 %collective-permute-start.1 = (bf16[2,6,16,256]{3,1,2,0:T(8,128)(2,1)S(1)}, bf16[2,6,16,256]{3,1,2,0:T(8,128)(2,1)S(1)}, u32[]{:S(2)}, u32[]{:S(2)}) collective-permute-start(bf16[2,6,16,256]{3,1,2,0:T(8,128)(2,1)S(1)} %copy.12), channel_id=1, source_target_pairs={{32,0},{64,32},{96,64},{33,1},{65,33},{97,65},{34,2},{66,34},{98,6... | collective-permute-start | bytes 294920 | tf_op jit(solution)/shard_map/ppermute | solution.py:498
  8.6 8.7 %collective-permute-start.3 = (bf16[2,2,76,256]{3,2,1,0:T(8,128)(2,1)S(1)}, bf16[2,2,76,256]{3,2,1,0:T(8,128)(2,1)S(1)}, u32[]{:S(2)}, u32[]{:S(2)}) collective-permute-start(bf16[2,2,76,256]{3,2,1,0:T(8,128)(2,1)S(1)} %pad_maximum_fusion.1), channel_id=1, source_target_pairs={{1,0},{2,1},{3,2},{4,3},{5,4},{6,5},{7,6},{8,7},{9,8},{10,9},{11,1... | collective-permute-start | bytes 466952 | tf_op jit(solution)/shard_map/ppermute | solution.py:509
  15.1 9.1 %collective-permute-start.2 = (bf16[2,2,76,256]{3,2,1,0:T(8,128)(2,1)S(1)}, bf16[2,2,76,256]{3,2,1,0:T(8,128)(2,1)S(1)}, u32[]{:S(2)}, u32[]{:S(2)}) collective-permute-start(bf16[2,2,76,256]{3,2,1,0:T(8,128)(2,1)S(1)} %pad_maximum_fusion), channel_id=1, source_target_pairs={{0,1},{1,2},{2,3},{3,4},{4,5},{5,6},{6,7},{7,8},{8,9},{9,10},{10,1... | collective-permute-start | bytes 466952 | tf_op jit(solution)/shard_map/ppermute | solution.py:506
  32.1 11.4 %all-to-all-start.1 = ((bf16[64,8,512]{2,1,0:T(8,128)(2,1)}), bf16[64,8,512]{2,1,0:T(8,128)(2,1)S(1)}, u32[]{:S(2)}, u32[]{:S(2)}) async-start(bf16[64,8,512]{2,1,0:T(8,128)(2,1)} %bitcast.19), calls=%async_computation.1 | async-start | bytes 1048576 | tf_op jit(solution)/shard_map/all_to_all | solution.py:545
  43.4 14.8 %all-to-all-start = ((bf16[64,8,512]{2,1,0:T(8,128)(2,1)}), bf16[64,8,512]{2,1,0:T(8,128)(2,1)S(1)}, u32[]{:S(2)}, u32[]{:S(2)}) async-start(bf16[64,8,512]{2,1,0:T(8,128)(2,1)} %bitcast.15), calls=%async_computation | async-start | bytes 1048576 | tf_op jit(solution)/shard_map/all_to_all | solution.py:545
  48.5 27.2 %collective-permute-start.8 = (bf16[8,8,8,512]{3,2,1,0:T(8,128)(2,1)S(1)}, bf16[8,8,8,512]{3,2,1,0:T(8,128)(2,1)S(1)}, u32[]{:S(2)}, u32[]{:S(2)}) collective-permute-start(bf16[8,8,8,512]{3,2,1,0:T(8,128)(2,1)S(1)} %bitcast.36), channel_id=1, source_target_pairs={{0,0},{1,1},{2,2},{3,3},{4,4},{5,5},{6,6},{7,7},{16,32},{17,33},{1... | collective-permute-start | bytes 1572872 | tf_op jit(solution)/shard_map/ppermute | solution.py:548
  49.2 27.2 %collective-permute-start.9 = (bf16[8,8,8,512]{3,2,1,0:T(8,128)(2,1)S(1)}, bf16[8,8,8,512]{3,2,1,0:T(8,128)(2,1)S(1)}, u32[]{:S(2)}, u32[]{:S(2)}) collective-permute-start(bf16[8,8,8,512]{3,2,1,0:T(8,128)(2,1)S(1)} %bitcast.37), channel_id=1, source_target_pairs={{8,0},{9,1},{10,2},{11,3},{12,4},{13,5},{14,6},{15,7},{24,32},{25,... | collective-permute-start | bytes 1572872 | tf_op jit(solution)/shard_map/ppermute | solution.py:549
  57.5 1.4 collective-permute-start.10
  58.2 21.5 %collective-permute-start.4 = (bf16[8,8,8,512]{3,2,1,0:T(8,128)(2,1)S(1)}, bf16[8,8,8,512]{3,2,1,0:T(8,128)(2,1)S(1)}, u32[]{:S(2)}, u32[]{:S(2)}) collective-permute-start(bf16[8,8,8,512]{3,2,1,0:T(8,128)(2,1)S(1)} %bitcast.33), channel_id=1, source_target_pairs={{0,0},{1,1},{2,2},{3,3},{4,4},{5,5},{6,6},{7,7},{16,32},{17,33},{1... | collective-permute-start | bytes 1572872 | tf_op jit(solution)/shard_map/ppermute | solution.py:548
  58.9 28.0 %collective-permute-start.5 = (bf16[8,8,8,512]{3,2,1,0:T(8,128)(2,1)S(1)}, bf16[8,8,8,512]{3,2,1,0:T(8,128)(2,1)S(1)}, u32[]{:S(2)}, u32[]{:S(2)}) collective-permute-start(bf16[8,8,8,512]{3,2,1,0:T(8,128)(2,1)S(1)} %bitcast.35), channel_id=1, source_target_pairs={{8,0},{9,1},{10,2},{11,3},{12,4},{13,5},{14,6},{15,7},{24,32},{25,... | collective-permute-start | bytes 1572872 | tf_op jit(solution)/shard_map/ppermute | solution.py:549
  75.7 3.9 %collective-permute-start.6 = (bf16[8,8,512]{2,1,0:T(8,128)(2,1)S(1)}, bf16[8,8,512]{2,1,0:T(8,128)(2,1)S(1)}, u32[]{:S(2)}, u32[]{:S(2)}) collective-permute-start(bf16[8,8,512]{2,1,0:T(8,128)(2,1)S(1)} %dynamic-slice_bitcast_fusion.1), channel_id=1, source_target_pairs={{8,32},{9,33},{10,34},{11,35},{12,36},{13,37},{14,38},{15,39},{16,... | collective-permute-start | bytes 196616 | tf_op jit(solution)/shard_map/ppermute | solution.py:551
  77.1 19.8 %collective-permute-start.15 = (bf16[2,136,512]{2,1,0:T(8,128)(2,1)S(1)}, bf16[2,136,512]{2,1,0:T(8,128)(2,1)S(1)}, u32[]{:S(2)}, u32[]{:S(2)}) collective-permute-start(bf16[2,136,512]{2,1,0:T(8,128)(2,1)S(1)} %get-tuple-element.28), channel_id=1, source_target_pairs={{0,64},{1,65},{2,66},{3,67},{4,68},{5,69},{6,70},{7,71},{8,72},{9,... | collective-permute-start | bytes 835592 | tf_op jit(solution)/shard_map/ppermute | solution.py:571
  78.4 24.2 %collective-permute-start.17 = (bf16[2,136,512]{2,1,0:T(8,128)(2,1)S(1)}, bf16[2,136,512]{2,1,0:T(8,128)(2,1)S(1)}, u32[]{:S(2)}, u32[]{:S(2)}) collective-permute-start(bf16[2,136,512]{2,1,0:T(8,128)(2,1)S(1)} %get-tuple-element.29), channel_id=1, source_target_pairs={{0,64},{1,65},{2,66},{3,67},{4,68},{5,69},{6,70},{7,71},{8,72},{9,... | collective-permute-start | bytes 835592 | tf_op jit(solution)/shard_map/ppermute | solution.py:571
  87.8 26.7 %collective-permute-start.11 = (bf16[2,136,512]{2,1,0:T(8,128)(2,1)S(1)}, bf16[2,136,512]{2,1,0:T(8,128)(2,1)S(1)}, u32[]{:S(2)}, u32[]{:S(2)}) collective-permute-start(bf16[2,136,512]{2,1,0:T(8,128)(2,1)S(1)} %get-tuple-element.26), channel_id=1, source_target_pairs={{0,64},{1,65},{2,66},{3,67},{4,68},{5,69},{6,70},{7,71},{8,72},{9,... | collective-permute-start | bytes 835592 | tf_op jit(solution)/shard_map/ppermute | solution.py:571
  89.1 30.4 %collective-permute-start.13 = (bf16[2,136,512]{2,1,0:T(8,128)(2,1)S(1)}, bf16[2,136,512]{2,1,0:T(8,128)(2,1)S(1)}, u32[]{:S(2)}, u32[]{:S(2)}) collective-permute-start(bf16[2,136,512]{2,1,0:T(8,128)(2,1)S(1)} %get-tuple-element.27), channel_id=1, source_target_pairs={{0,64},{1,65},{2,66},{3,67},{4,68},{5,69},{6,70},{7,71},{8,72},{9,... | collective-permute-start | bytes 835592 | tf_op jit(solution)/shard_map/ppermute | solution.py:571
  96.9 26.0 %collective-permute-start.16 = (bf16[2,136,512]{2,1,0:T(8,128)(2,1)S(1)}, bf16[2,136,512]{2,1,0:T(8,128)(2,1)S(1)}, u32[]{:S(2)}, u32[]{:S(2)}) collective-permute-start(bf16[2,136,512]{2,1,0:T(8,128)(2,1)S(1)} %collective-permute-done.15.refs_3_), channel_id=1, source_target_pairs={{64,65},{65,66},{66,67},{67,68},{68,69},{69,70},{70,71},{71,72},{7... | collective-permute-start | bytes 835592 | tf_op jit(solution)/shard_map/ppermute | solution.py:577
  102.6 20.2 %collective-permute-start.18 = (bf16[2,136,512]{2,1,0:T(8,128)(2,1)S(1)}, bf16[2,136,512]{2,1,0:T(8,128)(2,1)S(1)}, u32[]{:S(2)}, u32[]{:S(2)}) collective-permute-start(bf16[2,136,512]{2,1,0:T(8,128)(2,1)S(1)} %collective-permute-done.17.refs_2_), channel_id=1, source_target_pairs={{65,64},{66,65},{67,66},{68,67},{69,68},{70,69},{71,70},{72,71},{7... | collective-permute-start | bytes 835592 | tf_op jit(solution)/shard_map/ppermute | solution.py:578
  114.5 19.5 %collective-permute-start.12 = (bf16[2,136,512]{2,1,0:T(8,128)(2,1)S(1)}, bf16[2,136,512]{2,1,0:T(8,128)(2,1)S(1)}, u32[]{:S(2)}, u32[]{:S(2)}) collective-permute-start(bf16[2,136,512]{2,1,0:T(8,128)(2,1)S(1)} %collective-permute-done.11.refs_3_), channel_id=1, source_target_pairs={{64,65},{65,66},{66,67},{67,68},{68,69},{69,70},{70,71},{71,72},{7... | collective-permute-start | bytes 835592 | tf_op jit(solution)/shard_map/ppermute | solution.py:577
  119.6 14.4 %collective-permute-start.14 = (bf16[2,136,512]{2,1,0:T(8,128)(2,1)S(1)}, bf16[2,136,512]{2,1,0:T(8,128)(2,1)S(1)}, u32[]{:S(2)}, u32[]{:S(2)}) collective-permute-start(bf16[2,136,512]{2,1,0:T(8,128)(2,1)S(1)} %collective-permute-done.13.refs_2_), channel_id=1, source_target_pairs={{65,64},{66,65},{67,66},{68,67},{69,68},{70,69},{71,70},{72,71},{7... | collective-permute-start | bytes 835592 | tf_op jit(solution)/shard_map/ppermute | solution.py:578
  133.9 11.2 %collective-permute-start.19 = (bf16[4,128,512]{2,1,0:T(8,128)(2,1)S(1)}, bf16[4,128,512]{2,1,0:T(8,128)(2,1)S(1)}, u32[]{:S(2)}, u32[]{:S(2)}) collective-permute-start(bf16[4,128,512]{2,1,0:T(8,128)(2,1)S(1)} %get-tuple-element.35), channel_id=1, source_target_pairs={{0,32},{32,0},{64,96},{96,64},{1,33},{33,1},{65,97},{97,65},{2,34}... | collective-permute-start | bytes 1572872 | tf_op jit(solution)/shard_map/ppermute | solution.py:583
  145.0 2.0 %collective-permute-start.20 = (bf16[4,128,512]{2,1,0:T(8,128)(2,1)S(1)}, bf16[4,128,512]{2,1,0:T(8,128)(2,1)S(1)}, u32[]{:S(2)}, u32[]{:S(2)}) collective-permute-start(bf16[4,128,512]{2,1,0:T(8,128)(2,1)S(1)} %get-tuple-element.36), channel_id=1, source_target_pairs={{0,32},{32,0},{64,96},{96,64},{1,33},{33,1},{65,97},{97,65},{2,34}... | collective-permute-start | bytes 1572872 | tf_op jit(solution)/shard_map/ppermute | solution.py:583
  (1 other events, 1.2 us)
